TPU v7x, 32 devices: a whole 2x2x4 slice. The times are simulated.
32 devices in a mesh: gx: 8 (over z, y), row: 2 (over x), ta: 2 (over core).
Axes of the slice: x: 2, y: 2, z: 4, core: 2. Of those that a mesh axis runs over, the one named last changes fastest.
Arguments:
- conserved: float32 [5, 64, 64, 256], P(None, 'gx', 'row', 'ta'), may hold values from -6 to 6
- diffusivity: float32 [5], replicated, may hold values from 0.02 to 0.1
- axial_speed: float32 [5], replicated, may hold values from 0.2 to 0.6
- coupling: float32 [5, 5], replicated, may hold values from -0.6 to 0.6
- pressure_weights: float32 [5], replicated, may hold values from 0.5 to 1.5
- station_cell: int32 [512], P(('gx', 'row')), may hold values from 0 to 4095, as said below
- owner_row: int32 [512, 1], P(('gx', 'row')), may hold values from 0 to 1; in each aligned block of 32 rows (0 to 31, 32 to 63, ...) at most 16 rows name the same one
- window_table: int32 [4], replicated, may hold values from 1 to 8
Outputs:
- advanced: float32 [5, 64, 64, 256], P(None, 'gx', 'row', 'ta')
- spectra: float32 [16, 32, 1056], P(('gx', 'row'), 'ta')
Inputs may be any that keep to these rules, and one draw needn't show every extreme that they name: `station_cell`: entries b * 32 to (b + 1) * 32 - 1, with b = g * 2 + j, are distinct cells whose axial index lies in [g * 8, (g + 1) * 8) and radial index in [j * 32, (j + 1) * 32). `owner_row`: in each aligned block of 32 stations, no owner is named more than 16 times.
All inputs are finite; a program needn't handle non-finite values.
Results may differ from a plain program's by a relative error of at most 0.00013.
Values sent between devices are 32-bit elements; how exact they have to be, the bound alone decides.
No kernel may reach another device: no remote copies, remote signals or barrier semaphores. Data moves between devices by JAX's collectives and lax.ppermute only.
A program may use at most 64 MiB of HBM per device.

v0:
```python
import math

import jax
import jax.numpy as jnp
from jax import lax
from jax.sharding import PartitionSpec as P

NM = 33
NFREQ = 16
STEPS = 4
CAP = 16


exact_mode = lax.Precision.HIGHEST


def padded_2(x, sides, width, wrap):
    for axis, dim in sides:
        devices, length = (lax.axis_size(axis), x.shape[dim])
        up = [(i, (i + 1) % devices) for i in range(devices if wrap else devices - 1)]
        down = [(j, i) for i, j in up]
        last = lax.slice_in_dim(x, length - width, length, axis=dim)
        leading = lax.slice_in_dim(x, 0, width, axis=dim)
        before = lax.ppermute(last, axis, up)
        after = lax.ppermute(leading, axis, down)
        x = jnp.concatenate([before, x, after], axis=dim)
    return x


def change_of(padded, rate, velocity):
    lengths = (padded.shape[0] - 4, padded.shape[1] - 4, padded.shape[2] - 4)

    def shifted(offset_x, offset_r, offset_t):
        return padded[
            offset_x : offset_x + lengths[0],
            offset_r : offset_r + lengths[1],
            offset_t : offset_t + lengths[2],
        ]

    center = shifted(2, 2, 2)
    near = (
        shifted(3, 2, 2)
        + shifted(1, 2, 2)
        + shifted(2, 3, 2)
        + shifted(2, 1, 2)
        + shifted(2, 2, 3)
        + shifted(2, 2, 1)
    )
    far = (
        shifted(4, 2, 2)
        + shifted(0, 2, 2)
        + shifted(2, 4, 2)
        + shifted(2, 0, 2)
        + shifted(2, 2, 4)
        + shifted(2, 2, 0)
    )
    laplace = (16.0 * near - far - 90.0 * center) / 12.0
    gradient = (
        8.0 * (shifted(3, 2, 2) - shifted(1, 2, 2)) - (shifted(4, 2, 2) - shifted(0, 2, 2))
    ) / 12.0
    return rate * laplace - velocity * gradient


def advance(padded, diffusivity, axial_speed, coupling):
    center = padded[:, 2:-2, 2:-2, 2:-2]
    change = jax.vmap(change_of)(padded, diffusivity, axial_speed)
    mixed = jnp.einsum("fg,gxrt->fxrt", coupling, center, precision=exact_mode)
    return center + change + mixed


def azimuth_table(offset, count, total, modes):
    theta = offset + jnp.arange(count, dtype=jnp.int32)
    order = jnp.arange(modes, dtype=jnp.int32)
    turns = theta[:, None] * order[None, :] % total
    angle = 2.0 * math.pi / total * turns.astype(jnp.float32)
    return jnp.concatenate([jnp.cos(angle), jnp.sin(angle)], axis=1) * (1.0 / math.sqrt(total))


def spectral_increment(coeffs, weight, step_index, modes, freqs):
    cosine_part = coeffs[..., :modes]
    sine_part = coeffs[..., modes:]
    phase = math.pi * step_index / freqs * jnp.arange(1, freqs + 1, dtype=jnp.float32)
    cos_phase = jnp.cos(phase)[:, None]
    sin_phase = jnp.sin(phase)[:, None]
    real_part = cos_phase * cosine_part[..., None, :] - sin_phase * sine_part[..., None, :]
    imag_part = -(sin_phase * cosine_part[..., None, :] + cos_phase * sine_part[..., None, :])
    return weight * jnp.stack([real_part, imag_part], axis=-2)


def local(
    conserved,
    diffusivity,
    axial_speed,
    coupling,
    pressure_weights,
    station_cell,
    owner_row,
    window_table,
):
    cells_x = conserved.shape[1]
    cells_r = conserved.shape[2]
    cells_t = conserved.shape[3]
    peers = lax.axis_size("row")
    total_r = cells_r * peers
    total_theta = cells_t * lax.axis_size("ta")
    capacity = CAP
    start_x = lax.axis_index("gx") * cells_x
    start_r = lax.axis_index("row") * cells_r
    local_cell = (station_cell // total_r - start_x) * cells_r + (station_cell % total_r - start_r)
    owners = owner_row[:, 0]
    ordinal = jnp.arange(owners.shape[0], dtype=jnp.int32)
    earlier = ordinal[None, :] < ordinal[:, None]
    same_owner = owners[None, :] == owners[:, None]
    rank = jnp.sum((earlier & same_owner).astype(jnp.int32), axis=1)
    slot = owners * capacity + rank
    slot_onehot = (slot[None, :] == jnp.arange(peers * capacity, dtype=jnp.int32)[:, None]).astype(
        jnp.float32
    )
    cell_onehot = (
        local_cell[:, None] == jnp.arange(cells_x * cells_r, dtype=jnp.int32)[None, :]
    ).astype(jnp.float32)
    placement = jnp.dot(slot_onehot, cell_onehot, precision=exact_mode)
    table = azimuth_table(lax.axis_index("ta") * cells_t, cells_t, total_theta, NM)
    state = conserved
    buffers = []
    for step_index in range(STEPS):
        padded = padded_2(state, (("ta", 3),), 2, True)
        padded = padded_2(padded, (("gx", 1), ("row", 2)), 2, False)
        state = advance(padded, diffusivity, axial_speed, coupling)
        pressure = jnp.einsum("f,fxrt->xrt", pressure_weights, state, precision=exact_mode)
        pressure = pressure.reshape(cells_x * cells_r, cells_t)
        buffers.append(
            jnp.dot(placement, pressure, precision=exact_mode).reshape(peers, capacity, cells_t)
        )
    received = []
    for step_index in range(STEPS):
        received.append(
            jnp.einsum(
                "pcq,qm->pcm",
                lax.all_to_all(buffers[step_index], "row", split_axis=0, concat_axis=0, tiled=True),
                table,
                precision=exact_mode,
            )
        )
    coeff_steps = jnp.stack(received, axis=2)
    coeffs = lax.psum_scatter(coeff_steps, "ta", scatter_dimension=0, tiled=True)
    result = jnp.zeros((coeffs.shape[0], coeffs.shape[1], NFREQ, 2, NM), jnp.float32)
    for step_index in range(STEPS):
        result = result + spectral_increment(
            coeffs[:, :, step_index],
            window_table[step_index].astype(jnp.float32) / 8.0,
            step_index,
            NM,
            NFREQ,
        )
    spectra = result.reshape(1, result.shape[0] * capacity, NFREQ * 2 * NM)
    return (state, spectra)


def solution(mesh):
    in_specs = (
        P(None, "gx", "row", "ta"),
        P(),
        P(),
        P(),
        P(),
        P(("gx", "row")),
        P(("gx", "row"), None),
        P(),
    )
    out_specs = (P(None, "gx", "row", "ta"), P(("gx", "row"), "ta", None))
    return jax.shard_map(local, mesh=mesh, in_specs=in_specs, out_specs=out_specs, check_vma=False)
```

profile of v0, /device:TPU:9, one launch (start us, length us, event | category | flops | bytes accessed | tf_op | source)
XLA Modules:
  0.0 236.5 jit_solution(9305396921475063936)
XLA Ops:
  0.6 1.6 fusion.116
  6.8 3.1 %collective-permute-start.3 = (f32[5,2,32,132]{3,0,2,1:T(8,128)S(1)}, f32[5,2,32,132]{3,0,2,1:T(8,128)S(1)}, u32[]{:S(2)}, u32[]{:S(2)}) collective-permute-start(f32[5,2,32,132]{3,0,2,1:T(8,128)S(1)} %get-tuple-element.26), channel_id=1, source_target_pairs={{0,4},{4,8},{8,12},{12,16},{16,20},{20,24},{24,28},{1,5},{5,9},{9,... | collective-permute-start | bytes 506888 | tf_op jit(solution)/shard_map/ppermute | solution.py:24
  10.0 3.0 %collective-permute-start.2 = (f32[5,2,32,132]{3,0,2,1:T(8,128)S(1)}, f32[5,2,32,132]{3,0,2,1:T(8,128)S(1)}, u32[]{:S(2)}, u32[]{:S(2)}) collective-permute-start(f32[5,2,32,132]{3,0,2,1:T(8,128)S(1)} %get-tuple-element.27), channel_id=1, source_target_pairs={{4,0},{8,4},{12,8},{16,12},{20,16},{24,20},{28,24},{5,1},{9,5},{13... | collective-permute-start | bytes 506888 | tf_op jit(solution)/shard_map/ppermute | solution.py:25
  13.0 18.9 %collective-permute-done.3 = f32[5,2,32,132]{3,0,2,1:T(8,128)S(1)} collective-permute-done((f32[5,2,32,132]{3,0,2,1:T(8,128)S(1)}, f32[5,2,32,132]{3,0,2,1:T(8,128)S(1)}, u32[]{:S(2)}, u32[]{:S(2)}) %collective-permute-start.3) | collective-permute-done | bytes 168992 | tf_op jit(solution)/shard_map/ppermute | solution.py:24
  32.0 2.7 %collective-permute-done.2 = f32[5,2,32,132]{3,0,2,1:T(8,128)S(1)} collective-permute-done((f32[5,2,32,132]{3,0,2,1:T(8,128)S(1)}, f32[5,2,32,132]{3,0,2,1:T(8,128)S(1)}, u32[]{:S(2)}, u32[]{:S(2)}) %collective-permute-start.2) | collective-permute-done | bytes 168992 | tf_op jit(solution)/shard_map/ppermute | solution.py:25
  34.9 1.3 collective-permute-start.4
  36.2 4.0 %collective-permute-start.5 = (f32[5,12,2,132]{3,0,2,1:T(8,128)S(1)}, f32[5,12,2,132]{3,0,2,1:T(8,128)S(1)}, u32[]{:S(2)}, u32[]{:S(2)}) collective-permute-start(f32[5,12,2,132]{3,0,2,1:T(8,128)S(1)} %get-tuple-element.19), channel_id=1, source_target_pairs={{0,2},{1,3},{4,6},{5,7},{8,10},{9,11},{12,14},{13,15},{16,18},{17,... | collective-permute-start | bytes 190088 | tf_op jit(solution)/shard_map/ppermute | solution.py:24
  40.2 2.5 %collective-permute-done.4 = f32[5,12,2,132]{3,0,2,1:T(8,128)S(1)} collective-permute-done((f32[5,12,2,132]{3,0,2,1:T(8,128)S(1)}, f32[5,12,2,132]{3,0,2,1:T(8,128)S(1)}, u32[]{:S(2)}, u32[]{:S(2)}) %collective-permute-start.4) | collective-permute-done | bytes 63392 | tf_op jit(solution)/shard_map/ppermute | solution.py:25
  42.7 0.9 collective-permute-done.5
  43.6 11.4 %convolution_add_fusion = f32[5,8,32,128]{3,0,2,1:T(8,128)S(1)} fusion(f32[5,8,32,128]{3,0,2,1:T(8,128)} %copy-done.3, f32[5,8,32,2]{3,0,2,1:T(8,128)S(1)} %copy.114, f32[5,8,32,2]{3,0,2,1:T(8,128)S(1)} %copy.116, f32[5,12,2,132]{3,0,2,1:T(8,128)S(1)} %collective-permute-done.5, f32[5,2,32,132]{3,0,2,1:T(8,128)S(1)} %collective-permute-done.2, ...), kind=kOutput, calls=%fused_computation.22 | convolution fusion | flops 19496960 | bytes 3237772 | tf_op jit(solution)/shard_map/fg,gxrt->fxrt/dot_general | solution.py:67
  56.1 1.7 collective-permute-start.6
  62.5 1.9 collective-permute-start.9
  64.4 4.3 %collective-permute-start.8 = (f32[5,2,32,132]{3,0,2,1:T(8,128)S(1)}, f32[5,2,32,132]{3,0,2,1:T(8,128)S(1)}, u32[]{:S(2)}, u32[]{:S(2)}) collective-permute-start(f32[5,2,32,132]{3,0,2,1:T(8,128)S(1)} %get-tuple-element.25), channel_id=1, source_target_pairs={{4,0},{8,4},{12,8},{16,12},{20,16},{24,20},{28,24},{5,1},{9,5},{13... | collective-permute-start | bytes 506888 | tf_op jit(solution)/shard_map/ppermute | solution.py:25
  68.7 1.0 fusion.91
  69.7 17.0 %collective-permute-done.9 = f32[5,2,32,132]{3,0,2,1:T(8,128)S(1)} collective-permute-done((f32[5,2,32,132]{3,0,2,1:T(8,128)S(1)}, f32[5,2,32,132]{3,0,2,1:T(8,128)S(1)}, u32[]{:S(2)}, u32[]{:S(2)}) %collective-permute-start.9) | collective-permute-done | bytes 168992 | tf_op jit(solution)/shard_map/ppermute | solution.py:24
  86.7 3.6 %collective-permute-done.8 = f32[5,2,32,132]{3,0,2,1:T(8,128)S(1)} collective-permute-done((f32[5,2,32,132]{3,0,2,1:T(8,128)S(1)}, f32[5,2,32,132]{3,0,2,1:T(8,128)S(1)}, u32[]{:S(2)}, u32[]{:S(2)}) %collective-permute-start.8) | collective-permute-done | bytes 168992 | tf_op jit(solution)/shard_map/ppermute | solution.py:25
  91.2 1.3 collective-permute-start.10
  92.5 4.8 %collective-permute-start.11 = (f32[5,12,2,132]{3,0,2,1:T(8,128)S(1)}, f32[5,12,2,132]{3,0,2,1:T(8,128)}, u32[]{:S(2)}, u32[]{:S(2)}) collective-permute-start(f32[5,12,2,132]{3,0,2,1:T(8,128)S(1)} %get-tuple-element.17), channel_id=1, source_target_pairs={{0,2},{1,3},{4,6},{5,7},{8,10},{9,11},{12,14},{13,15},{16,18},{17,... | collective-permute-start | bytes 190088 | tf_op jit(solution)/shard_map/ppermute | solution.py:24
  98.1 3.4 %all-to-all-start = ((f32[2,16,128]{2,1,0:T(8,128)}), f32[2,16,128]{2,1,0:T(8,128)S(1)}, u32[]{:S(2)}, u32[]{:S(2)}) async-start(f32[2,16,128]{2,1,0:T(8,128)} %fusion.118), calls=%async_computation | async-start | bytes 32768 | tf_op jit(solution)/shard_map/all_to_all | solution.py:140
  102.2 10.0 %fusion.2 = f32[5,8,32,128]{3,0,2,1:T(8,128)S(1)} fusion(f32[5,8,32,128]{3,0,2,1:T(8,128)S(1)} %convolution_add_fusion, f32[5,8,32,2]{3,0,2,1:T(8,128)} %copy-done.1, f32[5,8,32,2]{3,0,2,1:T(8,128)S(1)} %copy.127, f32[5,12,2,132]{3,0,2,1:T(8,128)} %collective-permute-done.11, f32[5,2,32,132]{3,0,2,1:T(8,128)} %copy-done.9, f32[5,2,32,132]{3,0,2,1:T(8,128)} %copy-done.6, ...), kind=kOutput, calls=%fused_computation.21 | convolution fusion | flops 19496960 | bytes 4281088 | tf_op jit(solution)/shard_map/fg,gxrt->fxrt/dot_general | solution.py:67
  113.4 1.0 collective-permute-start.12
  114.6 1.0 collective-permute-done.13
  116.9 1.9 collective-permute-start.15
  118.9 4.3 %collective-permute-start.14 = (f32[5,2,32,132]{3,0,2,1:T(8,128)S(1)}, f32[5,2,32,132]{3,0,2,1:T(8,128)S(1)}, u32[]{:S(2)}, u32[]{:S(2)}) collective-permute-start(f32[5,2,32,132]{3,0,2,1:T(8,128)S(1)} %get-tuple-element.23), channel_id=1, source_target_pairs={{4,0},{8,4},{12,8},{16,12},{20,16},{24,20},{28,24},{5,1},{9,5},{13... | collective-permute-start | bytes 506888 | tf_op jit(solution)/shard_map/ppermute | solution.py:25
  123.1 1.0 fusion.89
  124.1 17.3 %collective-permute-done.15 = f32[5,2,32,132]{3,0,2,1:T(8,128)S(1)} collective-permute-done((f32[5,2,32,132]{3,0,2,1:T(8,128)S(1)}, f32[5,2,32,132]{3,0,2,1:T(8,128)S(1)}, u32[]{:S(2)}, u32[]{:S(2)}) %collective-permute-start.15) | collective-permute-done | bytes 168992 | tf_op jit(solution)/shard_map/ppermute | solution.py:24
  141.5 3.4 %collective-permute-done.14 = f32[5,2,32,132]{3,0,2,1:T(8,128)S(1)} collective-permute-done((f32[5,2,32,132]{3,0,2,1:T(8,128)S(1)}, f32[5,2,32,132]{3,0,2,1:T(8,128)S(1)}, u32[]{:S(2)}, u32[]{:S(2)}) %collective-permute-start.14) | collective-permute-done | bytes 168992 | tf_op jit(solution)/shard_map/ppermute | solution.py:25
  144.8 0.9 pad_maximum_fusion.101
  145.7 1.3 collective-permute-start.16
  147.0 4.7 %collective-permute-start.17 = (f32[5,12,2,132]{3,0,2,1:T(8,128)S(1)}, f32[5,12,2,132]{3,0,2,1:T(8,128)}, u32[]{:S(2)}, u32[]{:S(2)}) collective-permute-start(f32[5,12,2,132]{3,0,2,1:T(8,128)S(1)} %get-tuple-element.15), channel_id=1, source_target_pairs={{0,2},{1,3},{4,6},{5,7},{8,10},{9,11},{12,14},{13,15},{16,18},{17,... | collective-permute-start | bytes 190088 | tf_op jit(solution)/shard_map/ppermute | solution.py:24
  152.5 3.5 %all-to-all-start.1 = ((f32[2,16,128]{2,1,0:T(8,128)}), f32[2,16,128]{2,1,0:T(8,128)S(1)}, u32[]{:S(2)}, u32[]{:S(2)}) async-start(f32[2,16,128]{2,1,0:T(8,128)} %fusion.119), calls=%async_computation.1 | async-start | bytes 32768 | tf_op jit(solution)/shard_map/all_to_all | solution.py:140
  156.6 10.0 %fusion.1 = f32[5,8,32,128]{3,0,2,1:T(8,128)S(1)} fusion(f32[5,8,32,128]{3,0,2,1:T(8,128)S(1)} %fusion.2, f32[5,8,32,2]{3,0,2,1:T(8,128)} %copy-done.2, f32[5,8,32,2]{3,0,2,1:T(8,128)S(1)} %copy.133, f32[5,12,2,132]{3,0,2,1:T(8,128)} %collective-permute-done.17, f32[5,2,32,132]{3,0,2,1:T(8,128)} %copy-done.10, f32[5,2,32,132]{3,0,2,1:T(8,128)} %copy-done.7, ...), kind=kOutput, calls=%fused_computation.19 | convolution fusion | flops 19496960 | bytes 4281088 | tf_op jit(solution)/shard_map/fg,gxrt->fxrt/dot_general | solution.py:67
  167.8 1.1 collective-permute-start.18
  169.1 1.0 collective-permute-done.19
  171.4 1.9 collective-permute-start.21
  173.3 4.3 %collective-permute-start.20 = (f32[5,2,32,132]{3,0,2,1:T(8,128)S(1)}, f32[5,2,32,132]{3,0,2,1:T(8,128)S(1)}, u32[]{:S(2)}, u32[]{:S(2)}) collective-permute-start(f32[5,2,32,132]{3,0,2,1:T(8,128)S(1)} %get-tuple-element.21), channel_id=1, source_target_pairs={{4,0},{8,4},{12,8},{16,12},{20,16},{24,20},{28,24},{5,1},{9,5},{13... | collective-permute-start | bytes 506888 | tf_op jit(solution)/shard_map/ppermute | solution.py:25
  177.6 1.0 fusion.87
  178.6 17.3 %collective-permute-done.21 = f32[5,2,32,132]{3,0,2,1:T(8,128)S(1)} collective-permute-done((f32[5,2,32,132]{3,0,2,1:T(8,128)S(1)}, f32[5,2,32,132]{3,0,2,1:T(8,128)S(1)}, u32[]{:S(2)}, u32[]{:S(2)}) %collective-permute-start.21) | collective-permute-done | bytes 168992 | tf_op jit(solution)/shard_map/ppermute | solution.py:24
  196.0 3.4 %collective-permute-done.20 = f32[5,2,32,132]{3,0,2,1:T(8,128)S(1)} collective-permute-done((f32[5,2,32,132]{3,0,2,1:T(8,128)S(1)}, f32[5,2,32,132]{3,0,2,1:T(8,128)S(1)}, u32[]{:S(2)}, u32[]{:S(2)}) %collective-permute-start.20) | collective-permute-done | bytes 168992 | tf_op jit(solution)/shard_map/ppermute | solution.py:25
  200.2 1.3 collective-permute-start.22
  201.5 5.3 %collective-permute-start.23 = (f32[5,12,2,132]{3,0,2,1:T(8,128)S(1)}, f32[5,12,2,132]{3,0,2,1:T(8,128)}, u32[]{:S(2)}, u32[]{:S(2)}) collective-permute-start(f32[5,12,2,132]{3,0,2,1:T(8,128)S(1)} %get-tuple-element.13), channel_id=1, source_target_pairs={{0,2},{1,3},{4,6},{5,7},{8,10},{9,11},{12,14},{13,15},{16,18},{17,... | collective-permute-start | bytes 190088 | tf_op jit(solution)/shard_map/ppermute | solution.py:24
  207.6 3.2 %all-to-all-start.2 = ((f32[2,16,128]{2,1,0:T(8,128)}), f32[2,16,128]{2,1,0:T(8,128)S(1)}, u32[]{:S(2)}, u32[]{:S(2)}) async-start(f32[2,16,128]{2,1,0:T(8,128)} %fusion.120), calls=%async_computation.2 | async-start | bytes 32768 | tf_op jit(solution)/shard_map/all_to_all | solution.py:140
  210.9 8.2 %fusion = f32[5,8,32,128]{3,0,2,1:T(8,128)} fusion(f32[5,8,32,128]{3,0,2,1:T(8,128)S(1)} %fusion.1, f32[5,8,32,2]{3,0,2,1:T(8,128)S(1)} %copy.138, f32[5,8,32,2]{3,0,2,1:T(8,128)S(1)} %copy.139, f32[5,12,2,132]{3,0,2,1:T(8,128)} %collective-permute-done.23, f32[5,2,32,132]{3,0,2,1:T(8,128)} %copy-done.8, f32[5,2,32,132]{3,0,2,1:T(8,128)} %copy-done.5, ...), kind=kOutput, calls=%fused_computation.17 | convolution fusion | flops 19496960 | bytes 5319424 | tf_op jit(solution)/shard_map/fg,gxrt->fxrt/dot_general | solution.py:67
  219.1 2.2 fusion.85
  222.2 3.2 %all-to-all-start.3 = ((f32[2,16,128]{2,1,0:T(8,128)}), f32[2,16,128]{2,1,0:T(8,128)S(1)}, u32[]{:S(2)}, u32[]{:S(2)}) async-start(f32[2,16,128]{2,1,0:T(8,128)} %fusion.121), calls=%async_computation.3 | async-start | bytes 32768 | tf_op jit(solution)/shard_map/all_to_all | solution.py:140
  225.6 2.2 copy.143
  228.3 5.6 %all-reduce = f32[2,16,4,66]{3,1,0,2:T(8,128)S(1)} all-reduce(f32[2,16,4,66]{3,1,0,2:T(8,128)S(1)} %pad_maximum_fusion.112), channel_id=2, replica_groups=mesh['gx'=8,'row'=2,'ta'=2] {'ta'}, use_global_device_ids=true, to_apply=%region_1.2.clone | all-reduce | flops 8448 | bytes 67584
  235.5 1.0 add.399
  (120 shorter events, 21.7 us)
Async XLA Ops:
  0.6 43.0 %copy-start = (f32[5,5]{1,0:T(8,128)S(1)}, f32[5,5]{1,0:T(8,128)}, u32[]{:S(2)}) copy-start(f32[5,5]{1,0:T(8,128)} %param.11) | copy-start | bytes 304
  2.2 1.5 copy-start.14
  2.2 1.7 copy-start.12
  2.2 2.4 %copy-start.13 = (s32[32]{0:T(128)S(1)}, s32[32]{0:T(128)}, u32[]{:S(2)}) copy-start(s32[32]{0:T(128)} %param.13) | copy-start | bytes 388
  2.3 2.7 %copy-start.4 = (f32[5,8,32,128]{3,2,1,0:T(8,128)S(1)}, f32[5,8,32,128]{3,2,1,0:T(8,128)}, u32[]{:S(2)}) copy-start(f32[5,8,32,128]{3,2,1,0:T(8,128)} %param.8) | copy-start | bytes 1966084
  2.6 3.3 %collective-permute-start = (f32[5,8,32,2]{2,1,3,0:T(8,128)S(1)}, f32[5,8,32,2]{2,1,3,0:T(8,128)S(1)}, u32[]{:S(2)}, u32[]{:S(2)}) collective-permute-start(f32[5,8,32,2]{2,1,3,0:T(8,128)S(1)} %copy.155), channel_id=1, source_target_pairs={{0,1},{1,0},{2,3},{3,2},{4,5},{5,4},{6,7},{7,6},{8,9},{9,8},{10,11... | collective-permute-start | bytes 30728 | tf_op jit(solution)/shard_map/ppermute | solution.py:24
  3.6 1.8 collective-permute-start.1
  5.4 29.3 %copy-start.3 = (f32[5,8,32,128]{3,0,2,1:T(8,128)}, f32[5,8,32,128]{3,0,2,1:T(8,128)S(1)}, u32[]{:S(2)}) copy-start(f32[5,8,32,128]{3,0,2,1:T(8,128)S(1)} %copy.122) | copy-start | bytes 1966084
  6.3 6.7 %copy-start.15 = (f32[5]{0:T(128)S(1)}, f32[5]{0:T(128)}, u32[]{:S(2)}) copy-start(f32[5]{0:T(128)} %param.10) | copy-start | bytes 64
  6.3 6.7 %copy-start.16 = (f32[5]{0:T(128)S(1)}, f32[5]{0:T(128)}, u32[]{:S(2)}) copy-start(f32[5]{0:T(128)} %param.9) | copy-start | bytes 64
  6.8 25.2 %collective-permute-start.3 = (f32[5,2,32,132]{3,0,2,1:T(8,128)S(1)}, f32[5,2,32,132]{3,0,2,1:T(8,128)S(1)}, u32[]{:S(2)}, u32[]{:S(2)}) collective-permute-start(f32[5,2,32,132]{3,0,2,1:T(8,128)S(1)} %get-tuple-element.26), channel_id=1, source_target_pairs={{0,4},{4,8},{8,12},{12,16},{16,20},{20,24},{24,28},{1,5},{5,9},{9,... | collective-permute-start | bytes 506888 | tf_op jit(solution)/shard_map/ppermute | solution.py:24
  10.0 24.7 %collective-permute-start.2 = (f32[5,2,32,132]{3,0,2,1:T(8,128)S(1)}, f32[5,2,32,132]{3,0,2,1:T(8,128)S(1)}, u32[]{:S(2)}, u32[]{:S(2)}) collective-permute-start(f32[5,2,32,132]{3,0,2,1:T(8,128)S(1)} %get-tuple-element.27), channel_id=1, source_target_pairs={{4,0},{8,4},{12,8},{16,12},{20,16},{24,20},{28,24},{5,1},{9,5},{13... | collective-permute-start | bytes 506888 | tf_op jit(solution)/shard_map/ppermute | solution.py:25
  34.9 7.9 %collective-permute-start.4 = (f32[5,12,2,132]{3,0,2,1:T(8,128)S(1)}, f32[5,12,2,132]{3,0,2,1:T(8,128)S(1)}, u32[]{:S(2)}, u32[]{:S(2)}) collective-permute-start(f32[5,12,2,132]{3,0,2,1:T(8,128)S(1)} %get-tuple-element.18), channel_id=1, source_target_pairs={{2,0},{3,1},{6,4},{7,5},{10,8},{11,9},{14,12},{15,13},{18,16},{19,... | collective-permute-start | bytes 190088 | tf_op jit(solution)/shard_map/ppermute | solution.py:25
  36.2 7.5 %collective-permute-start.5 = (f32[5,12,2,132]{3,0,2,1:T(8,128)S(1)}, f32[5,12,2,132]{3,0,2,1:T(8,128)S(1)}, u32[]{:S(2)}, u32[]{:S(2)}) collective-permute-start(f32[5,12,2,132]{3,0,2,1:T(8,128)S(1)} %get-tuple-element.19), channel_id=1, source_target_pairs={{0,2},{1,3},{4,6},{5,7},{8,10},{9,11},{12,14},{13,15},{16,18},{17,... | collective-permute-start | bytes 190088 | tf_op jit(solution)/shard_map/ppermute | solution.py:24
  55.4 5.1 %copy-start.19 = (u32[32]{0:T(128)S(1)}, u32[32]{0:T(128)}, u32[]{:S(2)}) copy-start(u32[32]{0:T(128)} %constant.106) | copy-start | bytes 388
  56.1 5.4 %collective-permute-start.6 = (f32[5,8,32,2]{2,1,3,0:T(8,128)S(1)}, f32[5,8,32,2]{2,1,3,0:T(8,128)S(1)}, u32[]{:S(2)}, u32[]{:S(2)}) collective-permute-start(f32[5,8,32,2]{2,1,3,0:T(8,128)S(1)} %copy.124), channel_id=1, source_target_pairs={{0,1},{1,0},{2,3},{3,2},{4,5},{5,4},{6,7},{7,6},{8,9},{9,8},{10,11... | collective-permute-start | bytes 30728 | tf_op jit(solution)/shard_map/ppermute | solution.py:24
  57.8 3.3 %collective-permute-start.7 = (f32[5,8,32,2]{2,1,3,0:T(8,128)S(1)}, f32[5,8,32,2]{2,1,3,0:T(8,128)S(1)}, u32[]{:S(2)}, u32[]{:S(2)}) collective-permute-start(f32[5,8,32,2]{2,1,3,0:T(8,128)S(1)} %copy.125), channel_id=1, source_target_pairs={{1,0},{0,1},{3,2},{2,3},{5,4},{4,5},{7,6},{6,7},{9,8},{8,9},{11,10... | collective-permute-start | bytes 30728 | tf_op jit(solution)/shard_map/ppermute | solution.py:25
  62.0 28.4 %copy-start.1 = (f32[5,8,32,2]{3,0,2,1:T(8,128)}, f32[5,8,32,2]{3,0,2,1:T(8,128)S(1)}, u32[]{:S(2)}) copy-start(f32[5,8,32,2]{3,0,2,1:T(8,128)S(1)} %copy.126) | copy-start | bytes 30724
  62.0 6.7 %copy-start.11 = (f32[5]{0:T(128)S(1)}, f32[5]{0:T(128)}, u32[]{:S(2)}) copy-start(f32[5]{0:T(128)} %param.12) | copy-start | bytes 64
  62.5 24.3 %collective-permute-start.9 = (f32[5,2,32,132]{3,0,2,1:T(8,128)S(1)}, f32[5,2,32,132]{3,0,2,1:T(8,128)S(1)}, u32[]{:S(2)}, u32[]{:S(2)}) collective-permute-start(f32[5,2,32,132]{3,0,2,1:T(8,128)S(1)} %get-tuple-element.24), channel_id=1, source_target_pairs={{0,4},{4,8},{8,12},{12,16},{16,20},{20,24},{24,28},{1,5},{5,9},{9,... | collective-permute-start | bytes 506888 | tf_op jit(solution)/shard_map/ppermute | solution.py:24
  64.4 26.0 %collective-permute-start.8 = (f32[5,2,32,132]{3,0,2,1:T(8,128)S(1)}, f32[5,2,32,132]{3,0,2,1:T(8,128)S(1)}, u32[]{:S(2)}, u32[]{:S(2)}) collective-permute-start(f32[5,2,32,132]{3,0,2,1:T(8,128)S(1)} %get-tuple-element.25), channel_id=1, source_target_pairs={{4,0},{8,4},{12,8},{16,12},{20,16},{24,20},{28,24},{5,1},{9,5},{13... | collective-permute-start | bytes 506888 | tf_op jit(solution)/shard_map/ppermute | solution.py:25
  86.7 4.5 %copy-start.6 = (f32[5,2,32,132]{3,0,2,1:T(8,128)}, f32[5,2,32,132]{3,0,2,1:T(8,128)S(1)}, u32[]{:S(2)}) copy-start(f32[5,2,32,132]{3,0,2,1:T(8,128)S(1)} %collective-permute-done.9) | copy-start | bytes 506884
  90.4 0.9 copy-start.9
  91.2 10.3 %collective-permute-start.10 = (f32[5,12,2,132]{3,0,2,1:T(8,128)}, f32[5,12,2,132]{3,0,2,1:T(8,128)S(1)}, u32[]{:S(2)}, u32[]{:S(2)}) collective-permute-start(f32[5,12,2,132]{3,0,2,1:T(8,128)} %get-tuple-element.16), channel_id=1, source_target_pairs={{2,0},{3,1},{6,4},{7,5},{10,8},{11,9},{14,12},{15,13},{18,16},{19,... | collective-permute-start | bytes 190088 | tf_op jit(solution)/shard_map/ppermute | solution.py:25
  92.5 9.7 %collective-permute-start.11 = (f32[5,12,2,132]{3,0,2,1:T(8,128)S(1)}, f32[5,12,2,132]{3,0,2,1:T(8,128)}, u32[]{:S(2)}, u32[]{:S(2)}) collective-permute-start(f32[5,12,2,132]{3,0,2,1:T(8,128)S(1)} %get-tuple-element.17), channel_id=1, source_target_pairs={{0,2},{1,3},{4,6},{5,7},{8,10},{9,11},{12,14},{13,15},{16,18},{17,... | collective-permute-start | bytes 190088 | tf_op jit(solution)/shard_map/ppermute | solution.py:24
  98.1 16.3 %all-to-all-start = ((f32[2,16,128]{2,1,0:T(8,128)}), f32[2,16,128]{2,1,0:T(8,128)S(1)}, u32[]{:S(2)}, u32[]{:S(2)}) async-start(f32[2,16,128]{2,1,0:T(8,128)} %fusion.118), calls=%async_computation | async-start | bytes 32768 | tf_op jit(solution)/shard_map/all_to_all | solution.py:140
  101.5 0.7 copy-start.17
  113.4 2.6 %collective-permute-start.12 = (f32[5,8,32,2]{2,1,3,0:T(8,128)S(1)}, f32[5,8,32,2]{2,1,3,0:T(8,128)S(1)}, u32[]{:S(2)}, u32[]{:S(2)}) collective-permute-start(f32[5,8,32,2]{2,1,3,0:T(8,128)S(1)} %copy.130), channel_id=1, source_target_pairs={{0,1},{1,0},{2,3},{3,2},{4,5},{5,4},{6,7},{7,6},{8,9},{9,8},{10,11... | collective-permute-start | bytes 30728 | tf_op jit(solution)/shard_map/ppermute | solution.py:24
  114.3 1.2 collective-permute-start.13
  116.4 28.4 %copy-start.2 = (f32[5,8,32,2]{3,0,2,1:T(8,128)}, f32[5,8,32,2]{3,0,2,1:T(8,128)S(1)}, u32[]{:S(2)}) copy-start(f32[5,8,32,2]{3,0,2,1:T(8,128)S(1)} %copy.132) | copy-start | bytes 30724
  116.9 24.5 %collective-permute-start.15 = (f32[5,2,32,132]{3,0,2,1:T(8,128)S(1)}, f32[5,2,32,132]{3,0,2,1:T(8,128)S(1)}, u32[]{:S(2)}, u32[]{:S(2)}) collective-permute-start(f32[5,2,32,132]{3,0,2,1:T(8,128)S(1)} %get-tuple-element.22), channel_id=1, source_target_pairs={{0,4},{4,8},{8,12},{12,16},{16,20},{20,24},{24,28},{1,5},{5,9},{9,... | collective-permute-start | bytes 506888 | tf_op jit(solution)/shard_map/ppermute | solution.py:24
  118.9 26.0 %collective-permute-start.14 = (f32[5,2,32,132]{3,0,2,1:T(8,128)S(1)}, f32[5,2,32,132]{3,0,2,1:T(8,128)S(1)}, u32[]{:S(2)}, u32[]{:S(2)}) collective-permute-start(f32[5,2,32,132]{3,0,2,1:T(8,128)S(1)} %get-tuple-element.23), channel_id=1, source_target_pairs={{4,0},{8,4},{12,8},{16,12},{20,16},{24,20},{28,24},{5,1},{9,5},{13... | collective-permute-start | bytes 506888 | tf_op jit(solution)/shard_map/ppermute | solution.py:25
  141.5 4.2 %copy-start.7 = (f32[5,2,32,132]{3,0,2,1:T(8,128)}, f32[5,2,32,132]{3,0,2,1:T(8,128)S(1)}, u32[]{:S(2)}) copy-start(f32[5,2,32,132]{3,0,2,1:T(8,128)S(1)} %collective-permute-done.15) | copy-start | bytes 506884
  144.8 0.9 copy-start.10
  145.7 10.2 %collective-permute-start.16 = (f32[5,12,2,132]{3,0,2,1:T(8,128)}, f32[5,12,2,132]{3,0,2,1:T(8,128)S(1)}, u32[]{:S(2)}, u32[]{:S(2)}) collective-permute-start(f32[5,12,2,132]{3,0,2,1:T(8,128)} %get-tuple-element.14), channel_id=1, source_target_pairs={{2,0},{3,1},{6,4},{7,5},{10,8},{11,9},{14,12},{15,13},{18,16},{19,... | collective-permute-start | bytes 190088 | tf_op jit(solution)/shard_map/ppermute | solution.py:25
  147.0 9.6 %collective-permute-start.17 = (f32[5,12,2,132]{3,0,2,1:T(8,128)S(1)}, f32[5,12,2,132]{3,0,2,1:T(8,128)}, u32[]{:S(2)}, u32[]{:S(2)}) collective-permute-start(f32[5,12,2,132]{3,0,2,1:T(8,128)S(1)} %get-tuple-element.15), channel_id=1, source_target_pairs={{0,2},{1,3},{4,6},{5,7},{8,10},{9,11},{12,14},{13,15},{16,18},{17,... | collective-permute-start | bytes 190088 | tf_op jit(solution)/shard_map/ppermute | solution.py:24
  152.5 16.4 %all-to-all-start.1 = ((f32[2,16,128]{2,1,0:T(8,128)}), f32[2,16,128]{2,1,0:T(8,128)S(1)}, u32[]{:S(2)}, u32[]{:S(2)}) async-start(f32[2,16,128]{2,1,0:T(8,128)} %fusion.119), calls=%async_computation.1 | async-start | bytes 32768 | tf_op jit(solution)/shard_map/all_to_all | solution.py:140
  155.9 0.7 copy-start.18
  167.8 2.7 %collective-permute-start.18 = (f32[5,8,32,2]{2,1,3,0:T(8,128)S(1)}, f32[5,8,32,2]{2,1,3,0:T(8,128)S(1)}, u32[]{:S(2)}, u32[]{:S(2)}) collective-permute-start(f32[5,8,32,2]{2,1,3,0:T(8,128)S(1)} %copy.136), channel_id=1, source_target_pairs={{0,1},{1,0},{2,3},{3,2},{4,5},{5,4},{6,7},{7,6},{8,9},{9,8},{10,11... | collective-permute-start | bytes 30728 | tf_op jit(solution)/shard_map/ppermute | solution.py:24
  168.8 1.2 collective-permute-start.19
  171.4 24.5 %collective-permute-start.21 = (f32[5,2,32,132]{3,0,2,1:T(8,128)S(1)}, f32[5,2,32,132]{3,0,2,1:T(8,128)S(1)}, u32[]{:S(2)}, u32[]{:S(2)}) collective-permute-start(f32[5,2,32,132]{3,0,2,1:T(8,128)S(1)} %get-tuple-element.20), channel_id=1, source_target_pairs={{0,4},{4,8},{8,12},{12,16},{16,20},{20,24},{24,28},{1,5},{5,9},{9,... | collective-permute-start | bytes 506888 | tf_op jit(solution)/shard_map/ppermute | solution.py:24
  173.3 26.0 %collective-permute-start.20 = (f32[5,2,32,132]{3,0,2,1:T(8,128)S(1)}, f32[5,2,32,132]{3,0,2,1:T(8,128)S(1)}, u32[]{:S(2)}, u32[]{:S(2)}) collective-permute-start(f32[5,2,32,132]{3,0,2,1:T(8,128)S(1)} %get-tuple-element.21), channel_id=1, source_target_pairs={{4,0},{8,4},{12,8},{16,12},{20,16},{24,20},{28,24},{5,1},{9,5},{13... | collective-permute-start | bytes 506888 | tf_op jit(solution)/shard_map/ppermute | solution.py:25
  196.0 4.2 %copy-start.5 = (f32[5,2,32,132]{3,0,2,1:T(8,128)}, f32[5,2,32,132]{3,0,2,1:T(8,128)S(1)}, u32[]{:S(2)}) copy-start(f32[5,2,32,132]{3,0,2,1:T(8,128)S(1)} %collective-permute-done.21) | copy-start | bytes 506884
  199.3 0.8 copy-start.8
  200.2 10.7 %collective-permute-start.22 = (f32[5,12,2,132]{3,0,2,1:T(8,128)}, f32[5,12,2,132]{3,0,2,1:T(8,128)}, u32[]{:S(2)}, u32[]{:S(2)}) collective-permute-start(f32[5,12,2,132]{3,0,2,1:T(8,128)} %get-tuple-element.12), channel_id=1, source_target_pairs={{2,0},{3,1},{6,4},{7,5},{10,8},{11,9},{14,12},{15,13},{18,16},{19,... | collective-permute-start | bytes 190088 | tf_op jit(solution)/shard_map/ppermute | solution.py:25
  201.5 9.4 %collective-permute-start.23 = (f32[5,12,2,132]{3,0,2,1:T(8,128)S(1)}, f32[5,12,2,132]{3,0,2,1:T(8,128)}, u32[]{:S(2)}, u32[]{:S(2)}) collective-permute-start(f32[5,12,2,132]{3,0,2,1:T(8,128)S(1)} %get-tuple-element.13), channel_id=1, source_target_pairs={{0,2},{1,3},{4,6},{5,7},{8,10},{9,11},{12,14},{13,15},{16,18},{17,... | collective-permute-start | bytes 190088 | tf_op jit(solution)/shard_map/ppermute | solution.py:24
  207.6 14.6 %all-to-all-start.2 = ((f32[2,16,128]{2,1,0:T(8,128)}), f32[2,16,128]{2,1,0:T(8,128)S(1)}, u32[]{:S(2)}, u32[]{:S(2)}) async-start(f32[2,16,128]{2,1,0:T(8,128)} %fusion.120), calls=%async_computation.2 | async-start | bytes 32768 | tf_op jit(solution)/shard_map/all_to_all | solution.py:140
  222.2 5.9 %all-to-all-start.3 = ((f32[2,16,128]{2,1,0:T(8,128)}), f32[2,16,128]{2,1,0:T(8,128)S(1)}, u32[]{:S(2)}, u32[]{:S(2)}) async-start(f32[2,16,128]{2,1,0:T(8,128)} %fusion.121), calls=%async_computation.3 | async-start | bytes 32768 | tf_op jit(solution)/shard_map/all_to_all | solution.py:140
where the time goes:
time: 237 us; the launch traced here: 236 us
  waiting for transfers between devices  89.4 us (38%)
  starting transfers between devices  66.7 us (28%)
  matrix products  49 us (21%)
  local copies, waits for them, and re-layouts  16.3 us (7%)
  other arithmetic  5.64 us (2%)
  blocking collectives  5.6 us (2%)
  between operations  3.86 us (2%)
    ppermute x12, waiting for transfers between devices, padded_2(): before = lax.ppermute(last, axis, up)  71.6 us
    dot_general x4, matrix products, advance(): mixed = jnp.einsum('fg,gxrt->fxrt', coupling, center, precision=exact_mode)  39.7 us
    ppermute x12, starting transfers between devices, padded_2(): before = lax.ppermute(last, axis, up)  32.1 us
    ppermute x12, starting transfers between devices, padded_2(): after = lax.ppermute(leading, axis, down)  21.3 us
    ppermute x12, waiting for transfers between devices, padded_2(): after = lax.ppermute(leading, axis, down)  17.5 us
    all_to_all x4, starting transfers between devices, local(): lax.all_to_all(buffers[step_index], 'row', split_axis=0, concat_axis=0, t...  13.3 us
    unnamed x1, blocking collectives  5.6 us
    dot_general x4, matrix products, local(): jnp.einsum('f,fxrt->xrt', pressure_weights, state, precision=exact_mode)  5.26 us
  transfers between devices with their start and end apart: 28, of which 13 were waited for; matrix products, arithmetic and copies ran while one was open for 19% of the time, Pallas kernels for 0%

commit v1 on v0

v1 whole, which is shorter than its diff:
```python
import functools
import math

import jax
import jax.numpy as jnp
import numpy as np
from jax import lax
from jax.experimental import pallas as pl
from jax.experimental.pallas import tpu as pltpu
from jax.sharding import PartitionSpec as P

NM = 33
NFREQ = 16
STEPS = 4
CAP = 16
HALO = 2 * STEPS
NCOEF = 11
PAD = 8

VMEM = pltpu.VMEM
SMEM = pltpu.SMEM


def mode_basis(total, cores):
    theta = np.arange(total)
    wave = []
    for m in range(NM):
        wave.append((m, 0))
    wave.append((total // 2, 0))
    for m in range(1, NM):
        wave.append((m, 1))
    for m in range(NM, total // 2):
        wave.append((m, 0))
        wave.append((m, 1))
    rows, turns = [], []
    for m, kind in wave:
        angle = 2.0 * math.pi * ((m * theta) % total) / total
        row = np.sin(angle) if kind else np.cos(angle)
        norm = 1.0 / total if m in (0, total // 2) else 2.0 / total
        rows.append(row * math.sqrt(norm))
        turns.append(2.0 * math.pi * m / total)
    basis = np.stack(rows).reshape(cores, total // cores, total)
    turns = np.array(turns)
    eigen = (32.0 * np.cos(turns) - 2.0 * np.cos(2.0 * turns) - 30.0) / 12.0
    return basis, eigen.reshape(cores, total // cores)


def split_const(table):
    table = np.asarray(table, np.float32)
    high = table.astype(jnp.bfloat16)
    low = (table - high.astype(np.float32)).astype(jnp.bfloat16)
    return high, low


def spectrum_table(lanes):
    out = np.zeros((STEPS, lanes, NFREQ, 2, NM))
    for t in range(STEPS):
        phase = math.pi * t / NFREQ * np.arange(1, NFREQ + 1)
        for m in range(NM):
            scale = 1.0 if m == 0 else math.sqrt(0.5)
            out[t, m, :, 0, m] = np.cos(phase) * scale
            out[t, m, :, 1, m] = -np.sin(phase) * scale
            if m > 0:
                out[t, NM + m, :, 0, m] = -np.sin(phase) * scale
                out[t, NM + m, :, 1, m] = -np.cos(phase) * scale
    return out.reshape(STEPS, lanes, NFREQ * 2 * NM)


def halves(x):
    high = x.astype(jnp.bfloat16)
    return high, (x - high.astype(jnp.float32)).astype(jnp.bfloat16)


def dot3(high, low, table_high, table_low):
    dot = functools.partial(jnp.dot, preferred_element_type=jnp.float32)
    return dot(high, table_high) + (dot(low, table_high) + dot(high, table_low))


def forward_kernel(peers, sizes, *refs):
    pieces = refs[: sizes["ta"]]
    hi_ref, lo_ref, va_ref, vb_ref, e0_ref, ep_ref, ec_ref = refs[sizes["ta"] :]
    fields, cx, cr, ct = pieces[0].shape
    core = lax.axis_index("ta")
    row = lax.axis_index("row")
    odd = lax.axis_index("gx") % 2
    table_high, table_low = hi_ref[core], lo_ref[core]
    half = cx // 2
    keep = HALO - 2
    pair_at, cross_at = (cx - keep) * (1 - odd), (cx - keep) * odd
    for f in range(fields):
        x = jnp.concatenate([p[f].reshape(cx * cr, ct) for p in pieces], axis=1)
        high, low = halves(x)
        v = dot3(high, low, table_high, table_low).reshape(cx, cr, ct)
        va_ref[:, f] = v[:half]
        vb_ref[:, f] = v[half:]
        if peers == 2:
            edges = [jnp.where(row == 0, v[:, cr - HALO :], v[:, :HALO])]
        else:
            edges = [v[:, cr - HALO :], v[:, :HALO]]
        for side, edge in enumerate(edges):
            e0_ref[side, :, f] = edge
    for side in range(e0_ref.shape[0]):
        ep_ref[side] = e0_ref[side, pl.ds(pair_at, keep)]
        ec_ref[side] = e0_ref[side, pl.ds(cross_at, keep)]


def update_kernel(
    peers, sizes, coef_ref, weight_ref, index_ref,
    va_ref, vb_ref, p1a_ref, p1b_ref, p2a_ref, p2b_ref, r0_ref, rp_ref, rc_ref,
    out_ref, cycle_ref, w0_ref, w1_ref,
):
    half, fields, cr, lanes = va_ref.shape
    cx = 2 * half
    keep = HALO - 2
    gx, row, core = lax.axis_index("gx"), lax.axis_index("row"), lax.axis_index("ta")
    odd = gx % 2
    rows = w0_ref.shape[2] - 2 * PAD
    blocks = rows // 8
    if peers == 2:
        own = pl.multiple_of(PAD + HALO * row, 8)
        spots = [pl.multiple_of(PAD + cr * (1 - row), 8)]
    else:
        own = PAD + HALO
        spots = [PAD, PAD + HALO + cr]
    left_open = (gx > 0).astype(jnp.int32)
    right_open = (gx < sizes["gx"] - 1).astype(jnp.int32)
    pair_at = 2 * cx * (1 - odd)
    cross_at = 2 * cx * odd
    zero = jnp.zeros((8, lanes), jnp.float32)

    def clear(x, carry):
        for f in range(fields):
            for w in (w0_ref, w1_ref):
                w[x, f, pl.ds(0, PAD)] = zero
                w[x, f, pl.ds(PAD + rows, PAD)] = zero
        return carry

    lax.fori_loop(0, 3 * cx, clear, 0)

    def place(src_ref, at, r):
        n = src_ref.shape[0]
        h = src_ref.shape[2]

        def one(i, carry):
            for f in range(fields):
                w0_ref[at + i, f, pl.ds(r, h)] = src_ref[i, f]
            return carry

        lax.fori_loop(0, n, one, 0)

    place(va_ref, cx, own)
    place(vb_ref, cx + half, own)
    place(p1a_ref, pair_at, own)
    place(p1b_ref, pair_at + half, own)
    place(p2a_ref, cross_at, own)
    place(p2b_ref, cross_at + half, own)
    for side, spot in enumerate(spots):
        place(r0_ref.at[side], cx, spot)
        place(rp_ref.at[side], pair_at + (cx - keep) * odd, spot)
        place(rc_ref.at[side], cross_at + (cx - keep) * (1 - odd), spot)

    def blank(x, carry):
        for f in range(fields):
            for b in range(blocks):
                w1_ref[x, f, pl.ds(PAD + 8 * b, 8)] = zero
        return carry

    lax.fori_loop(cx - 2, cx - 2 + 2 * (1 - left_open), blank, 0)
    lax.fori_loop(2 * cx, 2 * cx + 2 * (1 - right_open), blank, 0)

    def layer(src, store, x, base, count):
        v = [
            [src[x, f, pl.ds(base + 8 * b, 8)] for b in range(count)]
            for f in range(fields)
        ]
        for f in range(fields):
            c = [coef_ref[f, i] for i in range(NCOEF)]
            for b in range(count):
                r = base + 8 * b
                total = c[0] * v[0][b]
                for g in range(1, fields):
                    total = total + c[g] * v[g][b]
                near = src[x, f, pl.ds(r + 1, 8)] + src[x, f, pl.ds(r - 1, 8)]
                far = src[x, f, pl.ds(r + 2, 8)] + src[x, f, pl.ds(r - 2, 8)]
                side = c[fields] * near + c[fields + 1] * far
                one = c[fields + 2] * src[x + 1, f, pl.ds(r, 8)] + c[fields + 3] * src[x - 1, f, pl.ds(r, 8)]
                two = c[fields + 4] * src[x + 2, f, pl.ds(r, 8)] + c[fields + 5] * src[x - 2, f, pl.ds(r, 8)]
                store(x, f, b, (total + side) + (one + two))

    def gather(t, read):
        @pl.when(core == 0)
        def _():
            def station(s, carry):
                x, r, slot = index_ref[0, s], index_ref[1, s], index_ref[2, s]
                p = weight_ref[0] * read(x, 0, r)
                for f in range(1, fields):
                    p = p + weight_ref[f] * read(x, f, r)
                cycle_ref[t, pl.ds(slot, 1)] = p
                return carry

            lax.fori_loop(0, index_ref.shape[1], station, 0, unroll=8)

    cycle_ref[...] = jnp.zeros_like(cycle_ref)
    buffers = [w0_ref, w1_ref]
    for t in range(STEPS):
        src, dst = buffers[t % 2], buffers[(t + 1) % 2]
        reach = HALO - 2 * (t + 1)
        low = cx - reach * left_open
        high = 2 * cx + reach * right_open
        if t < STEPS - 1:

            def store(x, f, b, value, dst=dst):
                dst[x, f, pl.ds(PAD + 8 * b, 8)] = value

            def body(x, carry, src=src, store=store):
                layer(src, store, x, PAD, blocks)
                return carry

            lax.fori_loop(low, high, body, 0)
            if peers > 2:
                for edge, spot in ((0, spots[0]), (peers - 1, spots[1])):

                    @pl.when(row == edge)
                    def _(spot=spot, dst=dst, low=low, high=high):
                        def wipe(x, carry):
                            for f in range(fields):
                                dst[x, f, pl.ds(spot, HALO)] = jnp.zeros((HALO, lanes), jnp.float32)
                            return carry

                        lax.fori_loop(low, high, wipe, 0)

            gather(t, lambda x, f, r, dst=dst: dst[cx + x, f, pl.ds(own + r, 1)])
        else:

            def store_out(x, f, b, value):
                out_ref[x - cx, f, pl.ds(8 * b, 8)] = value

            def body_out(x, carry, src=src):
                layer(src, store_out, x, own, cr // 8)
                return carry

            lax.fori_loop(cx, 2 * cx, body_out, 0)
            gather(t, lambda x, f, r: out_ref[x, f, pl.ds(r, 1)])


def inverse_kernel(cores, *refs):
    pieces = refs[:cores]
    hi_ref, lo_ref, out_ref = refs[cores:]
    fields, cx, cr, ct = out_ref.shape
    core = lax.axis_index("ta")
    table_high, table_low = hi_ref[core], lo_ref[core]
    for f in range(fields):
        x = jnp.concatenate([p[:, f].reshape(cx * cr, ct) for p in pieces], axis=1)
        high, low = halves(x)
        out_ref[f] = dot3(high, low, table_high, table_low).reshape(cx, cr, ct)


def spectra_kernel(peers, cores, *refs):
    received = refs[:peers]
    window_ref, hi_ref, lo_ref, out_ref = refs[peers:]
    share = peers // cores
    first = lax.axis_index("ta") * share
    mine = lax.axis_index("row")
    rows = []
    for j in range(share):
        hop = (mine - (first + j) + peers) % peers
        value = jnp.where(hop == 0, received[0][...], 0.0)
        for k in range(1, peers):
            value = value + jnp.where(hop == k, received[k][...], 0.0)
        rows.append(value)
    x = rows[0] if share == 1 else jnp.concatenate(rows, axis=1)
    total = None
    for t in range(STEPS):
        weight = window_ref[t].astype(jnp.float32) * 0.125
        high, low = halves(x[t] * weight)
        part = dot3(high, low, hi_ref[t], lo_ref[t])
        total = part if total is None else total + part
    out_ref[0] = total


def spec(space, n):
    return [pl.BlockSpec(memory_space=space)] * n


def local(
    sizes,
    conserved,
    diffusivity,
    axial_speed,
    coupling,
    pressure_weights,
    station_cell,
    owner_row,
    window_table,
):
    fields, cx, cr, ct = conserved.shape
    nx, peers, cores = sizes["gx"], sizes["row"], sizes["ta"]
    assert cx == HALO and nx % 2 == 0 and peers % cores == 0
    total_r, total_t = cr * peers, ct * cores
    gx, row, core = lax.axis_index("gx"), lax.axis_index("row"), lax.axis_index("ta")
    half, keep = cx // 2, HALO - 2
    sides = 1 if peers == 2 else 2
    basis, eigen = mode_basis(total_t, cores)
    ahead = np.zeros((cores, total_t, ct))
    back = np.zeros((cores, total_t, ct))
    for c in range(cores):
        for k in range(cores):
            d = (c + k) % cores
            here = slice(k * ct, (k + 1) * ct)
            ahead[c, here] = basis[c][:, d * ct : (d + 1) * ct].T
            back[c, here] = basis[d][:, c * ct : (c + 1) * ct]

    def around(x):
        return [x] + [
            lax.ppermute(x, "ta", [((c + k) % cores, c) for c in range(cores)])
            for k in range(1, cores)
        ]

    tile = jax.ShapeDtypeStruct((half, fields, cr, ct), jnp.float32)
    edge = jax.ShapeDtypeStruct((sides, cx, fields, HALO, ct), jnp.float32)
    corner = jax.ShapeDtypeStruct((sides, keep, fields, HALO, ct), jnp.float32)
    va, vb, e0, ep, ec = pl.pallas_call(
        functools.partial(forward_kernel, peers, sizes),
        out_shape=(tile, tile, edge, corner, corner),
        in_specs=spec(VMEM, cores + 2),
        out_specs=tuple(spec(VMEM, 5)),
        name="forward",
    )(*around(conserved), *split_const(ahead))

    swap = [(i, i ^ 1) for i in range(nx)]
    forward = [(i, i + 2 if i % 2 == 0 else i - 2) for i in range(nx)]
    forward = [(a, b) for a, b in forward if 0 <= b < nx]
    cross = [(i, i - 1 if i % 2 == 0 else i + 1) for i in range(nx)]
    cross = [(a, b) for a, b in cross if 0 <= b < nx]
    p1a = lax.ppermute(va, "gx", swap)
    p1b = lax.ppermute(vb, "gx", swap)

    def radial(x, hops):
        got = []
        for side in range(sides):
            if peers == 2:
                turn = [(0, 1), (1, 0)]
            else:
                turn = [(r, r + 1) for r in range(peers - 1)]
                if side:
                    turn = [(b, a) for a, b in turn]
            pairs = [(a * peers + c, b * peers + d) for a, b in hops for c, d in turn]
            got.append(lax.ppermute(x[side : side + 1], ("gx", "row"), pairs))
        return got[0] if sides == 1 else jnp.concatenate(got, axis=0)

    r0 = radial(e0, [(i, i) for i in range(nx)])
    rp = radial(ep, swap)
    rc = radial(ec, cross)
    p2a = lax.ppermute(p1a, "gx", forward)
    p2b = lax.ppermute(p1b, "gx", forward)

    eigenvalue = jnp.asarray(eigen, jnp.float32)[core]
    rate, speed = diffusivity, axial_speed
    middle = 1.0 + rate[:, None] * (eigenvalue[None, :] - 5.0)
    mix = coupling[:, :, None] + jnp.eye(fields, dtype=jnp.float32)[:, :, None] * middle[:, None, :]
    line = jnp.stack(
        [
            rate * (16.0 / 12.0),
            rate * (-1.0 / 12.0),
            (16.0 * rate - 8.0 * speed) / 12.0,
            (16.0 * rate + 8.0 * speed) / 12.0,
            (speed - rate) / 12.0,
            -(speed + rate) / 12.0,
        ],
        axis=1,
    )
    coef = jnp.concatenate([mix, jnp.broadcast_to(line[:, :, None], (fields, 6, ct))], axis=1)
    coef = jnp.broadcast_to(coef[:, :, None, :], (fields, NCOEF, 8, ct))

    owners = owner_row[:, 0]
    ordinal = jnp.arange(owners.shape[0], dtype=jnp.int32)
    earlier = (ordinal[None, :] < ordinal[:, None]) & (owners[None, :] == owners[:, None])
    rank = jnp.sum(earlier.astype(jnp.int32), axis=1)
    index = jnp.stack(
        [
            station_cell // total_r - gx * cx,
            station_cell % total_r - row * cr,
            owners * CAP + rank,
        ]
    )

    rows = cr + HALO * sides + 2 * PAD
    work = pltpu.VMEM((3 * cx, fields, rows, ct), jnp.float32)
    modes, cycles = pl.pallas_call(
        functools.partial(update_kernel, peers, sizes),
        out_shape=(
            jax.ShapeDtypeStruct((cx, fields, cr, ct), jnp.float32),
            jax.ShapeDtypeStruct((STEPS, peers * CAP, ct), jnp.float32),
        ),
        in_specs=spec(VMEM, 1) + spec(SMEM, 2) + spec(VMEM, 9),
        out_specs=tuple(spec(VMEM, 2)),
        scratch_shapes=[work, work],
        name="update",
    )(coef, pressure_weights, index, va, vb, p1a, p1b, p2a, p2b, r0, rp, rc)

    share = peers // cores
    received = []
    for k in range(peers):
        pairs = []
        for j in range(peers):
            pairs.append((j * cores, (j + k) % peers * cores + j // share))
        start = (row + k) % peers * CAP
        block = lax.dynamic_slice_in_dim(cycles, start, CAP, axis=1)
        received.append(lax.ppermute(block, ("row", "ta"), pairs))

    advanced = pl.pallas_call(
        functools.partial(inverse_kernel, cores),
        out_shape=jax.ShapeDtypeStruct(conserved.shape, jnp.float32),
        in_specs=spec(VMEM, cores + 2),
        out_specs=pl.BlockSpec(memory_space=VMEM),
        name="inverse",
    )(*around(modes), *split_const(back))
    spectra = pl.pallas_call(
        functools.partial(spectra_kernel, peers, cores),
        out_shape=jax.ShapeDtypeStruct((1, share * CAP, NFREQ * 2 * NM), jnp.float32),
        in_specs=spec(VMEM, peers) + spec(SMEM, 1) + spec(VMEM, 2),
        out_specs=pl.BlockSpec(memory_space=VMEM),
        name="spectra",
    )(*received, window_table, *split_const(spectrum_table(ct)))
    return (advanced, spectra)


def solution(mesh):
    in_specs = (
        P(None, "gx", "row", "ta"),
        P(),
        P(),
        P(),
        P(),
        P(("gx", "row")),
        P(("gx", "row"), None),
        P(),
    )
    out_specs = (P(None, "gx", "row", "ta"), P(("gx", "row"), "ta", None))
    body = functools.partial(local, dict(mesh.shape))
    return jax.shard_map(body, mesh=mesh, in_specs=in_specs, out_specs=out_specs, check_vma=False)
```

time: 237 us -> 67.2 us (0.28)
  waiting for transfers between devices: 89.4 us -> 19.6 us
  matrix products: 49 us -> 0 us
  starting transfers between devices: 66.7 us -> 19.6 us
  Pallas kernels: 0 us -> 17.4 us
  local copies, waits for them, and re-layouts: 16.3 us -> 4.31 us
  blocking collectives: 5.6 us -> 0 us
  between operations: 3.86 us -> 0.79 us
    ppermute x24 -> x11, waiting for transfers between devices: 89.1 us -> 19.6 us  [the longest x1 7.91 us: local(): p1a = lax.ppermute(va, 'gx', swap)]
    dot_general x17 -> x0, matrix products: 49 us -> none  [the longest x4 39.7 us: advance(): mixed = jnp.einsum('fg,gxrt->fxrt', coupling, center, precision=exact_mode)]
    ppermute x24 -> x11, starting transfers between devices: 53.4 us -> 19.6 us  [the longest x3 5.44 us: radial(): got.append(lax.ppermute(x[side:side + 1], ('gx', 'row'), pairs))]
    pallas_call x0 -> x4, Pallas kernels: none -> 17.4 us  [the longest x1 8.68 us: local(): pl.pallas_call(functools.partial(update_kernel, peers, sizes), out_shape=...]
    all_to_all x4 -> x0, starting transfers between devices: 13.3 us -> none  [local(): lax.all_to_all(buffers[step_index], 'row', split_axis=0, concat_axis=0, t...]
    unnamed x1 -> x0, blocking collectives: 5.6 us -> none
    slice x11 -> x0, local copies, waits for them, and re-layouts: 5.45 us -> none  [the longest x7 3.7 us: padded_2(): leading = lax.slice_in_dim(x, 0, width, axis=dim)]
    ppermute x8 -> x0, local copies, waits for them, and re-layouts: 3.52 us -> none  [the longest x4 1.76 us: padded_2(): before = lax.ppermute(last, axis, up)]
  transfers between devices with their start and end apart: 28 -> 11, of which waited for: 13 -> 5; matrix products, arithmetic and copies ran while one was open for 19% -> 8% of each run, Pallas kernels for 0% -> 4%
where the time goes in v1:
time: 67.2 us; the launch traced here: 66.1 us
  starting transfers between devices  19.6 us (29%)
  waiting for transfers between devices  19.6 us (29%)
  Pallas kernels  17.4 us (26%)
  other arithmetic  4.34 us (6%)
  local copies, waits for them, and re-layouts  4.31 us (6%)
  between operations  0.79 us (1%)
    pallas_call x1, Pallas kernels, local(): pl.pallas_call(functools.partial(update_kernel, peers, sizes), out_shape=...  8.68 us
    ppermute x1, waiting for transfers between devices, local(): p1a = lax.ppermute(va, 'gx', swap)  7.91 us
    ppermute x3, starting transfers between devices, radial(): got.append(lax.ppermute(x[side:side + 1], ('gx', 'row'), pairs))  5.44 us
    ppermute x2, waiting for transfers between devices, local(): received.append(lax.ppermute(block, ('row', 'ta'), pairs))  5.03 us
    ppermute x2, starting transfers between devices, around(): lax.ppermute(x, 'ta', [((c + k) % cores, c) for c in range(cores)])  4.38 us
    ppermute x1, waiting for transfers between devices, local(): p1b = lax.ppermute(vb, 'gx', swap)  3.82 us
    ppermute x1, starting transfers between devices, local(): p2a = lax.ppermute(p1a, 'gx', forward)  3.19 us
    ppermute x1, starting transfers between devices, local(): p2b = lax.ppermute(p1b, 'gx', forward)  3.19 us
  transfers between devices with their start and end apart: 11, of which 5 were waited for; matrix products, arithmetic and copies ran while one was open for 8% of the time, Pallas kernels for 4%

profile of v1, /device:TPU:9, one launch (start us, length us, event | category | flops | bytes accessed | tf_op | source)
XLA Modules:
  0.0 66.1 jit_solution(10456104004310162752)
XLA Ops:
  0.6 0.0 copy-start.11
  0.6 0.0 copy-start.12
  0.6 0.7 %collective-permute-start = (f32[5,8,32,128]{3,2,1,0:T(8,128)}, f32[5,8,32,128]{3,2,1,0:T(8,128)S(1)}, u32[]{:S(2)}, u32[]{:S(2)}) collective-permute-start(f32[5,8,32,128]{3,2,1,0:T(8,128)} %refs_0_.1), channel_id=1, source_target_pairs={{1,0},{0,1},{3,2},{2,3},{5,4},{4,5},{7,6},{6,7},{9,8},{8,9},{11,10... | collective-permute-start | bytes 1966088 | tf_op jit(solution)/shard_map/ppermute | solution.py:315
  1.4 0.9 %convert_reduce_fusion = s32[32]{0:T(128)S(1)} fusion(s32[32]{0:T(128)} %bitcast.23), kind=kLoop, calls=%fused_computation.2 | loop fusion | flops 5088 | bytes 256 | tf_op jit(solution)/shard_map/reduce_sum | solution.py:378
  2.3 0.7 %fusion.3 = f32[128]{0:T(128)S(1)} fusion(f32[2,128]{1,0:T(2,128)} %constant.99.clone, s32[]{:T(128)S(6)} %select_n.31), kind=kLoop, calls=%fused_computation.18 | loop fusion | flops 128 | bytes 1028 | tf_op jit(solution)/shard_map/mul | solution.py:359
  3.0 0.7 bitcast_add_fusion
  3.7 0.7 %multiply_bitcast_fusion = (f32[5,1]{0,1:T(1,128)S(1)}, f32[5,1]{0,1:T(1,128)S(1)}, f32[5,1]{0,1:T(1,128)S(1)}, f32[5,1]{0,1:T(1,128)S(1)}, f32[5,1]{0,1:T(1,128)S(1)}, /*index=5*/f32[5,1]{0,1:T(1,128)S(1)}) fusion(f32[5]{0:T(128)} %param.17, f32[5]{0:T(128)} %param.16), kind=kLoop, calls=%fused_computation.23 | loop fusion | flops 65 | bytes 160 | tf_op jit(solution)/shard_map/stack | solution.py:361
  4.3 0.7 %multiply_add_fusion.1 = f32[5,128]{1,0:T(8,128)S(1)} fusion(f32[128]{0:T(128)S(1)} %fusion.3, f32[5]{0:T(128)} %param.16), kind=kLoop, calls=%fused_computation.5 | loop fusion | flops 1280 | bytes 3092 | tf_op jit(solution)/shard_map/add | solution.py:359
  5.1 0.0 collective-permute-done.refs_1_
  5.1 0.8 %copy-done = f32[5,8,32,128]{3,2,1,0:T(8,128)} copy-done((f32[5,8,32,128]{3,2,1,0:T(8,128)}, f32[5,8,32,128]{3,2,1,0:T(8,128)S(1)}, u32[]{:S(2)}) %copy-start) | copy-done | bytes 655384
  5.9 3.0 %forward.1 = (f32[4,5,32,128]{3,2,1,0:T(8,128)}, f32[4,5,32,128]{3,2,1,0:T(8,128)}, f32[1,8,5,8,128]{4,3,2,1,0:T(8,128)}, f32[1,6,5,8,128]{4,3,2,1,0:T(8,128)}, f32[1,6,5,8,128]{4,3,2,1,0:T(8,128)}) custom-call(f32[5,8,32,128]{3,2,1,0:T(8,128)} %refs_0_.1, f32[5,8,32,128]{3,2,1,0:T(8,128)} %copy-done, bf16[2,256,128]{2,1,0:T(8,128)(2,1)} %constant.97.clone.refs_2_, ...), custom_call_target="tpu_custom_call" | custom-call | tf_op jit(solution)/shard_map/forward/pallas_call | solution.py:322
  8.9 1.2 %collective-permute-start.1 = (f32[4,5,32,128]{3,2,1,0:T(8,128)}, f32[4,5,32,128]{3,2,1,0:T(8,128)S(1)}, u32[]{:S(2)}, u32[]{:S(2)}) collective-permute-start(f32[4,5,32,128]{3,2,1,0:T(8,128)} %get-tuple-element.9.va_ref), channel_id=1, source_target_pairs={{0,4},{4,0},{8,12},{12,8},{16,20},{20,16},{24,28},{28,24},{1,5},{5... | collective-permute-start | bytes 983048 | tf_op jit(solution)/shard_map/ppermute | solution.py:335
  10.1 0.2 collective-permute-start.2
  10.3 0.1 multiply_add_fusion
  10.4 7.9 %collective-permute-done.1.p1a_ref = f32[4,5,32,128]{3,2,1,0:T(8,128)S(1)} collective-permute-done((f32[4,5,32,128]{3,2,1,0:T(8,128)}, f32[4,5,32,128]{3,2,1,0:T(8,128)S(1)}, u32[]{:S(2)}, u32[]{:S(2)}) %collective-permute-start.1) | collective-permute-done | bytes 327712 | tf_op jit(solution)/shard_map/ppermute | solution.py:335
  18.3 3.2 %collective-permute-start.3 = (f32[4,5,32,128]{3,2,1,0:T(8,128)S(1)}, f32[4,5,32,128]{3,2,1,0:T(8,128)S(1)}, u32[]{:S(2)}, u32[]{:S(2)}) collective-permute-start(f32[4,5,32,128]{3,2,1,0:T(8,128)S(1)} %collective-permute-done.1.p1a_ref), channel_id=1, source_target_pairs={{0,8},{8,16},{12,4},{16,24},{20,12},{28,20},{1,9},{9,17},{13,5},{1... | collective-permute-start | bytes 983048 | tf_op jit(solution)/shard_map/ppermute | solution.py:354
  21.5 3.8 %collective-permute-done.2.p1b_ref = f32[4,5,32,128]{3,2,1,0:T(8,128)S(1)} collective-permute-done((f32[4,5,32,128]{3,2,1,0:T(8,128)}, f32[4,5,32,128]{3,2,1,0:T(8,128)S(1)}, u32[]{:S(2)}, u32[]{:S(2)}) %collective-permute-start.2) | collective-permute-done | bytes 327712 | tf_op jit(solution)/shard_map/ppermute | solution.py:336
  25.3 3.2 %collective-permute-start.4 = (f32[4,5,32,128]{3,2,1,0:T(8,128)S(1)}, f32[4,5,32,128]{3,2,1,0:T(8,128)S(1)}, u32[]{:S(2)}, u32[]{:S(2)}) collective-permute-start(f32[4,5,32,128]{3,2,1,0:T(8,128)S(1)} %collective-permute-done.2.p1b_ref), channel_id=1, source_target_pairs={{0,8},{8,16},{12,4},{16,24},{20,12},{28,20},{1,9},{9,17},{13,5},{1... | collective-permute-start | bytes 983048 | tf_op jit(solution)/shard_map/ppermute | solution.py:355
  28.6 1.3 %collective-permute-start.5 = (f32[1,8,5,8,128]{4,3,2,1,0:T(8,128)}, f32[1,8,5,8,128]{4,3,2,1,0:T(8,128)S(1)}, u32[]{:S(2)}, u32[]{:S(2)}) collective-permute-start(f32[1,8,5,8,128]{4,3,2,1,0:T(8,128)} %get-tuple-element.11), channel_id=1, source_target_pairs={{0,2},{2,0},{4,6},{6,4},{8,10},{10,8},{12,14},{14,12},{16,18},{18,... | collective-permute-start | bytes 491528 | tf_op jit(solution)/shard_map/ppermute | solution.py:348
  29.9 0.1 collective-permute-start.6
  29.9 4.1 %collective-permute-start.7 = (f32[1,6,5,8,128]{4,3,2,1,0:T(8,128)}, f32[1,6,5,8,128]{4,3,2,1,0:T(8,128)S(1)}, u32[]{:S(2)}, u32[]{:S(2)}) collective-permute-start(f32[1,6,5,8,128]{4,3,2,1,0:T(8,128)} %get-tuple-element.13), channel_id=1, source_target_pairs={{4,10},{6,8},{8,6},{10,4},{12,18},{14,16},{16,14},{18,12},{20,26},... | collective-permute-start | bytes 368648 | tf_op jit(solution)/shard_map/ppermute | solution.py:348
  34.0 0.6 pad_add_fusion.index_ref
  34.6 0.1 copy.18
  34.7 0.1 broadcast_in_dim.4
  34.8 1.5 %collective-permute-done.6.rp_ref = f32[1,6,5,8,128]{4,3,2,1,0:T(8,128)S(1)} collective-permute-done((f32[1,6,5,8,128]{4,3,2,1,0:T(8,128)}, f32[1,6,5,8,128]{4,3,2,1,0:T(8,128)S(1)}, u32[]{:S(2)}, u32[]{:S(2)}) %collective-permute-start.6) | collective-permute-done | bytes 122912 | tf_op jit(solution)/shard_map/ppermute | solution.py:348
  36.3 1.3 %collective-permute-done.7.rc_ref = f32[1,6,5,8,128]{4,3,2,1,0:T(8,128)S(1)} collective-permute-done((f32[1,6,5,8,128]{4,3,2,1,0:T(8,128)}, f32[1,6,5,8,128]{4,3,2,1,0:T(8,128)S(1)}, u32[]{:S(2)}, u32[]{:S(2)}) %collective-permute-start.7) | collective-permute-done | bytes 122912 | tf_op jit(solution)/shard_map/ppermute | solution.py:348
  37.7 0.0 collective-permute-done.5.r0_ref
  37.7 0.0 collective-permute-done.3.p2a_ref
  37.7 0.0 copy-start.4
  37.7 0.0 collective-permute-done.4.p2b_ref
  37.7 0.8 %broadcast_in_dim.5.coef_ref = f32[5,11,8,128]{3,2,1,0:T(8,128)} broadcast(f32[5,11,128]{2,1,0:T(8,128)S(1)} %pad_maximum_fusion), dimensions={0,1,3} | broadcast | bytes 253440 | tf_op jit(solution)/shard_map/broadcast_in_dim | solution.py:373
  38.5 0.0 copy-done.2
  38.5 0.0 copy-done.7
  38.5 0.0 copy-done.4
  38.6 0.1 copy-done.5
  38.7 8.7 %update.1 = (f32[8,5,32,128]{3,2,1,0:T(8,128)}, f32[4,32,128]{2,1,0:T(8,128)}) custom-call(f32[5,11,8,128]{3,2,1,0:T(8,128)} %broadcast_in_dim.5.coef_ref, f32[5]{0:T(128)} %weight_ref.1, s32[3,32]{1,0:T(4,128)} %pad_add_fusion.index_ref, f32[4,5,32,128]{3,2,1,0:T(8,128)} %get-tuple-element.9.va_ref, f32[4,5,32,128]{3,2,1,0:T(8,128)} %get-tuple-element.10.vb_ref, ...), custom_call_target="tpu_custom_call" | custom-call | tf_op jit(solution)/shard_map/update/pallas_call | solution.py:389
  47.4 3.6 %collective-permute-start.8 = (f32[8,5,32,128]{3,2,1,0:T(8,128)}, f32[8,5,32,128]{3,2,1,0:T(8,128)S(1)}, u32[]{:S(2)}, u32[]{:S(2)}) collective-permute-start(f32[8,5,32,128]{3,2,1,0:T(8,128)} %get-tuple-element.14.refs_0_), channel_id=1, source_target_pairs={{1,0},{0,1},{3,2},{2,3},{5,4},{4,5},{7,6},{6,7},{9,8},{8,9},{11,10... | collective-permute-start | bytes 1966088 | tf_op jit(solution)/shard_map/ppermute | solution.py:315
  51.0 0.8 %constant_dynamic-slice_fusion = (f32[4,16,128]{2,1,0:T(8,128)S(1)}, f32[4,16,128]{2,1,0:T(8,128)S(1)}) fusion(f32[4,32,128]{2,1,0:T(8,128)} %get-tuple-element.15, s32[]{:T(128)S(6)} %select_n.37, s32[]{:T(128)S(6)} %select_n.35), kind=kLoop, calls=%fused_computation.14 | loop fusion | bytes 131080 | tf_op jit(solution)/shard_map/dynamic_slice | solution.py:408
  51.8 0.7 collective-permute-start.9
  52.4 1.3 %collective-permute-start.10 = (f32[4,16,128]{2,1,0:T(8,128)S(1)}, f32[4,16,128]{2,1,0:T(8,128)S(1)}, u32[]{:S(2)}, u32[]{:S(2)}) collective-permute-start(f32[4,16,128]{2,1,0:T(8,128)S(1)} %get-tuple-element.16), channel_id=1, source_target_pairs={{0,2},{2,1},{4,6},{6,5},{8,10},{10,9},{12,14},{14,13},{16,18},{18,... | collective-permute-start | bytes 98312 | tf_op jit(solution)/shard_map/ppermute | solution.py:409
  53.7 0.0 collective-permute-done.9.refs_0_
  53.8 0.0 copy-start.9
  53.8 5.0 %collective-permute-done.10.refs_1_ = f32[4,16,128]{2,1,0:T(8,128)S(1)} collective-permute-done((f32[4,16,128]{2,1,0:T(8,128)S(1)}, f32[4,16,128]{2,1,0:T(8,128)S(1)}, u32[]{:S(2)}, u32[]{:S(2)}) %collective-permute-start.10) | collective-permute-done | bytes 32800 | tf_op jit(solution)/shard_map/ppermute | solution.py:409
  58.8 0.6 copy-done.10
  59.4 2.9 %spectra.1 = f32[1,16,1056]{2,1,0:T(8,128)} custom-call(f32[4,16,128]{2,1,0:T(8,128)} %copy-done.9, f32[4,16,128]{2,1,0:T(8,128)} %copy-done.10, s32[4]{0:T(128)} %refs_2_.3, bf16[4,128,1056]{2,1,0:T(8,128)(2,1)} %constant.102.clone.refs_3_, bf16[4,128,1056]{2,1,0:T(8,128)(2,1)} %constant.103.clone.refs_4_), custom_call_target="tpu_custom_call" | custom-call | tf_op jit(solution)/shard_map/spectra/pallas_call | solution.py:418
  62.3 0.0 collective-permute-done.8.refs_1_
  62.4 0.9 %copy-done.1 = f32[8,5,32,128]{3,2,1,0:T(8,128)} copy-done((f32[8,5,32,128]{3,2,1,0:T(8,128)}, f32[8,5,32,128]{3,2,1,0:T(8,128)S(1)}, u32[]{:S(2)}) %copy-start.1) | copy-done | bytes 655384
  63.2 2.8 %inverse.1 = f32[5,8,32,128]{3,2,1,0:T(8,128)} custom-call(f32[8,5,32,128]{3,2,1,0:T(8,128)} %get-tuple-element.14.refs_0_, f32[8,5,32,128]{3,2,1,0:T(8,128)} %copy-done.1, bf16[2,256,128]{2,1,0:T(8,128)(2,1)} %constant.100.clone.refs_2_, bf16[2,256,128]{2,1,0:T(8,128)(2,1)} %constant.101.clone.refs_3_), custom_call_target="tpu_custom_call" | custom-call | tf_op jit(solution)/shard_map/inverse/pallas_call | solution.py:411
  (19 shorter events, 0.1 us)
Async XLA Ops:
  0.6 9.7 %copy-start.11 = (f32[5,5]{1,0:T(8,128)S(1)}, f32[5,5]{1,0:T(8,128)}, u32[]{:S(2)}) copy-start(f32[5,5]{1,0:T(8,128)} %param.18) | copy-start | bytes 304
  0.6 27.9 %copy-start.12 = (s32[32]{0:T(128)S(1)}, s32[32]{0:T(128)}, u32[]{:S(2)}) copy-start(s32[32]{0:T(128)} %param.20) | copy-start | bytes 388
  0.6 4.4 %collective-permute-start = (f32[5,8,32,128]{3,2,1,0:T(8,128)}, f32[5,8,32,128]{3,2,1,0:T(8,128)S(1)}, u32[]{:S(2)}, u32[]{:S(2)}) collective-permute-start(f32[5,8,32,128]{3,2,1,0:T(8,128)} %refs_0_.1), channel_id=1, source_target_pairs={{1,0},{0,1},{3,2},{2,3},{5,4},{4,5},{7,6},{6,7},{9,8},{8,9},{11,10... | collective-permute-start | bytes 1966088 | tf_op jit(solution)/shard_map/ppermute | solution.py:315
  5.1 0.8 %copy-start = (f32[5,8,32,128]{3,2,1,0:T(8,128)}, f32[5,8,32,128]{3,2,1,0:T(8,128)S(1)}, u32[]{:S(2)}) copy-start(f32[5,8,32,128]{3,2,1,0:T(8,128)S(1)} %collective-permute-done.refs_1_) | copy-start | bytes 1966084
  8.9 9.5 %collective-permute-start.1 = (f32[4,5,32,128]{3,2,1,0:T(8,128)}, f32[4,5,32,128]{3,2,1,0:T(8,128)S(1)}, u32[]{:S(2)}, u32[]{:S(2)}) collective-permute-start(f32[4,5,32,128]{3,2,1,0:T(8,128)} %get-tuple-element.9.va_ref), channel_id=1, source_target_pairs={{0,4},{4,0},{8,12},{12,8},{16,20},{20,16},{24,28},{28,24},{1,5},{5... | collective-permute-start | bytes 983048 | tf_op jit(solution)/shard_map/ppermute | solution.py:335
  10.1 15.3 %collective-permute-start.2 = (f32[4,5,32,128]{3,2,1,0:T(8,128)}, f32[4,5,32,128]{3,2,1,0:T(8,128)S(1)}, u32[]{:S(2)}, u32[]{:S(2)}) collective-permute-start(f32[4,5,32,128]{3,2,1,0:T(8,128)} %get-tuple-element.10.vb_ref), channel_id=1, source_target_pairs={{0,4},{4,0},{8,12},{12,8},{16,20},{20,16},{24,28},{28,24},{1,5},{5... | collective-permute-start | bytes 983048 | tf_op jit(solution)/shard_map/ppermute | solution.py:336
  18.3 20.2 %copy-start.2 = (f32[4,5,32,128]{3,2,1,0:T(8,128)}, f32[4,5,32,128]{3,2,1,0:T(8,128)S(1)}, u32[]{:S(2)}) copy-start(f32[4,5,32,128]{3,2,1,0:T(8,128)S(1)} %collective-permute-done.1.p1a_ref) | copy-start | bytes 983044
  18.3 19.3 %collective-permute-start.3 = (f32[4,5,32,128]{3,2,1,0:T(8,128)S(1)}, f32[4,5,32,128]{3,2,1,0:T(8,128)S(1)}, u32[]{:S(2)}, u32[]{:S(2)}) collective-permute-start(f32[4,5,32,128]{3,2,1,0:T(8,128)S(1)} %collective-permute-done.1.p1a_ref), channel_id=1, source_target_pairs={{0,8},{8,16},{12,4},{16,24},{20,12},{28,20},{1,9},{9,17},{13,5},{1... | collective-permute-start | bytes 983048 | tf_op jit(solution)/shard_map/ppermute | solution.py:354
  25.3 13.2 %copy-start.3 = (f32[4,5,32,128]{3,2,1,0:T(8,128)}, f32[4,5,32,128]{3,2,1,0:T(8,128)S(1)}, u32[]{:S(2)}) copy-start(f32[4,5,32,128]{3,2,1,0:T(8,128)S(1)} %collective-permute-done.2.p1b_ref) | copy-start | bytes 983044
  25.3 12.3 %collective-permute-start.4 = (f32[4,5,32,128]{3,2,1,0:T(8,128)S(1)}, f32[4,5,32,128]{3,2,1,0:T(8,128)S(1)}, u32[]{:S(2)}, u32[]{:S(2)}) collective-permute-start(f32[4,5,32,128]{3,2,1,0:T(8,128)S(1)} %collective-permute-done.2.p1b_ref), channel_id=1, source_target_pairs={{0,8},{8,16},{12,4},{16,24},{20,12},{28,20},{1,9},{9,17},{13,5},{1... | collective-permute-start | bytes 983048 | tf_op jit(solution)/shard_map/ppermute | solution.py:355
  28.6 9.1 %collective-permute-start.5 = (f32[1,8,5,8,128]{4,3,2,1,0:T(8,128)}, f32[1,8,5,8,128]{4,3,2,1,0:T(8,128)S(1)}, u32[]{:S(2)}, u32[]{:S(2)}) collective-permute-start(f32[1,8,5,8,128]{4,3,2,1,0:T(8,128)} %get-tuple-element.11), channel_id=1, source_target_pairs={{0,2},{2,0},{4,6},{6,4},{8,10},{10,8},{12,14},{14,12},{16,18},{18,... | collective-permute-start | bytes 491528 | tf_op jit(solution)/shard_map/ppermute | solution.py:348
  29.9 6.4 %collective-permute-start.6 = (f32[1,6,5,8,128]{4,3,2,1,0:T(8,128)}, f32[1,6,5,8,128]{4,3,2,1,0:T(8,128)S(1)}, u32[]{:S(2)}, u32[]{:S(2)}) collective-permute-start(f32[1,6,5,8,128]{4,3,2,1,0:T(8,128)} %get-tuple-element.12), channel_id=1, source_target_pairs={{0,6},{2,4},{4,2},{6,0},{8,14},{10,12},{12,10},{14,8},{16,22},{18,... | collective-permute-start | bytes 368648 | tf_op jit(solution)/shard_map/ppermute | solution.py:348
  29.9 7.7 %collective-permute-start.7 = (f32[1,6,5,8,128]{4,3,2,1,0:T(8,128)}, f32[1,6,5,8,128]{4,3,2,1,0:T(8,128)S(1)}, u32[]{:S(2)}, u32[]{:S(2)}) collective-permute-start(f32[1,6,5,8,128]{4,3,2,1,0:T(8,128)} %get-tuple-element.13), channel_id=1, source_target_pairs={{4,10},{6,8},{8,6},{10,4},{12,18},{14,16},{16,14},{18,12},{20,26},... | collective-permute-start | bytes 368648 | tf_op jit(solution)/shard_map/ppermute | solution.py:348
  36.3 2.2 %copy-start.7 = (f32[1,6,5,8,128]{4,3,2,1,0:T(8,128)}, f32[1,6,5,8,128]{4,3,2,1,0:T(8,128)S(1)}, u32[]{:S(2)}) copy-start(f32[1,6,5,8,128]{4,3,2,1,0:T(8,128)S(1)} %collective-permute-done.6.rp_ref) | copy-start | bytes 368644
  37.7 0.9 %copy-start.8 = (f32[1,6,5,8,128]{4,3,2,1,0:T(8,128)}, f32[1,6,5,8,128]{4,3,2,1,0:T(8,128)S(1)}, u32[]{:S(2)}) copy-start(f32[1,6,5,8,128]{4,3,2,1,0:T(8,128)S(1)} %collective-permute-done.7.rc_ref) | copy-start | bytes 368644
  37.7 0.9 %copy-start.6 = (f32[1,8,5,8,128]{4,3,2,1,0:T(8,128)}, f32[1,8,5,8,128]{4,3,2,1,0:T(8,128)S(1)}, u32[]{:S(2)}) copy-start(f32[1,8,5,8,128]{4,3,2,1,0:T(8,128)S(1)} %collective-permute-done.5.r0_ref) | copy-start | bytes 491524
  37.7 0.9 %copy-start.4 = (f32[4,5,32,128]{3,2,1,0:T(8,128)}, f32[4,5,32,128]{3,2,1,0:T(8,128)S(1)}, u32[]{:S(2)}) copy-start(f32[4,5,32,128]{3,2,1,0:T(8,128)S(1)} %collective-permute-done.3.p2a_ref) | copy-start | bytes 983044
  37.7 1.0 %copy-start.5 = (f32[4,5,32,128]{3,2,1,0:T(8,128)}, f32[4,5,32,128]{3,2,1,0:T(8,128)S(1)}, u32[]{:S(2)}) copy-start(f32[4,5,32,128]{3,2,1,0:T(8,128)S(1)} %collective-permute-done.4.p2b_ref) | copy-start | bytes 983044
  47.4 15.0 %collective-permute-start.8 = (f32[8,5,32,128]{3,2,1,0:T(8,128)}, f32[8,5,32,128]{3,2,1,0:T(8,128)S(1)}, u32[]{:S(2)}, u32[]{:S(2)}) collective-permute-start(f32[8,5,32,128]{3,2,1,0:T(8,128)} %get-tuple-element.14.refs_0_), channel_id=1, source_target_pairs={{1,0},{0,1},{3,2},{2,3},{5,4},{4,5},{7,6},{6,7},{9,8},{8,9},{11,10... | collective-permute-start | bytes 1966088 | tf_op jit(solution)/shard_map/ppermute | solution.py:315
  51.8 2.0 %collective-permute-start.9 = (f32[4,16,128]{2,1,0:T(8,128)S(1)}, f32[4,16,128]{2,1,0:T(8,128)S(1)}, u32[]{:S(2)}, u32[]{:S(2)}) collective-permute-start(f32[4,16,128]{2,1,0:T(8,128)S(1)} %get-tuple-element.17), channel_id=1, source_target_pairs={{0,0},{2,3},{4,4},{6,7},{8,8},{10,11},{12,12},{14,15},{16,16},{18,... | collective-permute-start | bytes 98312 | tf_op jit(solution)/shard_map/ppermute | solution.py:409
  52.4 6.3 %collective-permute-start.10 = (f32[4,16,128]{2,1,0:T(8,128)S(1)}, f32[4,16,128]{2,1,0:T(8,128)S(1)}, u32[]{:S(2)}, u32[]{:S(2)}) collective-permute-start(f32[4,16,128]{2,1,0:T(8,128)S(1)} %get-tuple-element.16), channel_id=1, source_target_pairs={{0,2},{2,1},{4,6},{6,5},{8,10},{10,9},{12,14},{14,13},{16,18},{18,... | collective-permute-start | bytes 98312 | tf_op jit(solution)/shard_map/ppermute | solution.py:409
  53.8 5.0 %copy-start.9 = (f32[4,16,128]{2,1,0:T(8,128)}, f32[4,16,128]{2,1,0:T(8,128)S(1)}, u32[]{:S(2)}) copy-start(f32[4,16,128]{2,1,0:T(8,128)S(1)} %collective-permute-done.9.refs_0_) | copy-start | bytes 98308
  58.8 0.6 copy-start.10
  62.4 0.9 %copy-start.1 = (f32[8,5,32,128]{3,2,1,0:T(8,128)}, f32[8,5,32,128]{3,2,1,0:T(8,128)S(1)}, u32[]{:S(2)}) copy-start(f32[8,5,32,128]{3,2,1,0:T(8,128)S(1)} %collective-permute-done.8.refs_1_) | copy-start | bytes 1966084

commit v2 on v0

v2 whole, which is shorter than its diff:
```python
import functools
import math

import jax
import jax.numpy as jnp
import numpy as np
from jax import lax
from jax.experimental import pallas as pl
from jax.experimental.pallas import tpu as pltpu
from jax.sharding import PartitionSpec as P


NM = 33
NFREQ = 16
STEPS = 4
CAP = 16
HALO = 2 * STEPS
NCOEF = 11
PAD = 8
PIECES = 4
STRIP = 4

VMEM = pltpu.VMEM
SMEM = pltpu.SMEM
HBM = pltpu.HBM


def mode_basis(total, cores):
    theta = np.arange(total)
    wave = []
    for m in range(NM):
        wave.append((m, 0))
    wave.append((total // 2, 0))
    for m in range(1, NM):
        wave.append((m, 1))
    for m in range(NM, total // 2):
        wave.append((m, 0))
        wave.append((m, 1))
    rows, turns = [], []
    for m, kind in wave:
        angle = 2.0 * math.pi * ((m * theta) % total) / total
        row = np.sin(angle) if kind else np.cos(angle)
        norm = 1.0 / total if m in (0, total // 2) else 2.0 / total
        rows.append(row * math.sqrt(norm))
        turns.append(2.0 * math.pi * m / total)
    basis = np.stack(rows).reshape(cores, total // cores, total)
    turns = np.array(turns)
    eigen = (32.0 * np.cos(turns) - 2.0 * np.cos(2.0 * turns) - 30.0) / 12.0
    return basis, eigen.reshape(cores, total // cores)


def split_const(table):
    table = np.asarray(table, np.float32)
    high = table.astype(jnp.bfloat16)
    low = (table - high.astype(np.float32)).astype(jnp.bfloat16)
    return np.stack([high, low])


def spectrum_table(lanes):
    out = np.zeros((STEPS, lanes, NFREQ, 2, NM))
    for t in range(STEPS):
        phase = math.pi * t / NFREQ * np.arange(1, NFREQ + 1)
        for m in range(NM):
            scale = 1.0 if m == 0 else math.sqrt(0.5)
            out[t, m, :, 0, m] = np.cos(phase) * scale
            out[t, m, :, 1, m] = -np.sin(phase) * scale
            if m > 0:
                out[t, NM + m, :, 0, m] = -np.sin(phase) * scale
                out[t, NM + m, :, 1, m] = -np.cos(phase) * scale
    return out.reshape(STEPS, lanes, NFREQ * 2 * NM)


def halves(x):
    high = x.astype(jnp.bfloat16)
    return high, (x - high.astype(jnp.float32)).astype(jnp.bfloat16)


def dot3(high, low, table_high, table_low):
    dot = functools.partial(jnp.dot, preferred_element_type=jnp.float32)
    return dot(high, table_high) + (dot(low, table_high) + dot(high, table_low))


def position(sizes):
    gx, row, core = lax.axis_index("gx"), lax.axis_index("row"), lax.axis_index("ta")
    share = sizes["row"] // sizes["ta"]
    return gx, row, core, (core - row // share + sizes["ta"]) % sizes["ta"]


def stage_kernel(sizes, own_ref, table_ref, part_ref):
    fields, cx, cr, ct = own_ref.shape
    _, _, core, group = position(sizes)
    for f in range(fields):
        x = own_ref[f].reshape(cx * cr, ct)
        v = dot3(*halves(x), table_ref[0, group, core], table_ref[1, group, core])
        part_ref[:, f] = v.reshape(cx, cr, ct)


def forward_kernel(sizes, first, count, last, part_ref, table_ref, *refs):
    peers, cores = sizes["row"], sizes["ta"]
    sources, refs = refs[: cores - 1], refs[cores - 1 :]
    fields, cx, cr, ct = sources[0].shape
    _, row, core, group = position(sizes)
    step = cx // PIECES
    done = ()
    if last:
        done, refs = refs[:first], refs[first:]
    out = refs[:count]
    for f in range(fields):
        v = part_ref[first * step : (first + count) * step, f].reshape(count * step * cr, ct)
        for k, s in enumerate(sources):
            x = s[f, first * step : (first + count) * step].reshape(count * step * cr, ct)
            other = (core + k + 1) % cores
            v = v + dot3(*halves(x), table_ref[0, group, other], table_ref[1, group, other])
        v = v.reshape(count, step, cr, ct)
        for i in range(count):
            out[i][:, f] = v[i]
    if last:
        (e0_ref,) = refs[count:]
        for i, ref in enumerate(tuple(done) + tuple(out)):
            for side in range(e0_ref.shape[0]):
                top = 1 - row if peers == 2 else 1 - side
                rows = pl.ds(pl.multiple_of((cr - HALO) * top, 8), HALO)
                e0_ref[side, i * step : (i + 1) * step] = ref[:, :, rows]


def prepare_kernel(
    sizes, cx, cr, rate_ref, speed_ref, mix_ref, cell_ref, owner_ref, eigen_ref,
    coef_ref, place_ref, slots_ref, count_ref,
):
    peers = sizes["row"]
    fields = coef_ref.shape[0]
    shape = coef_ref.shape[2:]
    gx, row, _, group = position(sizes)
    eigen = eigen_ref[group]
    for f in range(fields):
        rate, speed = rate_ref[f], speed_ref[f]
        for g in range(fields):
            value = jnp.full(shape, mix_ref[f, g])
            if g == f:
                value = value + (1.0 + rate * (eigen - 5.0))
            coef_ref[f, g] = value
        line = [
            rate * (16.0 / 12.0),
            rate * (-1.0 / 12.0),
            (16.0 * rate - 8.0 * speed) * (1.0 / 12.0),
            (16.0 * rate + 8.0 * speed) * (1.0 / 12.0),
            (speed - rate) * (1.0 / 12.0),
            (speed + rate) * (-1.0 / 12.0),
        ]
        for i, value in enumerate(line):
            coef_ref[f, fields + i] = jnp.full(shape, value)
    slots_ref[...] = jnp.zeros_like(slots_ref)
    for o in range(peers):
        count_ref[o] = 0
    cells = lax.broadcasted_iota(jnp.int32, (1, cx * cr), 1)

    def station(s, carry):
        owner, cell = owner_ref[s], cell_ref[s]
        rank = count_ref[owner]
        count_ref[owner] = rank + 1
        slot = (owner - row + peers) % peers * CAP + rank
        here = (cell // (cr * peers) - gx * cx) * cr + cell % (cr * peers) - row * cr
        slots_ref[pl.ds(slot, 1)] = (cells == here).astype(jnp.float32)
        return carry

    lax.fori_loop(0, cell_ref.shape[0], station, 0)
    place_ref[...] = slots_ref[...].astype(jnp.bfloat16)


class Frame:
    def __init__(self, sizes, cx, cr, work_ref):
        self.peers, self.cx, self.cr = sizes["row"], cx, cr
        self.fields, self.lanes = work_ref.shape[1], work_ref.shape[3]
        self.rows = work_ref.shape[2] - 2 * PAD
        self.blocks = self.rows // 8
        gx, self.row, self.core, self.group = position(sizes)
        self.odd = gx % 2
        self.even = 1 - self.odd
        self.left = (gx > 0).astype(jnp.int32)
        self.right = (gx < sizes["gx"] - 1).astype(jnp.int32)
        self.sides = 1 if self.peers == 2 else 2
        self.own = PAD + HALO * self.row if self.peers == 2 else PAD + HALO
        if self.peers == 2:
            self.own = pl.multiple_of(self.own, 8)
        self.pair_at = 2 * cx * self.even
        self.far_at = 2 * cx * self.odd

    def halo(self, side):
        if self.peers == 2:
            return PAD + self.cr * (1 - self.row)
        return self.own - HALO if side == 0 else self.own + self.cr

    def clear(self, low, high, *works):
        zero = jnp.zeros((PAD, self.lanes), jnp.float32)

        def one(x, carry):
            for f in range(self.fields):
                for w in works:
                    w[x, f, pl.ds(0, PAD)] = zero
                    w[x, f, pl.ds(PAD + self.rows, PAD)] = zero
            return carry

        lax.fori_loop(low, high, one, 0)

    def blank(self, low, high, work):
        zero = jnp.zeros((8, self.lanes), jnp.float32)

        def one(x, carry):
            for f in range(self.fields):
                for b in range(self.blocks):
                    work[x, f, pl.ds(PAD + 8 * b, 8)] = zero
            return carry

        lax.fori_loop(low, high, one, 0)

    def place(self, source, work, at, r, low=0, high=None):
        h = source.shape[2]

        def one(i, carry):
            for f in range(self.fields):
                work[at + i, f, pl.ds(r, h)] = source[i, f]
            return carry

        lax.fori_loop(low, source.shape[0] if high is None else high, one, 0)

    def place_edge(self, edge_ref, work, at):
        for side in range(self.sides):
            self.place(edge_ref.at[side], work, at, pl.multiple_of(self.halo(side), 8))

    def layer(self, coef_ref, src, store, x, base, count):
        fields = self.fields
        v = [[src[x, f, pl.ds(base + 8 * b, 8)] for b in range(count)] for f in range(fields)]
        for f in range(fields):
            c = [coef_ref[f, i] for i in range(NCOEF)]
            for b in range(count):
                r = base + 8 * b
                total = c[0] * v[0][b]
                for g in range(1, fields):
                    total = total + c[g] * v[g][b]
                near = src[x, f, pl.ds(r + 1, 8)] + src[x, f, pl.ds(r - 1, 8)]
                far = src[x, f, pl.ds(r + 2, 8)] + src[x, f, pl.ds(r - 2, 8)]
                side = c[fields] * near + c[fields + 1] * far
                one = c[fields + 2] * src[x + 1, f, pl.ds(r, 8)] + c[fields + 3] * src[x - 1, f, pl.ds(r, 8)]
                two = c[fields + 4] * src[x + 2, f, pl.ds(r, 8)] + c[fields + 5] * src[x - 2, f, pl.ds(r, 8)]
                store(x, f, b, (total + side) + (one + two))

    def sweep(self, coef_ref, src, dst, low, high):
        def store(x, f, b, value):
            dst[x, f, pl.ds(PAD + 8 * b, 8)] = value

        def body(x, carry):
            self.layer(coef_ref, src, store, x, PAD, self.blocks)
            return carry

        lax.fori_loop(low, high, body, 0)
        if self.peers > 2:
            for side, edge in ((0, 0), (1, self.peers - 1)):

                @pl.when(self.row == edge)
                def _(side=side):
                    def wipe(x, carry):
                        for f in range(self.fields):
                            dst[x, f, pl.ds(self.halo(side), HALO)] = jnp.zeros(
                                (HALO, self.lanes), jnp.float32
                            )
                        return carry

                    lax.fori_loop(low, high, wipe, 0)

    def pressure(self, weight_ref, p_ref, t, read, low, high):
        def one(x, carry):
            for b in range(self.cr // 8):
                p = weight_ref[0] * read(x, 0, 8 * b)
                for f in range(1, self.fields):
                    p = p + weight_ref[f] * read(x, f, 8 * b)
                p_ref[t, pl.ds(pl.multiple_of((x - self.cx) * self.cr + 8 * b, 8), 8)] = p
            return carry

        lax.fori_loop(low, high, one, 0)


def near_kernel(sizes, coef_ref, weight_ref, *refs):
    own_refs, pair_refs = refs[:PIECES], refs[PIECES : 2 * PIECES]
    r0_ref, rp_ref, strip_ref, p_ref, w0_ref, w1_ref = refs[2 * PIECES :]
    step, cr = own_refs[0].shape[0], own_refs[0].shape[2]
    cx = step * PIECES
    z = Frame(sizes, cx, cr, w0_ref)
    first = cx * z.even
    z.clear(first, first + 2 * cx, w0_ref, w1_ref)
    for i in range(PIECES):
        z.place(own_refs[i], w0_ref, cx + i * step, z.own)
        z.place(pair_refs[i], w0_ref, z.pair_at + i * step, z.own)
    z.place_edge(r0_ref, w0_ref, cx)
    z.place_edge(rp_ref, w0_ref, z.pair_at)
    p_ref[...] = jnp.zeros_like(p_ref)
    works = [w0_ref, w1_ref]
    for t in range(1, STEPS):
        src, dst = works[(t - 1) % 2], works[t % 2]
        low = (cx + 2 * t) * z.even + 2 * t * z.odd
        high = (3 * cx - 2 * t) * z.even + (2 * cx - 2 * t) * z.odd
        z.sweep(coef_ref, src, dst, low, high)
        edge = low * z.even + (high - STRIP) * z.odd
        for i in range(STRIP):
            strip_ref[t - 1, i] = dst[edge + i, :, pl.ds(PAD, z.rows)]
        z.pressure(
            weight_ref, p_ref, t - 1,
            lambda x, f, r, dst=dst: dst[x, f, pl.ds(z.own + r, 8)],
            cx + 2 * t * z.even, 2 * cx - 2 * t * z.odd,
        )


def far_kernel(sizes, coef_ref, weight_ref, place_ref, *refs):
    own_refs, far_refs = refs[:PIECES], refs[PIECES : 2 * PIECES]
    r0_ref, rc_ref, strip_ref, part_ref, out_ref = refs[2 * PIECES : 2 * PIECES + 5]
    cycle_refs = refs[2 * PIECES + 5 : -3]
    w0_ref, w1_ref, p_ref = refs[-3:]
    step, cr = own_refs[0].shape[0], own_refs[0].shape[2]
    cx = step * PIECES
    z = Frame(sizes, cx, cr, w0_ref)
    first = cx * z.odd
    z.clear(first, first + 2 * cx, w0_ref, w1_ref)
    for i in range(PIECES):
        z.place(own_refs[i], w0_ref, cx + i * step, z.own)
        z.place(far_refs[i], w0_ref, z.far_at + i * step, z.own)
    z.place_edge(r0_ref, w0_ref, cx)
    z.place_edge(rc_ref, w0_ref, z.far_at)
    z.blank(cx - 2, cx - 2 + 2 * (1 - z.left), w1_ref)
    z.blank(2 * cx, 2 * cx + 2 * (1 - z.right), w1_ref)
    works = [w0_ref, w1_ref]
    for t in range(1, STEPS):
        src, dst = works[(t - 1) % 2], works[t % 2]
        reach = HALO - 2 * t
        low = (cx - reach * z.left) * z.even + (2 * cx - 2 * t) * z.odd
        high = (cx + 2 * t) * z.even + (2 * cx + reach * z.right) * z.odd
        z.sweep(coef_ref, src, dst, low, high)
        edge = (cx + 2 * t) * z.even + (2 * cx - 2 * t - STRIP) * z.odd
        for i in range(STRIP):
            dst[edge + i, :, pl.ds(PAD, z.rows)] = strip_ref[t - 1, i]
        p_ref[t - 1] = part_ref[t - 1]
        z.pressure(
            weight_ref, p_ref, t - 1,
            lambda x, f, r, dst=dst: dst[x, f, pl.ds(z.own + r, 8)],
            cx * z.even + (2 * cx - 2 * t) * z.odd, (cx + 2 * t) * z.even + 2 * cx * z.odd,
        )
    src = works[(STEPS - 1) % 2]

    def store_out(x, f, b, value):
        out_ref[x - cx, f, pl.ds(8 * b, 8)] = value

    def body_out(x, carry):
        z.layer(coef_ref, src, store_out, x, z.own, cr // 8)
        return carry

    lax.fori_loop(cx, 2 * cx, body_out, 0)
    z.pressure(weight_ref, p_ref, STEPS - 1, lambda x, f, r: out_ref[x - cx, f, pl.ds(r, 8)], cx, 2 * cx)
    dot = functools.partial(jnp.dot, preferred_element_type=jnp.float32)
    for t in range(STEPS):
        high, low = halves(p_ref[t])
        picked = dot(place_ref[...], high) + dot(place_ref[...], low)
        for k, ref in enumerate(cycle_refs):
            ref[t] = picked[k * CAP : (k + 1) * CAP]


def inverse_kernel(sizes, *refs):
    cores = sizes["ta"]
    sources = refs[:cores]
    table_ref, out_ref, x_ref, sems = refs[cores:]
    fields, cx, cr, ct = out_ref.shape
    _, _, core, group = position(sizes)
    table = [
        jnp.concatenate([table_ref[i, (group + k) % cores, core] for k in range(cores)], axis=0)
        for i in range(2)
    ]
    copies = []
    for f in range(fields):
        x = jnp.concatenate([s[:, f].reshape(cx * cr, ct) for s in sources], axis=1)
        x_ref[f] = dot3(*halves(x), *table).reshape(cx, cr, ct)
        copies.append(pltpu.make_async_copy(x_ref.at[f], out_ref.at[f], sems.at[f]))
        copies[f].start()
    for copy in copies:
        copy.wait()


def spectra_kernel(sizes, *refs):
    peers = sizes["row"]
    received = refs[:peers]
    window_ref, table_ref, out_ref = refs[peers:]
    _, row, core, _ = position(sizes)
    share = peers // sizes["ta"]
    blocks = []
    for j in range(share):
        hop = (row - (core * share + j) + peers) % peers
        value = jnp.where(hop == 0, received[0][...], 0.0)
        for k in range(1, peers):
            value = jnp.where(hop == k, received[k][...], value)
        blocks.append(value)
    x = blocks[0] if share == 1 else jnp.concatenate(blocks, axis=1)
    n = x.shape[1]
    dot = functools.partial(jnp.dot, preferred_element_type=jnp.float32)
    total = None
    for t in range(0, STEPS, 2):
        pair = jnp.concatenate(
            [x[i] * (window_ref[i].astype(jnp.float32) * 0.125) for i in (t, t + 1)], axis=1
        )
        high, low = halves(pair)
        both = dot(jnp.concatenate([high, low], axis=0), table_ref[0, t // 2])
        part = both[:n] + both[n:] + dot(high, table_ref[1, t // 2])
        total = part if total is None else total + part
    out_ref[0] = total


def spec(space, n):
    return [pl.BlockSpec(memory_space=space)] * n


def limit(mib):
    return pltpu.CompilerParams(vmem_limit_bytes=mib << 20)


def work_for(flops):
    return pl.CostEstimate(flops=flops, bytes_accessed=10**6, transcendentals=0)


def local(
    sizes,
    conserved,
    diffusivity,
    axial_speed,
    coupling,
    pressure_weights,
    station_cell,
    owner_row,
    window_table,
):
    fields, cx, cr, ct = conserved.shape
    nx, peers, cores = sizes["gx"], sizes["row"], sizes["ta"]
    assert cx == HALO and nx % 2 == 0 and peers % cores == 0
    share = peers // cores
    step = cx // PIECES
    sides = 1 if peers == 2 else 2
    basis, eigen = mode_basis(ct * cores, cores)
    blocks = basis.reshape(cores, ct, cores, ct).transpose(0, 2, 3, 1)
    ahead = split_const(blocks)
    back = split_const(blocks.transpose(0, 1, 3, 2))

    def shape(*dims):
        return jax.ShapeDtypeStruct(dims, jnp.float32)

    def others(x):
        return [
            lax.ppermute(x, "ta", [((c + k) % cores, c) for c in range(cores)])
            for k in range(1, cores)
        ]

    sources = others(conserved)
    part = pl.pallas_call(
        functools.partial(stage_kernel, sizes),
        out_shape=shape(cx, fields, cr, ct),
        in_specs=spec(VMEM, 2),
        out_specs=pl.BlockSpec(memory_space=VMEM),
        compiler_params=limit(8),
        cost_estimate=work_for(10**7),
        name="stage",
    )(conserved, ahead)
    tile = shape(step, fields, cr, ct)
    edge = shape(sides, cx, fields, HALO, ct)
    early = PIECES // 2
    own = list(
        pl.pallas_call(
            functools.partial(forward_kernel, sizes, 0, early, False),
            out_shape=(tile,) * early,
            in_specs=spec(VMEM, cores + 1),
            out_specs=tuple(spec(VMEM, early)),
            compiler_params=limit(8),
            cost_estimate=work_for(10**6),
            name="forward_early",
        )(part, ahead, *sources)
    )
    *rest, e0 = pl.pallas_call(
        functools.partial(forward_kernel, sizes, early, PIECES - early, True),
        out_shape=(tile,) * (PIECES - early) + (edge,),
        in_specs=spec(VMEM, cores + 1 + early),
        out_specs=tuple(spec(VMEM, PIECES - early + 1)),
        compiler_params=limit(8),
        cost_estimate=work_for(10**6),
        name="forward_late",
    )(part, ahead, *sources, *own)
    own += rest

    swap = [(i, i ^ 1) for i in range(nx)]
    onward = [(i, i + 2 if i % 2 == 0 else i - 2) for i in range(nx)]
    onward = [(a, b) for a, b in onward if 0 <= b < nx]

    r0 = []
    for side in range(sides):
        if peers == 2:
            turn = [(0, 1), (1, 0)]
        else:
            turn = [(r, r + 1) for r in range(peers - 1)]
            if side:
                turn = [(b, a) for a, b in turn]
        hops = [
            (r * cores + (g + r // share) % cores, q * cores + (g + q // share) % cores)
            for r, q in turn
            for g in range(cores)
        ]
        r0.append(lax.ppermute(e0[side : side + 1], ("row", "ta"), hops))
    r0 = r0[0] if sides == 1 else jnp.concatenate(r0, axis=0)
    pair, far = [], []
    for x in own:
        pair.append(lax.ppermute(x, "gx", swap))
    rp = lax.ppermute(r0, "gx", swap)
    rc = lax.ppermute(rp, "gx", onward)
    for x in pair:
        far.append(lax.ppermute(x, "gx", onward))

    lines = np.broadcast_to(eigen[:, None, :], (cores, 8, ct)).astype(np.float32)
    coef, place = pl.pallas_call(
        functools.partial(prepare_kernel, sizes, cx, cr),
        out_shape=(
            shape(fields, NCOEF, 8, ct),
            jax.ShapeDtypeStruct((peers * CAP, cx * cr), jnp.bfloat16),
        ),
        in_specs=spec(SMEM, 5) + spec(VMEM, 1),
        out_specs=tuple(spec(VMEM, 2)),
        scratch_shapes=[
            pltpu.VMEM((peers * CAP, cx * cr), jnp.float32),
            pltpu.SMEM((peers,), jnp.int32),
        ],
        compiler_params=limit(4),
        cost_estimate=work_for(10**6),
        name="prepare",
    )(diffusivity, axial_speed, coupling, station_cell, owner_row.reshape(-1), lines)

    rows = cr + HALO * sides
    work = pltpu.VMEM((3 * cx, fields, rows + 2 * PAD, ct), jnp.float32)
    strip, parts = pl.pallas_call(
        functools.partial(near_kernel, sizes),
        out_shape=(shape(STEPS - 1, STRIP, fields, rows, ct), shape(STEPS - 1, cx * cr, ct)),
        in_specs=spec(VMEM, 1) + spec(SMEM, 1) + spec(VMEM, 2 * PIECES + 2),
        out_specs=tuple(spec(VMEM, 2)),
        scratch_shapes=[work, work],
        compiler_params=limit(20),
        cost_estimate=work_for(10**7),
        name="near",
    )(coef, pressure_weights, *own, *pair, r0, rp)
    modes, *cycles = pl.pallas_call(
        functools.partial(far_kernel, sizes),
        out_shape=(shape(cx, fields, cr, ct),) + (shape(STEPS, CAP, ct),) * peers,
        in_specs=spec(VMEM, 1) + spec(SMEM, 1) + spec(VMEM, 1 + 2 * PIECES + 4),
        out_specs=tuple(spec(VMEM, 1 + peers)),
        scratch_shapes=[work, work, pltpu.VMEM((STEPS, cx * cr, ct), jnp.float32)],
        compiler_params=limit(20),
        cost_estimate=work_for(10**7),
        name="rest",
    )(coef, pressure_weights, place, *own, *far, r0, rc, strip, parts)

    received = [cycles[0]]
    for k in range(1, peers):
        pairs = []
        for j in range(peers):
            pairs.append((j * cores + j // share, (j + k) % peers * cores + j // share))
        received.append(lax.ppermute(cycles[k], ("row", "ta"), pairs))

    advanced = pl.pallas_call(
        functools.partial(inverse_kernel, sizes),
        out_shape=jax.ShapeDtypeStruct(conserved.shape, jnp.float32),
        in_specs=spec(VMEM, cores + 1),
        out_specs=pl.BlockSpec(memory_space=HBM),
        scratch_shapes=[pltpu.VMEM(conserved.shape, jnp.float32), pltpu.SemaphoreType.DMA((fields,))],
        compiler_params=limit(8),
        cost_estimate=work_for(10**6),
        name="inverse",
    )(modes, *others(modes), back)
    spectra = pl.pallas_call(
        functools.partial(spectra_kernel, sizes),
        out_shape=shape(1, share * CAP, NFREQ * 2 * NM),
        in_specs=spec(VMEM, peers) + spec(SMEM, 1) + spec(VMEM, 1),
        out_specs=pl.BlockSpec(memory_space=VMEM),
        compiler_params=limit(8),
        cost_estimate=work_for(10**6),
        name="spectra",
    )(*received, window_table, split_const(spectrum_table(ct).reshape(STEPS // 2, 2 * ct, -1)))
    return (advanced, spectra)


def solution(mesh):
    in_specs = (
        P(None, "gx", "row", "ta"),
        P(),
        P(),
        P(),
        P(),
        P(("gx", "row")),
        P(("gx", "row"), None),
        P(),
    )
    out_specs = (P(None, "gx", "row", "ta"), P(("gx", "row"), "ta", None))

    def body(*args):
        return local(dict(mesh.shape), *args)

    return jax.shard_map(body, mesh=mesh, in_specs=in_specs, out_specs=out_specs, check_vma=False)
```

time: 237 us -> 48.6 us (0.21)
  waiting for transfers between devices: 89.4 us -> 6.08 us
  matrix products: 49 us -> 0 us
  starting transfers between devices: 66.7 us -> 25.6 us
  local copies, waits for them, and re-layouts: 16.3 us -> 2.08 us
  Pallas kernels: 0 us -> 13.7 us
  other arithmetic: 5.64 us -> 0 us
  blocking collectives: 5.6 us -> 0 us
  between operations: 3.86 us -> 0.9 us
    ppermute x24 -> x14, waiting for transfers between devices: 89.1 us -> 6.08 us  [the longest x1 3.36 us: local(): received.append(lax.ppermute(cycles[k], ('row', 'ta'), pairs))]
    dot_general x17 -> x0, matrix products: 49 us -> none  [the longest x4 39.7 us: advance(): mixed = jnp.einsum('fg,gxrt->fxrt', coupling, center, precision=exact_mode)]
    ppermute x24 -> x14, starting transfers between devices: 53.4 us -> 25.6 us  [the longest x4 12.4 us: local(): far.append(lax.ppermute(x, 'gx', onward))]
    pallas_call x0 -> x8, Pallas kernels: none -> 13.7 us  [the longest x1 4.65 us: local(): pl.pallas_call(functools.partial(far_kernel, sizes), out_shape=(shape(cx,...]
    all_to_all x4 -> x0, starting transfers between devices: 13.3 us -> none  [local(): lax.all_to_all(buffers[step_index], 'row', split_axis=0, concat_axis=0, t...]
    unnamed x1 -> x0, blocking collectives: 5.6 us -> none
    slice x11 -> x0, local copies, waits for them, and re-layouts: 5.45 us -> none  [the longest x7 3.7 us: padded_2(): leading = lax.slice_in_dim(x, 0, width, axis=dim)]
    ppermute x8 -> x0, local copies, waits for them, and re-layouts: 3.52 us -> none  [the longest x4 1.76 us: padded_2(): before = lax.ppermute(last, axis, up)]
  transfers between devices with their start and end apart: 28 -> 14, of which waited for: 13 -> 4; matrix products, arithmetic and copies ran while one was open for 19% -> 0% of each run, Pallas kernels for 0% -> 15%
where the time goes in v2:
time: 48.6 us; the launch traced here: 48.3 us
  starting transfers between devices  25.6 us (53%)
  Pallas kernels  13.7 us (28%)
  waiting for transfers between devices  6.08 us (13%)
  local copies, waits for them, and re-layouts  2.08 us (4%)
  between operations  0.9 us (2%)
    ppermute x4, starting transfers between devices, local(): far.append(lax.ppermute(x, 'gx', onward))  12.4 us
    pallas_call x1, Pallas kernels, local(): pl.pallas_call(functools.partial(far_kernel, sizes), out_shape=(shape(cx,...  4.65 us
    pallas_call x1, Pallas kernels, local(): pl.pallas_call(functools.partial(near_kernel, sizes), out_shape=(shape(ST...  3.65 us
    ppermute x2, starting transfers between devices, others(): lax.ppermute(x, 'ta', [((c + k) % cores, c) for c in range(cores)])  3.38 us
    ppermute x1, waiting for transfers between devices, local(): received.append(lax.ppermute(cycles[k], ('row', 'ta'), pairs))  3.36 us
    ppermute x1, starting transfers between devices, local(): rc = lax.ppermute(rp, 'gx', onward)  3.19 us
    ppermute x4, starting transfers between devices, local(): pair.append(lax.ppermute(x, 'gx', swap))  2.93 us
    unnamed x24, local copies, waits for them, and re-layouts  2.08 us
  transfers between devices with their start and end apart: 14, of which 4 were waited for; matrix products, arithmetic and copies ran while one was open for 0% of the time, Pallas kernels for 15%

profile of v2, /device:TPU:9, one launch (start us, length us, event | category | flops | bytes accessed | tf_op | source)
XLA Modules:
  0.0 48.3 jit_solution(4551526503068945744)
XLA Ops:
  0.6 0.7 %collective-permute-start = (f32[5,8,32,128]{3,2,1,0:T(8,128)}, f32[5,8,32,128]{3,2,1,0:T(8,128)S(1)}, u32[]{:S(2)}, u32[]{:S(2)}) collective-permute-start(f32[5,8,32,128]{3,2,1,0:T(8,128)} %own_ref.1), channel_id=1, source_target_pairs={{1,0},{0,1},{3,2},{2,3},{5,4},{4,5},{7,6},{6,7},{9,8},{8,9},{11,10... | collective-permute-start | bytes 1966088 | tf_op jit(solution)/shard_map/ppermute | solution.py:451
  1.4 0.9 %copy-done.1 = bf16[2,2,2,128,128]{4,3,2,1,0:T(8,128)(2,1)S(1)} copy-done((bf16[2,2,2,128,128]{4,3,2,1,0:T(8,128)(2,1)S(1)}, bf16[2,2,2,128,128]{4,3,2,1,0:T(8,128)(2,1)}, u32[]{:S(2)}) %copy-start.1) | copy-done | bytes 262168
  2.3 1.1 %copy-done.2 = f32[5,8,32,128]{3,2,1,0:T(8,128)S(1)} copy-done((f32[5,8,32,128]{3,2,1,0:T(8,128)S(1)}, f32[5,8,32,128]{3,2,1,0:T(8,128)}, u32[]{:S(2)}) %copy-start.2) | copy-done | bytes 655384
  3.4 0.0 copy-start.9
  3.4 0.0 copy-start.10
  3.4 0.0 copy-start.6
  3.5 0.4 stage.1.part_ref
  3.9 0.0 collective-permute-done.refs_0_
  3.9 0.3 forward_early.1
  4.2 0.3 forward_late.1
  4.5 1.2 %collective-permute-start.9 = (f32[1,8,5,8,128]{4,3,2,1,0:T(8,128)S(1)}, f32[1,8,5,8,128]{4,3,2,1,0:T(8,128)S(1)}, u32[]{:S(2)}, u32[]{:S(2)}) collective-permute-start(f32[1,8,5,8,128]{4,3,2,1,0:T(8,128)S(1)} %get-tuple-element.20), channel_id=1, source_target_pairs={{0,3},{1,2},{3,0},{2,1},{4,7},{5,6},{7,4},{6,5},{8,11},{9,10},{11,... | collective-permute-start | bytes 491528 | tf_op jit(solution)/shard_map/ppermute | solution.py:507
  5.7 1.2 %collective-permute-start.5 = (f32[2,5,32,128]{3,2,1,0:T(8,128)S(1)}, f32[2,5,32,128]{3,2,1,0:T(8,128)S(1)}, u32[]{:S(2)}, u32[]{:S(2)}) collective-permute-start(f32[2,5,32,128]{3,2,1,0:T(8,128)S(1)} %get-tuple-element.18.refs_2_), channel_id=1, source_target_pairs={{0,4},{4,0},{8,12},{12,8},{16,20},{20,16},{24,28},{28,24},{1,5},{5... | collective-permute-start | bytes 491528 | tf_op jit(solution)/shard_map/ppermute | solution.py:511
  6.9 0.2 collective-permute-start.7
  7.2 1.2 %collective-permute-start.1 = (f32[2,5,32,128]{3,2,1,0:T(8,128)S(1)}, f32[2,5,32,128]{3,2,1,0:T(8,128)S(1)}, u32[]{:S(2)}, u32[]{:S(2)}) collective-permute-start(f32[2,5,32,128]{3,2,1,0:T(8,128)S(1)} %get-tuple-element.16.refs_1_.refs_0_), channel_id=1, source_target_pairs={{0,4},{4,0},{8,12},{12,8},{16,20},{20,16},{24,28},{28,24},{1,5},{5... | collective-permute-start | bytes 491528 | tf_op jit(solution)/shard_map/ppermute | solution.py:511
  8.4 0.2 collective-permute-start.3
  8.6 2.1 %collective-permute-done.9.refs_8_ = f32[1,8,5,8,128]{4,3,2,1,0:T(8,128)S(1)} collective-permute-done((f32[1,8,5,8,128]{4,3,2,1,0:T(8,128)S(1)}, f32[1,8,5,8,128]{4,3,2,1,0:T(8,128)S(1)}, u32[]{:S(2)}, u32[]{:S(2)}) %collective-permute-start.9) | collective-permute-done | bytes 163872 | tf_op jit(solution)/shard_map/ppermute | solution.py:507
  10.7 1.2 %collective-permute-start.10 = (f32[1,8,5,8,128]{4,3,2,1,0:T(8,128)S(1)}, f32[1,8,5,8,128]{4,3,2,1,0:T(8,128)S(1)}, u32[]{:S(2)}, u32[]{:S(2)}) collective-permute-start(f32[1,8,5,8,128]{4,3,2,1,0:T(8,128)S(1)} %collective-permute-done.9.refs_8_), channel_id=1, source_target_pairs={{0,4},{4,0},{8,12},{12,8},{16,20},{20,16},{24,28},{28,24},{1,5},{5... | collective-permute-start | bytes 491528 | tf_op jit(solution)/shard_map/ppermute | solution.py:512
  11.9 0.0 collective-permute-done.5.refs_6_
  11.9 3.2 %collective-permute-start.6 = (f32[2,5,32,128]{3,2,1,0:T(8,128)S(1)}, f32[2,5,32,128]{3,2,1,0:T(8,128)S(1)}, u32[]{:S(2)}, u32[]{:S(2)}) collective-permute-start(f32[2,5,32,128]{3,2,1,0:T(8,128)S(1)} %collective-permute-done.5.refs_6_), channel_id=1, source_target_pairs={{0,8},{8,16},{12,4},{16,24},{20,12},{28,20},{1,9},{9,17},{13,5},{1... | collective-permute-start | bytes 491528 | tf_op jit(solution)/shard_map/ppermute | solution.py:515
  15.1 0.0 collective-permute-done.7.refs_7_
  15.2 3.2 %collective-permute-start.8 = (f32[2,5,32,128]{3,2,1,0:T(8,128)S(1)}, f32[2,5,32,128]{3,2,1,0:T(8,128)S(1)}, u32[]{:S(2)}, u32[]{:S(2)}) collective-permute-start(f32[2,5,32,128]{3,2,1,0:T(8,128)S(1)} %collective-permute-done.7.refs_7_), channel_id=1, source_target_pairs={{0,8},{8,16},{12,4},{16,24},{20,12},{28,20},{1,9},{9,17},{13,5},{1... | collective-permute-start | bytes 491528 | tf_op jit(solution)/shard_map/ppermute | solution.py:515
  18.4 0.0 collective-permute-done.1.refs_4_
  18.4 2.8 %collective-permute-start.2 = (f32[2,5,32,128]{3,2,1,0:T(8,128)S(1)}, f32[2,5,32,128]{3,2,1,0:T(8,128)S(1)}, u32[]{:S(2)}, u32[]{:S(2)}) collective-permute-start(f32[2,5,32,128]{3,2,1,0:T(8,128)S(1)} %collective-permute-done.1.refs_4_), channel_id=1, source_target_pairs={{0,8},{8,16},{12,4},{16,24},{20,12},{28,20},{1,9},{9,17},{13,5},{1... | collective-permute-start | bytes 491528 | tf_op jit(solution)/shard_map/ppermute | solution.py:515
  21.2 0.3 collective-permute-done.3.refs_5_
  21.5 3.2 %collective-permute-start.4 = (f32[2,5,32,128]{3,2,1,0:T(8,128)S(1)}, f32[2,5,32,128]{3,2,1,0:T(8,128)S(1)}, u32[]{:S(2)}, u32[]{:S(2)}) collective-permute-start(f32[2,5,32,128]{3,2,1,0:T(8,128)S(1)} %collective-permute-done.3.refs_5_), channel_id=1, source_target_pairs={{0,8},{8,16},{12,4},{16,24},{20,12},{28,20},{1,9},{9,17},{13,5},{1... | collective-permute-start | bytes 491528 | tf_op jit(solution)/shard_map/ppermute | solution.py:515
  24.7 0.3 collective-permute-done.10.refs_9_
  25.0 3.2 %collective-permute-start.11 = (f32[1,8,5,8,128]{4,3,2,1,0:T(8,128)S(1)}, f32[1,8,5,8,128]{4,3,2,1,0:T(8,128)S(1)}, u32[]{:S(2)}, u32[]{:S(2)}) collective-permute-start(f32[1,8,5,8,128]{4,3,2,1,0:T(8,128)S(1)} %collective-permute-done.10.refs_9_), channel_id=1, source_target_pairs={{0,8},{8,16},{12,4},{16,24},{20,12},{28,20},{1,9},{9,17},{13,5},{1... | collective-permute-start | bytes 491528 | tf_op jit(solution)/shard_map/ppermute | solution.py:513
  28.2 0.0 copy-done.4
  28.2 0.0 copy-done.5
  28.2 0.0 copy-done.7
  28.2 0.0 copy-done.8
  28.3 1.3 %prepare.1 = (f32[5,11,8,128]{3,2,1,0:T(8,128)S(1)}, bf16[32,256]{1,0:T(8,128)(2,1)S(1)}) custom-call(f32[5]{0:T(128)S(1)} %copy-done.7, f32[5]{0:T(128)S(1)} %copy-done.8, f32[5,5]{1,0:T(8,128)S(1)} %copy-done.5, s32[32]{0:T(128)S(1)} %copy-done.9, s32[32]{0:T(128)S(1)} %bitcast.1, f32[2,8,128]{2,1,0:T(8,128)S(1)} %copy-done.4), custom_call_target="tpu_custom_call" | custom-call | flops 1000000 | bytes 1000000 | tf_op jit(solution)/shard_map/prepare/pallas_call | solution.py:518
  29.6 0.0 copy-start
  29.6 0.0 copy-start.11
  29.6 3.6 %near.1 = (f32[3,4,5,40,128]{4,3,2,1,0:T(8,128)S(1)}, f32[3,256,128]{2,1,0:T(8,128)S(1)}) custom-call(f32[5,11,8,128]{3,2,1,0:T(8,128)S(1)} %get-tuple-element.14.coef_ref, f32[5]{0:T(128)S(1)} %copy-done.6, f32[2,5,32,128]{3,2,1,0:T(8,128)S(1)} %get-tuple-element.16.refs_1_.refs_0_, f32[2,5,32,128]{3,2,1,0:T(8,128)S(1)} %get-tuple-element.17.refs_2_.refs_1_, ...), custom_call_target="tpu_custom_call" | custom-call | flops 10000000 | bytes 1000000 | tf_op jit(solution)/shard_map/near/pallas_call | solution.py:537
  33.3 0.0 collective-permute-done.6.refs_6_
  33.3 0.0 collective-permute-done.8.refs_7_
  33.3 0.0 collective-permute-done.2.refs_4_
  33.3 0.0 collective-permute-done.4.refs_5_
  33.3 0.0 collective-permute-done.11.refs_9_
  33.3 0.0 copy-start.3
  33.3 4.6 %rest.1 = (f32[8,5,32,128]{3,2,1,0:T(8,128)S(1)}, f32[4,16,128]{2,1,0:T(8,128)S(1)}, f32[4,16,128]{2,1,0:T(8,128)S(1)}) custom-call(f32[5,11,8,128]{3,2,1,0:T(8,128)S(1)} %get-tuple-element.14.coef_ref, f32[5]{0:T(128)S(1)} %copy-done.6, bf16[32,256]{1,0:T(8,128)(2,1)S(1)} %get-tuple-element.15.place_ref, ...), custom_call_target="tpu_custom_call" | custom-call | flops 10000000 | bytes 1000000 | tf_op jit(solution)/shard_map/rest/pallas_call | solution.py:547
  38.0 2.6 %collective-permute-start.12 = (f32[8,5,32,128]{3,2,1,0:T(8,128)S(1)}, f32[8,5,32,128]{3,2,1,0:T(8,128)S(1)}, u32[]{:S(2)}, u32[]{:S(2)}) collective-permute-start(f32[8,5,32,128]{3,2,1,0:T(8,128)S(1)} %get-tuple-element.23.refs_0_), channel_id=1, source_target_pairs={{1,0},{0,1},{3,2},{2,3},{5,4},{4,5},{7,6},{6,7},{9,8},{8,9},{11,10... | collective-permute-start | bytes 1966088 | tf_op jit(solution)/shard_map/ppermute | solution.py:451
  40.6 1.3 %collective-permute-start.13 = (f32[4,16,128]{2,1,0:T(8,128)S(1)}, f32[4,16,128]{2,1,0:T(8,128)S(1)}, u32[]{:S(2)}, u32[]{:S(2)}) collective-permute-start(f32[4,16,128]{2,1,0:T(8,128)S(1)} %get-tuple-element.25), channel_id=1, source_target_pairs={{0,2},{3,1},{4,6},{7,5},{8,10},{11,9},{12,14},{15,13},{16,18},{19,... | collective-permute-start | bytes 98312 | tf_op jit(solution)/shard_map/ppermute | solution.py:563
  41.9 3.4 %collective-permute-done.13.refs_1_ = f32[4,16,128]{2,1,0:T(8,128)S(1)} collective-permute-done((f32[4,16,128]{2,1,0:T(8,128)S(1)}, f32[4,16,128]{2,1,0:T(8,128)S(1)}, u32[]{:S(2)}, u32[]{:S(2)}) %collective-permute-start.13) | collective-permute-done | bytes 32800 | tf_op jit(solution)/shard_map/ppermute | solution.py:563
  45.3 1.6 %spectra.1 = f32[1,16,1056]{2,1,0:T(8,128)} custom-call(f32[4,16,128]{2,1,0:T(8,128)S(1)} %get-tuple-element.24.refs_0_, f32[4,16,128]{2,1,0:T(8,128)S(1)} %collective-permute-done.13.refs_1_, s32[4]{0:T(128)S(1)} %copy-done.11, bf16[2,2,256,1056]{3,2,1,0:T(8,128)(2,1)S(1)} %copy-done), custom_call_target="tpu_custom_call" | custom-call | flops 1000000 | bytes 1000000 | tf_op jit(solution)/shard_map/spectra/pallas_call | solution.py:575
  46.9 0.0 collective-permute-done.12.refs_1_
  46.9 1.4 %inverse.1 = f32[5,8,32,128]{3,2,1,0:T(8,128)} custom-call(f32[8,5,32,128]{3,2,1,0:T(8,128)S(1)} %get-tuple-element.23.refs_0_, f32[8,5,32,128]{3,2,1,0:T(8,128)S(1)} %collective-permute-done.12.refs_1_, bf16[2,2,2,128,128]{4,3,2,1,0:T(8,128)(2,1)S(1)} %copy-done.3), custom_call_target="tpu_custom_call" | custom-call | flops 1000000 | bytes 1000000 | tf_op jit(solution)/shard_map/inverse/pallas_call | solution.py:565
  (12 shorter events, 0.0 us)
Async XLA Ops:
  0.6 3.3 %collective-permute-start = (f32[5,8,32,128]{3,2,1,0:T(8,128)}, f32[5,8,32,128]{3,2,1,0:T(8,128)S(1)}, u32[]{:S(2)}, u32[]{:S(2)}) collective-permute-start(f32[5,8,32,128]{3,2,1,0:T(8,128)} %own_ref.1), channel_id=1, source_target_pairs={{1,0},{0,1},{3,2},{2,3},{5,4},{4,5},{7,6},{6,7},{9,8},{8,9},{11,10... | collective-permute-start | bytes 1966088 | tf_op jit(solution)/shard_map/ppermute | solution.py:451
  1.4 0.9 %copy-start.1 = (bf16[2,2,2,128,128]{4,3,2,1,0:T(8,128)(2,1)S(1)}, bf16[2,2,2,128,128]{4,3,2,1,0:T(8,128)(2,1)}, u32[]{:S(2)}) copy-start(bf16[2,2,2,128,128]{4,3,2,1,0:T(8,128)(2,1)} %constant.8.clone.table_ref) | copy-start | bytes 786436
  2.3 1.1 %copy-start.2 = (f32[5,8,32,128]{3,2,1,0:T(8,128)S(1)}, f32[5,8,32,128]{3,2,1,0:T(8,128)}, u32[]{:S(2)}) copy-start(f32[5,8,32,128]{3,2,1,0:T(8,128)} %own_ref.1) | copy-start | bytes 1966084
  3.4 24.8 %copy-start.4 = (f32[2,8,128]{2,1,0:T(8,128)S(1)}, f32[2,8,128]{2,1,0:T(8,128)}, u32[]{:S(2)}) copy-start(f32[2,8,128]{2,1,0:T(8,128)} %constant.9.clone.eigen_ref) | copy-start | bytes 24580
  3.4 24.8 %copy-start.5 = (f32[5,5]{1,0:T(8,128)S(1)}, f32[5,5]{1,0:T(8,128)}, u32[]{:S(2)}) copy-start(f32[5,5]{1,0:T(8,128)} %mix_ref.1) | copy-start | bytes 304
  3.4 24.8 %copy-start.7 = (f32[5]{0:T(128)S(1)}, f32[5]{0:T(128)}, u32[]{:S(2)}) copy-start(f32[5]{0:T(128)} %rate_ref.1) | copy-start | bytes 64
  3.4 24.8 %copy-start.8 = (f32[5]{0:T(128)S(1)}, f32[5]{0:T(128)}, u32[]{:S(2)}) copy-start(f32[5]{0:T(128)} %speed_ref.1) | copy-start | bytes 64
  3.4 24.8 %copy-start.9 = (s32[32]{0:T(128)S(1)}, s32[32]{0:T(128)}, u32[]{:S(2)}) copy-start(s32[32]{0:T(128)} %cell_ref.1) | copy-start | bytes 388
  3.4 24.8 %copy-start.10 = (s32[32,1]{0,1:T(1,128)S(1)}, s32[32,1]{0,1:T(1,128)}, u32[]{:S(2)}) copy-start(s32[32,1]{0,1:T(1,128)} %param.18) | copy-start | bytes 388
  3.4 26.2 %copy-start.6 = (f32[5]{0:T(128)S(1)}, f32[5]{0:T(128)}, u32[]{:S(2)}) copy-start(f32[5]{0:T(128)} %weight_ref.3) | copy-start | bytes 64
  4.5 6.2 %collective-permute-start.9 = (f32[1,8,5,8,128]{4,3,2,1,0:T(8,128)S(1)}, f32[1,8,5,8,128]{4,3,2,1,0:T(8,128)S(1)}, u32[]{:S(2)}, u32[]{:S(2)}) collective-permute-start(f32[1,8,5,8,128]{4,3,2,1,0:T(8,128)S(1)} %get-tuple-element.20), channel_id=1, source_target_pairs={{0,3},{1,2},{3,0},{2,1},{4,7},{5,6},{7,4},{6,5},{8,11},{9,10},{11,... | collective-permute-start | bytes 491528 | tf_op jit(solution)/shard_map/ppermute | solution.py:507
  5.7 6.3 %collective-permute-start.5 = (f32[2,5,32,128]{3,2,1,0:T(8,128)S(1)}, f32[2,5,32,128]{3,2,1,0:T(8,128)S(1)}, u32[]{:S(2)}, u32[]{:S(2)}) collective-permute-start(f32[2,5,32,128]{3,2,1,0:T(8,128)S(1)} %get-tuple-element.18.refs_2_), channel_id=1, source_target_pairs={{0,4},{4,0},{8,12},{12,8},{16,20},{20,16},{24,28},{28,24},{1,5},{5... | collective-permute-start | bytes 491528 | tf_op jit(solution)/shard_map/ppermute | solution.py:511
  6.9 8.2 %collective-permute-start.7 = (f32[2,5,32,128]{3,2,1,0:T(8,128)S(1)}, f32[2,5,32,128]{3,2,1,0:T(8,128)S(1)}, u32[]{:S(2)}, u32[]{:S(2)}) collective-permute-start(f32[2,5,32,128]{3,2,1,0:T(8,128)S(1)} %get-tuple-element.19.refs_3_), channel_id=1, source_target_pairs={{0,4},{4,0},{8,12},{12,8},{16,20},{20,16},{24,28},{28,24},{1,5},{5... | collective-permute-start | bytes 491528 | tf_op jit(solution)/shard_map/ppermute | solution.py:511
  7.2 11.2 %collective-permute-start.1 = (f32[2,5,32,128]{3,2,1,0:T(8,128)S(1)}, f32[2,5,32,128]{3,2,1,0:T(8,128)S(1)}, u32[]{:S(2)}, u32[]{:S(2)}) collective-permute-start(f32[2,5,32,128]{3,2,1,0:T(8,128)S(1)} %get-tuple-element.16.refs_1_.refs_0_), channel_id=1, source_target_pairs={{0,4},{4,0},{8,12},{12,8},{16,20},{20,16},{24,28},{28,24},{1,5},{5... | collective-permute-start | bytes 491528 | tf_op jit(solution)/shard_map/ppermute | solution.py:511
  8.4 13.1 %collective-permute-start.3 = (f32[2,5,32,128]{3,2,1,0:T(8,128)S(1)}, f32[2,5,32,128]{3,2,1,0:T(8,128)S(1)}, u32[]{:S(2)}, u32[]{:S(2)}) collective-permute-start(f32[2,5,32,128]{3,2,1,0:T(8,128)S(1)} %get-tuple-element.17.refs_2_.refs_1_), channel_id=1, source_target_pairs={{0,4},{4,0},{8,12},{12,8},{16,20},{20,16},{24,28},{28,24},{1,5},{5... | collective-permute-start | bytes 491528 | tf_op jit(solution)/shard_map/ppermute | solution.py:511
  10.7 14.3 %collective-permute-start.10 = (f32[1,8,5,8,128]{4,3,2,1,0:T(8,128)S(1)}, f32[1,8,5,8,128]{4,3,2,1,0:T(8,128)S(1)}, u32[]{:S(2)}, u32[]{:S(2)}) collective-permute-start(f32[1,8,5,8,128]{4,3,2,1,0:T(8,128)S(1)} %collective-permute-done.9.refs_8_), channel_id=1, source_target_pairs={{0,4},{4,0},{8,12},{12,8},{16,20},{20,16},{24,28},{28,24},{1,5},{5... | collective-permute-start | bytes 491528 | tf_op jit(solution)/shard_map/ppermute | solution.py:512
  11.9 21.3 %collective-permute-start.6 = (f32[2,5,32,128]{3,2,1,0:T(8,128)S(1)}, f32[2,5,32,128]{3,2,1,0:T(8,128)S(1)}, u32[]{:S(2)}, u32[]{:S(2)}) collective-permute-start(f32[2,5,32,128]{3,2,1,0:T(8,128)S(1)} %collective-permute-done.5.refs_6_), channel_id=1, source_target_pairs={{0,8},{8,16},{12,4},{16,24},{20,12},{28,20},{1,9},{9,17},{13,5},{1... | collective-permute-start | bytes 491528 | tf_op jit(solution)/shard_map/ppermute | solution.py:515
  15.2 18.1 %collective-permute-start.8 = (f32[2,5,32,128]{3,2,1,0:T(8,128)S(1)}, f32[2,5,32,128]{3,2,1,0:T(8,128)S(1)}, u32[]{:S(2)}, u32[]{:S(2)}) collective-permute-start(f32[2,5,32,128]{3,2,1,0:T(8,128)S(1)} %collective-permute-done.7.refs_7_), channel_id=1, source_target_pairs={{0,8},{8,16},{12,4},{16,24},{20,12},{28,20},{1,9},{9,17},{13,5},{1... | collective-permute-start | bytes 491528 | tf_op jit(solution)/shard_map/ppermute | solution.py:515
  18.4 14.9 %collective-permute-start.2 = (f32[2,5,32,128]{3,2,1,0:T(8,128)S(1)}, f32[2,5,32,128]{3,2,1,0:T(8,128)S(1)}, u32[]{:S(2)}, u32[]{:S(2)}) collective-permute-start(f32[2,5,32,128]{3,2,1,0:T(8,128)S(1)} %collective-permute-done.1.refs_4_), channel_id=1, source_target_pairs={{0,8},{8,16},{12,4},{16,24},{20,12},{28,20},{1,9},{9,17},{13,5},{1... | collective-permute-start | bytes 491528 | tf_op jit(solution)/shard_map/ppermute | solution.py:515
  21.5 11.8 %collective-permute-start.4 = (f32[2,5,32,128]{3,2,1,0:T(8,128)S(1)}, f32[2,5,32,128]{3,2,1,0:T(8,128)S(1)}, u32[]{:S(2)}, u32[]{:S(2)}) collective-permute-start(f32[2,5,32,128]{3,2,1,0:T(8,128)S(1)} %collective-permute-done.3.refs_5_), channel_id=1, source_target_pairs={{0,8},{8,16},{12,4},{16,24},{20,12},{28,20},{1,9},{9,17},{13,5},{1... | collective-permute-start | bytes 491528 | tf_op jit(solution)/shard_map/ppermute | solution.py:515
  25.0 8.3 %collective-permute-start.11 = (f32[1,8,5,8,128]{4,3,2,1,0:T(8,128)S(1)}, f32[1,8,5,8,128]{4,3,2,1,0:T(8,128)S(1)}, u32[]{:S(2)}, u32[]{:S(2)}) collective-permute-start(f32[1,8,5,8,128]{4,3,2,1,0:T(8,128)S(1)} %collective-permute-done.10.refs_9_), channel_id=1, source_target_pairs={{0,8},{8,16},{12,4},{16,24},{20,12},{28,20},{1,9},{9,17},{13,5},{1... | collective-permute-start | bytes 491528 | tf_op jit(solution)/shard_map/ppermute | solution.py:513
  29.6 15.7 %copy-start = (bf16[2,2,256,1056]{3,2,1,0:T(8,128)(2,1)S(1)}, bf16[2,2,256,1056]{3,2,1,0:T(8,128)(2,1)}, u32[]{:S(2)}) copy-start(bf16[2,2,256,1056]{3,2,1,0:T(8,128)(2,1)} %constant.11.clone.refs_3_) | copy-start | bytes 6488068
  29.6 15.7 %copy-start.11 = (s32[4]{0:T(128)S(1)}, s32[4]{0:T(128)}, u32[]{:S(2)}) copy-start(s32[4]{0:T(128)} %refs_2_.2) | copy-start | bytes 52
  33.3 13.6 %copy-start.3 = (bf16[2,2,2,128,128]{4,3,2,1,0:T(8,128)(2,1)S(1)}, bf16[2,2,2,128,128]{4,3,2,1,0:T(8,128)(2,1)}, u32[]{:S(2)}) copy-start(bf16[2,2,2,128,128]{4,3,2,1,0:T(8,128)(2,1)} %constant.10.clone.refs_2_) | copy-start | bytes 786436
  38.0 8.9 %collective-permute-start.12 = (f32[8,5,32,128]{3,2,1,0:T(8,128)S(1)}, f32[8,5,32,128]{3,2,1,0:T(8,128)S(1)}, u32[]{:S(2)}, u32[]{:S(2)}) collective-permute-start(f32[8,5,32,128]{3,2,1,0:T(8,128)S(1)} %get-tuple-element.23.refs_0_), channel_id=1, source_target_pairs={{1,0},{0,1},{3,2},{2,3},{5,4},{4,5},{7,6},{6,7},{9,8},{8,9},{11,10... | collective-permute-start | bytes 1966088 | tf_op jit(solution)/shard_map/ppermute | solution.py:451
  40.6 4.6 %collective-permute-start.13 = (f32[4,16,128]{2,1,0:T(8,128)S(1)}, f32[4,16,128]{2,1,0:T(8,128)S(1)}, u32[]{:S(2)}, u32[]{:S(2)}) collective-permute-start(f32[4,16,128]{2,1,0:T(8,128)S(1)} %get-tuple-element.25), channel_id=1, source_target_pairs={{0,2},{3,1},{4,6},{7,5},{8,10},{11,9},{12,14},{15,13},{16,18},{19,... | collective-permute-start | bytes 98312 | tf_op jit(solution)/shard_map/ppermute | solution.py:563

commit v3 on v2

--- a/solution.py
+++ b/solution.py
@@ -23,6 +23,9 @@
 VMEM = pltpu.VMEM
 SMEM = pltpu.SMEM
 HBM = pltpu.HBM
+
+
+CORNER = [HALO - 2 * ((min(x + 1, HALO - x) + 1) // 2) for x in range(HALO)]
 
 
 def mode_basis(total, cores):
@@ -56,20 +59,6 @@
     return np.stack([high, low])
 
 
-def spectrum_table(lanes):
-    out = np.zeros((STEPS, lanes, NFREQ, 2, NM))
-    for t in range(STEPS):
-        phase = math.pi * t / NFREQ * np.arange(1, NFREQ + 1)
-        for m in range(NM):
-            scale = 1.0 if m == 0 else math.sqrt(0.5)
-            out[t, m, :, 0, m] = np.cos(phase) * scale
-            out[t, m, :, 1, m] = -np.sin(phase) * scale
-            if m > 0:
-                out[t, NM + m, :, 0, m] = -np.sin(phase) * scale
-                out[t, NM + m, :, 1, m] = -np.cos(phase) * scale
-    return out.reshape(STEPS, lanes, NFREQ * 2 * NM)
-
-
 def halves(x):
     high = x.astype(jnp.bfloat16)
     return high, (x - high.astype(jnp.float32)).astype(jnp.bfloat16)
@@ -115,12 +104,19 @@
         for i in range(count):
             out[i][:, f] = v[i]
     if last:
-        (e0_ref,) = refs[count:]
+        e0_ref, eu_ref = refs[count:]
+        at = 0
         for i, ref in enumerate(tuple(done) + tuple(out)):
             for side in range(e0_ref.shape[0]):
                 top = 1 - row if peers == 2 else 1 - side
                 rows = pl.ds(pl.multiple_of((cr - HALO) * top, 8), HALO)
                 e0_ref[side, i * step : (i + 1) * step] = ref[:, :, rows]
+            for j in range(step):
+                n = CORNER[i * step + j]
+                for side in range(e0_ref.shape[0]):
+                    top = 1 - row if peers == 2 else 1 - side
+                    eu_ref[side, :, at : at + n] = ref[j, :, pl.ds((cr - n) * top, n)]
+                at += n
 
 
 def prepare_kernel(
@@ -185,10 +181,10 @@
         self.pair_at = 2 * cx * self.even
         self.far_at = 2 * cx * self.odd
 
-    def halo(self, side):
+    def halo(self, side, n=HALO):
         if self.peers == 2:
-            return PAD + self.cr * (1 - self.row)
-        return self.own - HALO if side == 0 else self.own + self.cr
+            return PAD + self.row * (HALO - n) + self.cr * (1 - self.row)
+        return self.own - n if side == 0 else self.own + self.cr
 
     def clear(self, low, high, *works):
         zero = jnp.zeros((PAD, self.lanes), jnp.float32)
@@ -226,6 +222,13 @@
     def place_edge(self, edge_ref, work, at):
         for side in range(self.sides):
             self.place(edge_ref.at[side], work, at, pl.multiple_of(self.halo(side), 8))
+
+    def place_corner(self, corner_ref, work, at):
+        for side in range(self.sides):
+            row = 0
+            for x, n in enumerate(CORNER):
+                work[at + x, :, pl.ds(self.halo(side, n), n)] = corner_ref[side, :, row : row + n]
+                row += n
 
     def layer(self, coef_ref, src, store, x, base, count):
         fields = self.fields
@@ -291,7 +294,7 @@
         z.place(own_refs[i], w0_ref, cx + i * step, z.own)
         z.place(pair_refs[i], w0_ref, z.pair_at + i * step, z.own)
     z.place_edge(r0_ref, w0_ref, cx)
-    z.place_edge(rp_ref, w0_ref, z.pair_at)
+    z.place_corner(rp_ref, w0_ref, z.pair_at)
     p_ref[...] = jnp.zeros_like(p_ref)
     works = [w0_ref, w1_ref]
     for t in range(1, STEPS):
@@ -323,7 +326,7 @@
         z.place(own_refs[i], w0_ref, cx + i * step, z.own)
         z.place(far_refs[i], w0_ref, z.far_at + i * step, z.own)
     z.place_edge(r0_ref, w0_ref, cx)
-    z.place_edge(rc_ref, w0_ref, z.far_at)
+    z.place_corner(rc_ref, w0_ref, z.far_at)
     z.blank(cx - 2, cx - 2 + 2 * (1 - z.left), w1_ref)
     z.blank(2 * cx, 2 * cx + 2 * (1 - z.right), w1_ref)
     works = [w0_ref, w1_ref]
@@ -384,7 +387,7 @@
 def spectra_kernel(sizes, *refs):
     peers = sizes["row"]
     received = refs[:peers]
-    window_ref, table_ref, out_ref = refs[peers:]
+    window_ref, out_ref = refs[peers:]
     _, row, core, _ = position(sizes)
     share = peers // sizes["ta"]
     blocks = []
@@ -395,18 +398,25 @@
             value = jnp.where(hop == k, received[k][...], value)
         blocks.append(value)
     x = blocks[0] if share == 1 else jnp.concatenate(blocks, axis=1)
-    n = x.shape[1]
-    dot = functools.partial(jnp.dot, preferred_element_type=jnp.float32)
-    total = None
-    for t in range(0, STEPS, 2):
-        pair = jnp.concatenate(
-            [x[i] * (window_ref[i].astype(jnp.float32) * 0.125) for i in (t, t + 1)], axis=1
-        )
-        high, low = halves(pair)
-        both = dot(jnp.concatenate([high, low], axis=0), table_ref[0, t // 2])
-        part = both[:n] + both[n:] + dot(high, table_ref[1, t // 2])
-        total = part if total is None else total + part
-    out_ref[0] = total
+    lane = lax.broadcasted_iota(jnp.int32, (1, x.shape[2]), 1)
+    scale = jnp.where(lane == 0, 1.0, math.sqrt(0.5))
+    keep = jnp.where(lane == 0, 0.0, math.sqrt(0.5))
+    cosine, sine = [], []
+    for t in range(STEPS):
+        value = x[t] * (window_ref[t].astype(jnp.float32) * 0.125)
+        cosine.append(value * scale)
+        sine.append(pltpu.roll(value, x.shape[2] - NM, 1) * keep)
+    for k in range(NFREQ):
+        real = imag = None
+        for t in range(STEPS):
+            phase = math.pi * t * (k + 1) / NFREQ
+            c, s = math.cos(phase), math.sin(phase)
+            re = cosine[t] if t == 0 else c * cosine[t] - s * sine[t]
+            im = -sine[t] if t == 0 else -s * cosine[t] - c * sine[t]
+            real = re if real is None else real + re
+            imag = im if imag is None else imag + im
+        out_ref[0, :, 2 * k * NM : (2 * k + 1) * NM] = real[:, :NM]
+        out_ref[0, :, (2 * k + 1) * NM : (2 * k + 2) * NM] = imag[:, :NM]
 
 
 def spec(space, n):
@@ -476,11 +486,11 @@
             name="forward_early",
         )(part, ahead, *sources)
     )
-    *rest, e0 = pl.pallas_call(
+    *rest, e0, eu = pl.pallas_call(
         functools.partial(forward_kernel, sizes, early, PIECES - early, True),
-        out_shape=(tile,) * (PIECES - early) + (edge,),
+        out_shape=(tile,) * (PIECES - early) + (edge, shape(sides, fields, sum(CORNER), ct)),
         in_specs=spec(VMEM, cores + 1 + early),
-        out_specs=tuple(spec(VMEM, PIECES - early + 1)),
+        out_specs=tuple(spec(VMEM, PIECES - early + 2)),
         compiler_params=limit(8),
         cost_estimate=work_for(10**6),
         name="forward_late",
@@ -491,25 +501,29 @@
     onward = [(i, i + 2 if i % 2 == 0 else i - 2) for i in range(nx)]
     onward = [(a, b) for a, b in onward if 0 <= b < nx]
 
-    r0 = []
-    for side in range(sides):
-        if peers == 2:
-            turn = [(0, 1), (1, 0)]
-        else:
-            turn = [(r, r + 1) for r in range(peers - 1)]
-            if side:
-                turn = [(b, a) for a, b in turn]
-        hops = [
-            (r * cores + (g + r // share) % cores, q * cores + (g + q // share) % cores)
-            for r, q in turn
-            for g in range(cores)
-        ]
-        r0.append(lax.ppermute(e0[side : side + 1], ("row", "ta"), hops))
-    r0 = r0[0] if sides == 1 else jnp.concatenate(r0, axis=0)
+    def radial(x):
+        got = []
+        for side in range(sides):
+            if peers == 2:
+                turn = [(0, 1), (1, 0)]
+            else:
+                turn = [(r, r + 1) for r in range(peers - 1)]
+                if side:
+                    turn = [(b, a) for a, b in turn]
+            hops = [
+                (r * cores + (g + r // share) % cores, q * cores + (g + q // share) % cores)
+                for r, q in turn
+                for g in range(cores)
+            ]
+            got.append(lax.ppermute(x[side : side + 1], ("row", "ta"), hops))
+        return got[0] if sides == 1 else jnp.concatenate(got, axis=0)
+
+    r0 = radial(e0)
+    ru = radial(eu)
     pair, far = [], []
     for x in own:
         pair.append(lax.ppermute(x, "gx", swap))
-    rp = lax.ppermute(r0, "gx", swap)
+    rp = lax.ppermute(ru, "gx", swap)
     rc = lax.ppermute(rp, "gx", onward)
     for x in pair:
         far.append(lax.ppermute(x, "gx", onward))
@@ -575,12 +589,12 @@
     spectra = pl.pallas_call(
         functools.partial(spectra_kernel, sizes),
         out_shape=shape(1, share * CAP, NFREQ * 2 * NM),
-        in_specs=spec(VMEM, peers) + spec(SMEM, 1) + spec(VMEM, 1),
+        in_specs=spec(VMEM, peers) + spec(SMEM, 1),
         out_specs=pl.BlockSpec(memory_space=VMEM),
         compiler_params=limit(8),
         cost_estimate=work_for(10**6),
         name="spectra",
-    )(*received, window_table, split_const(spectrum_table(ct).reshape(STEPS // 2, 2 * ct, -1)))
+    )(*received, window_table)
     return (advanced, spectra)
 
 

time: 48.6 us -> 49.2 us (1.012)
  waiting for transfers between devices: 6.08 us -> 7.6 us
  starting transfers between devices: 25.6 us -> 24.9 us
    ppermute x2 -> x3, waiting for transfers between devices: 2.39 us -> 0.01 us  [the longest x2 0.01 us: radial(): got.append(lax.ppermute(x[side:side + 1], ('row', 'ta'), hops))]
    ppermute x4, waiting for transfers between devices: 0.32 us -> 2.61 us  [local(): pair.append(lax.ppermute(x, 'gx', swap))]
    ppermute x4, starting transfers between devices: 12.4 us -> 10.2 us  [local(): far.append(lax.ppermute(x, 'gx', onward))]
    ppermute x1, waiting for transfers between devices: 0.01 us -> 1.61 us  [local(): rc = lax.ppermute(rp, 'gx', onward)]
    ppermute x2 -> x3, starting transfers between devices: 2.41 us -> 3.61 us  [the longest x2 2.37 us: radial(): got.append(lax.ppermute(x[side:side + 1], ('row', 'ta'), hops))]
    ppermute x4, starting transfers between devices: 2.93 us -> 3.73 us  [local(): pair.append(lax.ppermute(x, 'gx', swap))]
    unnamed x24 -> x22, local copies, waits for them, and re-layouts: 2.08 us -> 2.09 us
  transfers between devices with their start and end apart: 14 -> 15, of which waited for: 4 -> 4; matrix products, arithmetic and copies ran while one was open for 0% -> 0% of each run, Pallas kernels for 15% -> 14%
where the time goes in v3:
time: 49.2 us; the launch traced here: 48.9 us
  starting transfers between devices  24.9 us (51%)
  Pallas kernels  13.4 us (27%)
  waiting for transfers between devices  7.6 us (15%)
  local copies, waits for them, and re-layouts  2.09 us (4%)
  between operations  0.9 us (2%)
    ppermute x4, starting transfers between devices, local(): far.append(lax.ppermute(x, 'gx', onward))  10.2 us
    pallas_call x1, Pallas kernels, local(): pl.pallas_call(functools.partial(far_kernel, sizes), out_shape=(shape(cx,...  4.61 us
    ppermute x4, starting transfers between devices, local(): pair.append(lax.ppermute(x, 'gx', swap))  3.73 us
    pallas_call x1, Pallas kernels, local(): pl.pallas_call(functools.partial(near_kernel, sizes), out_shape=(shape(ST...  3.61 us
    ppermute x1, waiting for transfers between devices, local(): received.append(lax.ppermute(cycles[k], ('row', 'ta'), pairs))  3.36 us
    ppermute x1, starting transfers between devices, local(): rc = lax.ppermute(rp, 'gx', onward)  3.13 us
    ppermute x2, starting transfers between devices, others(): lax.ppermute(x, 'ta', [((c + k) % cores, c) for c in range(cores)])  2.94 us
    ppermute x4, waiting for transfers between devices, local(): pair.append(lax.ppermute(x, 'gx', swap))  2.61 us
  transfers between devices with their start and end apart: 15, of which 4 were waited for; matrix products, arithmetic and copies ran while one was open for 0% of the time, Pallas kernels for 14%

profile of v3, /device:TPU:9, one launch (start us, length us, event | category | flops | bytes accessed | tf_op | source)
XLA Modules:
  0.0 48.9 jit_solution(12708699075004282397)
XLA Ops:
  0.6 0.7 %collective-permute-start = (f32[5,8,32,128]{3,2,1,0:T(8,128)}, f32[5,8,32,128]{3,2,1,0:T(8,128)S(1)}, u32[]{:S(2)}, u32[]{:S(2)}) collective-permute-start(f32[5,8,32,128]{3,2,1,0:T(8,128)} %own_ref.1), channel_id=1, source_target_pairs={{1,0},{0,1},{3,2},{2,3},{5,4},{4,5},{7,6},{6,7},{9,8},{8,9},{11,10... | collective-permute-start | bytes 1966088 | tf_op jit(solution)/shard_map/ppermute | solution.py:461
  1.4 0.9 %copy-done = bf16[2,2,2,128,128]{4,3,2,1,0:T(8,128)(2,1)S(1)} copy-done((bf16[2,2,2,128,128]{4,3,2,1,0:T(8,128)(2,1)S(1)}, bf16[2,2,2,128,128]{4,3,2,1,0:T(8,128)(2,1)}, u32[]{:S(2)}) %copy-start) | copy-done | bytes 262168
  2.3 1.1 %copy-done.1 = f32[5,8,32,128]{3,2,1,0:T(8,128)S(1)} copy-done((f32[5,8,32,128]{3,2,1,0:T(8,128)S(1)}, f32[5,8,32,128]{3,2,1,0:T(8,128)}, u32[]{:S(2)}) %copy-start.1) | copy-done | bytes 655384
  3.4 0.4 stage.1.part_ref
  3.8 0.0 collective-permute-done.refs_0_
  3.8 0.3 forward_early.1
  4.1 0.0 copy-start.3
  4.2 0.0 copy-start.4
  4.2 0.0 copy-start.7
  4.2 0.0 copy-start.8
  4.2 0.0 copy-start.9
  4.2 0.0 copy-start.10
  4.2 0.0 copy-start.5
  4.2 0.3 forward_late.1
  4.6 1.2 %collective-permute-start.10 = (f32[1,5,40,128]{3,2,1,0:T(8,128)S(1)}, f32[1,5,40,128]{3,2,1,0:T(8,128)S(1)}, u32[]{:S(2)}, u32[]{:S(2)}) collective-permute-start(f32[1,5,40,128]{3,2,1,0:T(8,128)S(1)} %get-tuple-element.22), channel_id=1, source_target_pairs={{0,3},{1,2},{3,0},{2,1},{4,7},{5,6},{7,4},{6,5},{8,11},{9,10},{11,... | collective-permute-start | bytes 307208 | tf_op jit(solution)/shard_map/ppermute | solution.py:518
  5.7 1.2 %collective-permute-start.5 = (f32[2,5,32,128]{3,2,1,0:T(8,128)S(1)}, f32[2,5,32,128]{3,2,1,0:T(8,128)S(1)}, u32[]{:S(2)}, u32[]{:S(2)}) collective-permute-start(f32[2,5,32,128]{3,2,1,0:T(8,128)S(1)} %get-tuple-element.19.refs_2_), channel_id=1, source_target_pairs={{0,4},{4,0},{8,12},{12,8},{16,20},{20,16},{24,28},{28,24},{1,5},{5... | collective-permute-start | bytes 491528 | tf_op jit(solution)/shard_map/ppermute | solution.py:525
  7.0 0.2 collective-permute-start.7
  7.2 1.2 %collective-permute-start.9 = (f32[1,8,5,8,128]{4,3,2,1,0:T(8,128)S(1)}, f32[1,8,5,8,128]{4,3,2,1,0:T(8,128)S(1)}, u32[]{:S(2)}, u32[]{:S(2)}) collective-permute-start(f32[1,8,5,8,128]{4,3,2,1,0:T(8,128)S(1)} %get-tuple-element.21), channel_id=1, source_target_pairs={{0,3},{1,2},{3,0},{2,1},{4,7},{5,6},{7,4},{6,5},{8,11},{9,10},{11,... | collective-permute-start | bytes 491528 | tf_op jit(solution)/shard_map/ppermute | solution.py:518
  8.4 1.2 %collective-permute-start.1 = (f32[2,5,32,128]{3,2,1,0:T(8,128)S(1)}, f32[2,5,32,128]{3,2,1,0:T(8,128)S(1)}, u32[]{:S(2)}, u32[]{:S(2)}) collective-permute-start(f32[2,5,32,128]{3,2,1,0:T(8,128)S(1)} %get-tuple-element.17.refs_1_.refs_0_), channel_id=1, source_target_pairs={{0,4},{4,0},{8,12},{12,8},{16,20},{20,16},{24,28},{28,24},{1,5},{5... | collective-permute-start | bytes 491528 | tf_op jit(solution)/shard_map/ppermute | solution.py:525
  9.6 0.0 collective-permute-done.10
  9.6 1.0 %collective-permute-start.3 = (f32[2,5,32,128]{3,2,1,0:T(8,128)S(1)}, f32[2,5,32,128]{3,2,1,0:T(8,128)S(1)}, u32[]{:S(2)}, u32[]{:S(2)}) collective-permute-start(f32[2,5,32,128]{3,2,1,0:T(8,128)S(1)} %get-tuple-element.18.refs_2_.refs_1_), channel_id=1, source_target_pairs={{0,4},{4,0},{8,12},{12,8},{16,20},{20,16},{24,28},{28,24},{1,5},{5... | collective-permute-start | bytes 491528 | tf_op jit(solution)/shard_map/ppermute | solution.py:525
  10.7 0.3 collective-permute-done.5.refs_6_
  11.0 1.2 %collective-permute-start.11 = (f32[1,5,40,128]{3,2,1,0:T(8,128)S(1)}, f32[1,5,40,128]{3,2,1,0:T(8,128)S(1)}, u32[]{:S(2)}, u32[]{:S(2)}) collective-permute-start(f32[1,5,40,128]{3,2,1,0:T(8,128)S(1)} %collective-permute-done.10), channel_id=1, source_target_pairs={{0,4},{4,0},{8,12},{12,8},{16,20},{20,16},{24,28},{28,24},{1,5},{5... | collective-permute-start | bytes 307208 | tf_op jit(solution)/shard_map/ppermute | solution.py:526
  12.2 2.3 %collective-permute-done.7.refs_7_ = f32[2,5,32,128]{3,2,1,0:T(8,128)S(1)} collective-permute-done((f32[2,5,32,128]{3,2,1,0:T(8,128)S(1)}, f32[2,5,32,128]{3,2,1,0:T(8,128)S(1)}, u32[]{:S(2)}, u32[]{:S(2)}) %collective-permute-start.7) | collective-permute-done | bytes 163872 | tf_op jit(solution)/shard_map/ppermute | solution.py:525
  14.5 3.2 %collective-permute-start.6 = (f32[2,5,32,128]{3,2,1,0:T(8,128)S(1)}, f32[2,5,32,128]{3,2,1,0:T(8,128)S(1)}, u32[]{:S(2)}, u32[]{:S(2)}) collective-permute-start(f32[2,5,32,128]{3,2,1,0:T(8,128)S(1)} %collective-permute-done.5.refs_6_), channel_id=1, source_target_pairs={{0,8},{8,16},{12,4},{16,24},{20,12},{28,20},{1,9},{9,17},{13,5},{1... | collective-permute-start | bytes 491528 | tf_op jit(solution)/shard_map/ppermute | solution.py:529
  17.7 0.0 collective-permute-done.9.refs_8_
  17.7 3.2 %collective-permute-start.8 = (f32[2,5,32,128]{3,2,1,0:T(8,128)S(1)}, f32[2,5,32,128]{3,2,1,0:T(8,128)S(1)}, u32[]{:S(2)}, u32[]{:S(2)}) collective-permute-start(f32[2,5,32,128]{3,2,1,0:T(8,128)S(1)} %collective-permute-done.7.refs_7_), channel_id=1, source_target_pairs={{0,8},{8,16},{12,4},{16,24},{20,12},{28,20},{1,9},{9,17},{13,5},{1... | collective-permute-start | bytes 491528 | tf_op jit(solution)/shard_map/ppermute | solution.py:529
  20.9 0.0 collective-permute-done.1.refs_4_
  20.9 1.9 %collective-permute-start.2 = (f32[2,5,32,128]{3,2,1,0:T(8,128)S(1)}, f32[2,5,32,128]{3,2,1,0:T(8,128)S(1)}, u32[]{:S(2)}, u32[]{:S(2)}) collective-permute-start(f32[2,5,32,128]{3,2,1,0:T(8,128)S(1)} %collective-permute-done.1.refs_4_), channel_id=1, source_target_pairs={{0,8},{8,16},{12,4},{16,24},{20,12},{28,20},{1,9},{9,17},{13,5},{1... | collective-permute-start | bytes 491528 | tf_op jit(solution)/shard_map/ppermute | solution.py:529
  22.9 0.0 collective-permute-done.3.refs_5_
  22.9 1.9 %collective-permute-start.4 = (f32[2,5,32,128]{3,2,1,0:T(8,128)S(1)}, f32[2,5,32,128]{3,2,1,0:T(8,128)S(1)}, u32[]{:S(2)}, u32[]{:S(2)}) collective-permute-start(f32[2,5,32,128]{3,2,1,0:T(8,128)S(1)} %collective-permute-done.3.refs_5_), channel_id=1, source_target_pairs={{0,8},{8,16},{12,4},{16,24},{20,12},{28,20},{1,9},{9,17},{13,5},{1... | collective-permute-start | bytes 491528 | tf_op jit(solution)/shard_map/ppermute | solution.py:529
  24.8 0.0 collective-permute-done.11.refs_9_
  24.8 3.1 %collective-permute-start.12 = (f32[1,5,40,128]{3,2,1,0:T(8,128)S(1)}, f32[1,5,40,128]{3,2,1,0:T(8,128)S(1)}, u32[]{:S(2)}, u32[]{:S(2)}) collective-permute-start(f32[1,5,40,128]{3,2,1,0:T(8,128)S(1)} %collective-permute-done.11.refs_9_), channel_id=1, source_target_pairs={{0,8},{8,16},{12,4},{16,24},{20,12},{28,20},{1,9},{9,17},{13,5},{1... | collective-permute-start | bytes 307208 | tf_op jit(solution)/shard_map/ppermute | solution.py:527
  28.0 1.3 %prepare.1 = (f32[5,11,8,128]{3,2,1,0:T(8,128)S(1)}, bf16[32,256]{1,0:T(8,128)(2,1)S(1)}) custom-call(f32[5]{0:T(128)S(1)} %copy-done.7, f32[5]{0:T(128)S(1)} %copy-done.8, f32[5,5]{1,0:T(8,128)S(1)} %copy-done.4, s32[32]{0:T(128)S(1)} %copy-done.9, s32[32]{0:T(128)S(1)} %bitcast.1, f32[2,8,128]{2,1,0:T(8,128)S(1)} %copy-done.3), custom_call_target="tpu_custom_call" | custom-call | flops 1000000 | bytes 1000000 | tf_op jit(solution)/shard_map/prepare/pallas_call | solution.py:532
  29.4 3.6 %near.1 = (f32[3,4,5,40,128]{4,3,2,1,0:T(8,128)S(1)}, f32[3,256,128]{2,1,0:T(8,128)S(1)}) custom-call(f32[5,11,8,128]{3,2,1,0:T(8,128)S(1)} %get-tuple-element.15.coef_ref, f32[5]{0:T(128)S(1)} %copy-done.5, f32[2,5,32,128]{3,2,1,0:T(8,128)S(1)} %get-tuple-element.17.refs_1_.refs_0_, f32[2,5,32,128]{3,2,1,0:T(8,128)S(1)} %get-tuple-element.18.refs_2_.refs_1_, ...), custom_call_target="tpu_custom_call" | custom-call | flops 10000000 | bytes 1000000 | tf_op jit(solution)/shard_map/near/pallas_call | solution.py:551
  33.0 1.6 %collective-permute-done.12.refs_9_ = f32[1,5,40,128]{3,2,1,0:T(8,128)S(1)} collective-permute-done((f32[1,5,40,128]{3,2,1,0:T(8,128)S(1)}, f32[1,5,40,128]{3,2,1,0:T(8,128)S(1)}, u32[]{:S(2)}, u32[]{:S(2)}) %collective-permute-start.12) | collective-permute-done | bytes 102432 | tf_op jit(solution)/shard_map/ppermute | solution.py:527
  34.6 0.0 collective-permute-done.6.refs_6_
  34.6 0.0 collective-permute-done.8.refs_7_
  34.6 0.0 collective-permute-done.4.refs_5_
  34.6 0.0 copy-start.6
  34.6 0.0 copy-start.2
  34.6 4.6 %rest.1 = (f32[8,5,32,128]{3,2,1,0:T(8,128)S(1)}, f32[4,16,128]{2,1,0:T(8,128)S(1)}, f32[4,16,128]{2,1,0:T(8,128)S(1)}) custom-call(f32[5,11,8,128]{3,2,1,0:T(8,128)S(1)} %get-tuple-element.15.coef_ref, f32[5]{0:T(128)S(1)} %copy-done.5, bf16[32,256]{1,0:T(8,128)(2,1)S(1)} %get-tuple-element.16.place_ref, ...), custom_call_target="tpu_custom_call" | custom-call | flops 10000000 | bytes 1000000 | tf_op jit(solution)/shard_map/rest/pallas_call | solution.py:561
  39.3 2.2 %collective-permute-start.13 = (f32[8,5,32,128]{3,2,1,0:T(8,128)S(1)}, f32[8,5,32,128]{3,2,1,0:T(8,128)S(1)}, u32[]{:S(2)}, u32[]{:S(2)}) collective-permute-start(f32[8,5,32,128]{3,2,1,0:T(8,128)S(1)} %get-tuple-element.25.refs_0_), channel_id=1, source_target_pairs={{1,0},{0,1},{3,2},{2,3},{5,4},{4,5},{7,6},{6,7},{9,8},{8,9},{11,10... | collective-permute-start | bytes 1966088 | tf_op jit(solution)/shard_map/ppermute | solution.py:461
  41.5 1.3 %collective-permute-start.14 = (f32[4,16,128]{2,1,0:T(8,128)S(1)}, f32[4,16,128]{2,1,0:T(8,128)S(1)}, u32[]{:S(2)}, u32[]{:S(2)}) collective-permute-start(f32[4,16,128]{2,1,0:T(8,128)S(1)} %get-tuple-element.27), channel_id=1, source_target_pairs={{0,2},{3,1},{4,6},{7,5},{8,10},{11,9},{12,14},{15,13},{16,18},{19,... | collective-permute-start | bytes 98312 | tf_op jit(solution)/shard_map/ppermute | solution.py:577
  42.8 3.4 %collective-permute-done.14.refs_1_ = f32[4,16,128]{2,1,0:T(8,128)S(1)} collective-permute-done((f32[4,16,128]{2,1,0:T(8,128)S(1)}, f32[4,16,128]{2,1,0:T(8,128)S(1)}, u32[]{:S(2)}, u32[]{:S(2)}) %collective-permute-start.14) | collective-permute-done | bytes 32800 | tf_op jit(solution)/shard_map/ppermute | solution.py:577
  46.1 1.4 %spectra.1 = f32[1,16,1056]{2,1,0:T(8,128)} custom-call(f32[4,16,128]{2,1,0:T(8,128)S(1)} %get-tuple-element.26.refs_0_, f32[4,16,128]{2,1,0:T(8,128)S(1)} %collective-permute-done.14.refs_1_, s32[4]{0:T(128)S(1)} %copy-done.6), custom_call_target="tpu_custom_call" | custom-call | flops 1000000 | bytes 1000000 | tf_op jit(solution)/shard_map/spectra/pallas_call | solution.py:589
  47.5 0.0 collective-permute-done.13.refs_1_
  47.5 1.4 %inverse.1 = f32[5,8,32,128]{3,2,1,0:T(8,128)} custom-call(f32[8,5,32,128]{3,2,1,0:T(8,128)S(1)} %get-tuple-element.25.refs_0_, f32[8,5,32,128]{3,2,1,0:T(8,128)S(1)} %collective-permute-done.13.refs_1_, bf16[2,2,2,128,128]{4,3,2,1,0:T(8,128)(2,1)S(1)} %copy-done.2), custom_call_target="tpu_custom_call" | custom-call | flops 1000000 | bytes 1000000 | tf_op jit(solution)/shard_map/inverse/pallas_call | solution.py:579
  (12 shorter events, 0.0 us)
Async XLA Ops:
  0.6 3.2 %collective-permute-start = (f32[5,8,32,128]{3,2,1,0:T(8,128)}, f32[5,8,32,128]{3,2,1,0:T(8,128)S(1)}, u32[]{:S(2)}, u32[]{:S(2)}) collective-permute-start(f32[5,8,32,128]{3,2,1,0:T(8,128)} %own_ref.1), channel_id=1, source_target_pairs={{1,0},{0,1},{3,2},{2,3},{5,4},{4,5},{7,6},{6,7},{9,8},{8,9},{11,10... | collective-permute-start | bytes 1966088 | tf_op jit(solution)/shard_map/ppermute | solution.py:461
  1.4 0.9 %copy-start = (bf16[2,2,2,128,128]{4,3,2,1,0:T(8,128)(2,1)S(1)}, bf16[2,2,2,128,128]{4,3,2,1,0:T(8,128)(2,1)}, u32[]{:S(2)}) copy-start(bf16[2,2,2,128,128]{4,3,2,1,0:T(8,128)(2,1)} %constant.6.clone.table_ref) | copy-start | bytes 786436
  2.3 1.1 %copy-start.1 = (f32[5,8,32,128]{3,2,1,0:T(8,128)S(1)}, f32[5,8,32,128]{3,2,1,0:T(8,128)}, u32[]{:S(2)}) copy-start(f32[5,8,32,128]{3,2,1,0:T(8,128)} %own_ref.1) | copy-start | bytes 1966084
  4.1 23.8 %copy-start.3 = (f32[2,8,128]{2,1,0:T(8,128)S(1)}, f32[2,8,128]{2,1,0:T(8,128)}, u32[]{:S(2)}) copy-start(f32[2,8,128]{2,1,0:T(8,128)} %constant.7.clone.eigen_ref) | copy-start | bytes 24580
  4.2 23.8 %copy-start.4 = (f32[5,5]{1,0:T(8,128)S(1)}, f32[5,5]{1,0:T(8,128)}, u32[]{:S(2)}) copy-start(f32[5,5]{1,0:T(8,128)} %mix_ref.1) | copy-start | bytes 304
  4.2 23.8 %copy-start.7 = (f32[5]{0:T(128)S(1)}, f32[5]{0:T(128)}, u32[]{:S(2)}) copy-start(f32[5]{0:T(128)} %rate_ref.1) | copy-start | bytes 64
  4.2 23.8 %copy-start.8 = (f32[5]{0:T(128)S(1)}, f32[5]{0:T(128)}, u32[]{:S(2)}) copy-start(f32[5]{0:T(128)} %speed_ref.1) | copy-start | bytes 64
  4.2 23.8 %copy-start.9 = (s32[32]{0:T(128)S(1)}, s32[32]{0:T(128)}, u32[]{:S(2)}) copy-start(s32[32]{0:T(128)} %cell_ref.1) | copy-start | bytes 388
  4.2 23.8 %copy-start.10 = (s32[32,1]{0,1:T(1,128)S(1)}, s32[32,1]{0,1:T(1,128)}, u32[]{:S(2)}) copy-start(s32[32,1]{0,1:T(1,128)} %param.17) | copy-start | bytes 388
  4.2 25.1 %copy-start.5 = (f32[5]{0:T(128)S(1)}, f32[5]{0:T(128)}, u32[]{:S(2)}) copy-start(f32[5]{0:T(128)} %weight_ref.3) | copy-start | bytes 64
  4.6 5.1 %collective-permute-start.10 = (f32[1,5,40,128]{3,2,1,0:T(8,128)S(1)}, f32[1,5,40,128]{3,2,1,0:T(8,128)S(1)}, u32[]{:S(2)}, u32[]{:S(2)}) collective-permute-start(f32[1,5,40,128]{3,2,1,0:T(8,128)S(1)} %get-tuple-element.22), channel_id=1, source_target_pairs={{0,3},{1,2},{3,0},{2,1},{4,7},{5,6},{7,4},{6,5},{8,11},{9,10},{11,... | collective-permute-start | bytes 307208 | tf_op jit(solution)/shard_map/ppermute | solution.py:518
  5.7 5.3 %collective-permute-start.5 = (f32[2,5,32,128]{3,2,1,0:T(8,128)S(1)}, f32[2,5,32,128]{3,2,1,0:T(8,128)S(1)}, u32[]{:S(2)}, u32[]{:S(2)}) collective-permute-start(f32[2,5,32,128]{3,2,1,0:T(8,128)S(1)} %get-tuple-element.19.refs_2_), channel_id=1, source_target_pairs={{0,4},{4,0},{8,12},{12,8},{16,20},{20,16},{24,28},{28,24},{1,5},{5... | collective-permute-start | bytes 491528 | tf_op jit(solution)/shard_map/ppermute | solution.py:525
  7.0 7.5 %collective-permute-start.7 = (f32[2,5,32,128]{3,2,1,0:T(8,128)S(1)}, f32[2,5,32,128]{3,2,1,0:T(8,128)S(1)}, u32[]{:S(2)}, u32[]{:S(2)}) collective-permute-start(f32[2,5,32,128]{3,2,1,0:T(8,128)S(1)} %get-tuple-element.20.refs_3_), channel_id=1, source_target_pairs={{0,4},{4,0},{8,12},{12,8},{16,20},{20,16},{24,28},{28,24},{1,5},{5... | collective-permute-start | bytes 491528 | tf_op jit(solution)/shard_map/ppermute | solution.py:525
  7.2 10.5 %collective-permute-start.9 = (f32[1,8,5,8,128]{4,3,2,1,0:T(8,128)S(1)}, f32[1,8,5,8,128]{4,3,2,1,0:T(8,128)S(1)}, u32[]{:S(2)}, u32[]{:S(2)}) collective-permute-start(f32[1,8,5,8,128]{4,3,2,1,0:T(8,128)S(1)} %get-tuple-element.21), channel_id=1, source_target_pairs={{0,3},{1,2},{3,0},{2,1},{4,7},{5,6},{7,4},{6,5},{8,11},{9,10},{11,... | collective-permute-start | bytes 491528 | tf_op jit(solution)/shard_map/ppermute | solution.py:518
  8.4 12.5 %collective-permute-start.1 = (f32[2,5,32,128]{3,2,1,0:T(8,128)S(1)}, f32[2,5,32,128]{3,2,1,0:T(8,128)S(1)}, u32[]{:S(2)}, u32[]{:S(2)}) collective-permute-start(f32[2,5,32,128]{3,2,1,0:T(8,128)S(1)} %get-tuple-element.17.refs_1_.refs_0_), channel_id=1, source_target_pairs={{0,4},{4,0},{8,12},{12,8},{16,20},{20,16},{24,28},{28,24},{1,5},{5... | collective-permute-start | bytes 491528 | tf_op jit(solution)/shard_map/ppermute | solution.py:525
  9.6 13.2 %collective-permute-start.3 = (f32[2,5,32,128]{3,2,1,0:T(8,128)S(1)}, f32[2,5,32,128]{3,2,1,0:T(8,128)S(1)}, u32[]{:S(2)}, u32[]{:S(2)}) collective-permute-start(f32[2,5,32,128]{3,2,1,0:T(8,128)S(1)} %get-tuple-element.18.refs_2_.refs_1_), channel_id=1, source_target_pairs={{0,4},{4,0},{8,12},{12,8},{16,20},{20,16},{24,28},{28,24},{1,5},{5... | collective-permute-start | bytes 491528 | tf_op jit(solution)/shard_map/ppermute | solution.py:525
  11.0 13.8 %collective-permute-start.11 = (f32[1,5,40,128]{3,2,1,0:T(8,128)S(1)}, f32[1,5,40,128]{3,2,1,0:T(8,128)S(1)}, u32[]{:S(2)}, u32[]{:S(2)}) collective-permute-start(f32[1,5,40,128]{3,2,1,0:T(8,128)S(1)} %collective-permute-done.10), channel_id=1, source_target_pairs={{0,4},{4,0},{8,12},{12,8},{16,20},{20,16},{24,28},{28,24},{1,5},{5... | collective-permute-start | bytes 307208 | tf_op jit(solution)/shard_map/ppermute | solution.py:526
  14.5 20.1 %collective-permute-start.6 = (f32[2,5,32,128]{3,2,1,0:T(8,128)S(1)}, f32[2,5,32,128]{3,2,1,0:T(8,128)S(1)}, u32[]{:S(2)}, u32[]{:S(2)}) collective-permute-start(f32[2,5,32,128]{3,2,1,0:T(8,128)S(1)} %collective-permute-done.5.refs_6_), channel_id=1, source_target_pairs={{0,8},{8,16},{12,4},{16,24},{20,12},{28,20},{1,9},{9,17},{13,5},{1... | collective-permute-start | bytes 491528 | tf_op jit(solution)/shard_map/ppermute | solution.py:529
  17.7 16.9 %collective-permute-start.8 = (f32[2,5,32,128]{3,2,1,0:T(8,128)S(1)}, f32[2,5,32,128]{3,2,1,0:T(8,128)S(1)}, u32[]{:S(2)}, u32[]{:S(2)}) collective-permute-start(f32[2,5,32,128]{3,2,1,0:T(8,128)S(1)} %collective-permute-done.7.refs_7_), channel_id=1, source_target_pairs={{0,8},{8,16},{12,4},{16,24},{20,12},{28,20},{1,9},{9,17},{13,5},{1... | collective-permute-start | bytes 491528 | tf_op jit(solution)/shard_map/ppermute | solution.py:529
  20.9 13.7 %collective-permute-start.2 = (f32[2,5,32,128]{3,2,1,0:T(8,128)S(1)}, f32[2,5,32,128]{3,2,1,0:T(8,128)S(1)}, u32[]{:S(2)}, u32[]{:S(2)}) collective-permute-start(f32[2,5,32,128]{3,2,1,0:T(8,128)S(1)} %collective-permute-done.1.refs_4_), channel_id=1, source_target_pairs={{0,8},{8,16},{12,4},{16,24},{20,12},{28,20},{1,9},{9,17},{13,5},{1... | collective-permute-start | bytes 491528 | tf_op jit(solution)/shard_map/ppermute | solution.py:529
  22.9 11.7 %collective-permute-start.4 = (f32[2,5,32,128]{3,2,1,0:T(8,128)S(1)}, f32[2,5,32,128]{3,2,1,0:T(8,128)S(1)}, u32[]{:S(2)}, u32[]{:S(2)}) collective-permute-start(f32[2,5,32,128]{3,2,1,0:T(8,128)S(1)} %collective-permute-done.3.refs_5_), channel_id=1, source_target_pairs={{0,8},{8,16},{12,4},{16,24},{20,12},{28,20},{1,9},{9,17},{13,5},{1... | collective-permute-start | bytes 491528 | tf_op jit(solution)/shard_map/ppermute | solution.py:529
  24.8 9.8 %collective-permute-start.12 = (f32[1,5,40,128]{3,2,1,0:T(8,128)S(1)}, f32[1,5,40,128]{3,2,1,0:T(8,128)S(1)}, u32[]{:S(2)}, u32[]{:S(2)}) collective-permute-start(f32[1,5,40,128]{3,2,1,0:T(8,128)S(1)} %collective-permute-done.11.refs_9_), channel_id=1, source_target_pairs={{0,8},{8,16},{12,4},{16,24},{20,12},{28,20},{1,9},{9,17},{13,5},{1... | collective-permute-start | bytes 307208 | tf_op jit(solution)/shard_map/ppermute | solution.py:527
  34.6 11.5 %copy-start.6 = (s32[4]{0:T(128)S(1)}, s32[4]{0:T(128)}, u32[]{:S(2)}) copy-start(s32[4]{0:T(128)} %refs_2_.2) | copy-start | bytes 52
  34.6 12.9 %copy-start.2 = (bf16[2,2,2,128,128]{4,3,2,1,0:T(8,128)(2,1)S(1)}, bf16[2,2,2,128,128]{4,3,2,1,0:T(8,128)(2,1)}, u32[]{:S(2)}) copy-start(bf16[2,2,2,128,128]{4,3,2,1,0:T(8,128)(2,1)} %constant.8.clone.refs_2_) | copy-start | bytes 786436
  39.3 8.3 %collective-permute-start.13 = (f32[8,5,32,128]{3,2,1,0:T(8,128)S(1)}, f32[8,5,32,128]{3,2,1,0:T(8,128)S(1)}, u32[]{:S(2)}, u32[]{:S(2)}) collective-permute-start(f32[8,5,32,128]{3,2,1,0:T(8,128)S(1)} %get-tuple-element.25.refs_0_), channel_id=1, source_target_pairs={{1,0},{0,1},{3,2},{2,3},{5,4},{4,5},{7,6},{6,7},{9,8},{8,9},{11,10... | collective-permute-start | bytes 1966088 | tf_op jit(solution)/shard_map/ppermute | solution.py:461
  41.5 4.6 %collective-permute-start.14 = (f32[4,16,128]{2,1,0:T(8,128)S(1)}, f32[4,16,128]{2,1,0:T(8,128)S(1)}, u32[]{:S(2)}, u32[]{:S(2)}) collective-permute-start(f32[4,16,128]{2,1,0:T(8,128)S(1)} %get-tuple-element.27), channel_id=1, source_target_pairs={{0,2},{3,1},{4,6},{7,5},{8,10},{11,9},{12,14},{15,13},{16,18},{19,... | collective-permute-start | bytes 98312 | tf_op jit(solution)/shard_map/ppermute | solution.py:577

commit v4 on v3

--- a/solution.py
+++ b/solution.py
@@ -18,7 +18,7 @@
 NCOEF = 11
 PAD = 8
 PIECES = 4
-STRIP = 4
+NEAR_PIECES = 2
 
 VMEM = pltpu.VMEM
 SMEM = pltpu.SMEM
@@ -88,35 +88,38 @@
     peers, cores = sizes["row"], sizes["ta"]
     sources, refs = refs[: cores - 1], refs[cores - 1 :]
     fields, cx, cr, ct = sources[0].shape
-    _, row, core, group = position(sizes)
+    gx, row, core, group = position(sizes)
+    odd = gx % 2
     step = cx // PIECES
+    low = step * (first + (PIECES - 2 * first - count) * odd)
     done = ()
     if last:
         done, refs = refs[:first], refs[first:]
     out = refs[:count]
     for f in range(fields):
-        v = part_ref[first * step : (first + count) * step, f].reshape(count * step * cr, ct)
+        v = part_ref[pl.ds(low, count * step), f].reshape(count * step * cr, ct)
         for k, s in enumerate(sources):
-            x = s[f, first * step : (first + count) * step].reshape(count * step * cr, ct)
+            x = s[f, pl.ds(low, count * step)].reshape(count * step * cr, ct)
             other = (core + k + 1) % cores
             v = v + dot3(*halves(x), table_ref[0, group, other], table_ref[1, group, other])
         v = v.reshape(count, step, cr, ct)
         for i in range(count):
-            out[i][:, f] = v[i]
+            out[i][:, f] = jnp.where(odd == 1, v[count - 1 - i], v[i])
     if last:
         e0_ref, eu_ref = refs[count:]
-        at = 0
+        starts = [sum(CORNER[:x]) for x in range(cx)]
         for i, ref in enumerate(tuple(done) + tuple(out)):
+            block = i + (PIECES - 1 - 2 * i) * odd
+            mirror = step * (PIECES - 1 - i)
             for side in range(e0_ref.shape[0]):
                 top = 1 - row if peers == 2 else 1 - side
                 rows = pl.ds(pl.multiple_of((cr - HALO) * top, 8), HALO)
-                e0_ref[side, i * step : (i + 1) * step] = ref[:, :, rows]
-            for j in range(step):
-                n = CORNER[i * step + j]
-                for side in range(e0_ref.shape[0]):
-                    top = 1 - row if peers == 2 else 1 - side
-                    eu_ref[side, :, at : at + n] = ref[j, :, pl.ds((cr - n) * top, n)]
-                at += n
+                e0_ref[side, pl.ds(block * step, step)] = ref[:, :, rows]
+                for j in range(step):
+                    n = CORNER[i * step + j]
+                    at = starts[i * step + j]
+                    at = at + (starts[mirror + j] - at) * odd
+                    eu_ref[side, :, pl.ds(at, n)] = ref[j, :, pl.ds((cr - n) * top, n)]
 
 
 def prepare_kernel(
@@ -181,6 +184,12 @@
         self.pair_at = 2 * cx * self.even
         self.far_at = 2 * cx * self.odd
 
+    def block(self, piece, odd):
+        return piece + (PIECES - 1 - 2 * piece) * odd
+
+    def tile(self, work):
+        return lambda x, f, r: work[x, f, pl.ds(self.own + r, 8)]
+
     def halo(self, side, n=HALO):
         if self.peers == 2:
             return PAD + self.row * (HALO - n) + self.cr * (1 - self.row)
@@ -270,98 +279,110 @@
 
                     lax.fori_loop(low, high, wipe, 0)
 
-    def pressure(self, weight_ref, p_ref, t, read, low, high):
-        def one(x, carry):
+    def pressure(self, weight_ref, p_ref, t, read, low, count):
+        for i in range(count):
+            x = low + i
             for b in range(self.cr // 8):
                 p = weight_ref[0] * read(x, 0, 8 * b)
                 for f in range(1, self.fields):
                     p = p + weight_ref[f] * read(x, f, 8 * b)
                 p_ref[t, pl.ds(pl.multiple_of((x - self.cx) * self.cr + 8 * b, 8), 8)] = p
-            return carry
-
-        lax.fori_loop(low, high, one, 0)
-
-
-def near_kernel(sizes, coef_ref, weight_ref, *refs):
-    own_refs, pair_refs = refs[:PIECES], refs[PIECES : 2 * PIECES]
-    r0_ref, rp_ref, strip_ref, p_ref, w0_ref, w1_ref = refs[2 * PIECES :]
+
+
+def setup_kernel(sizes, *refs):
+    own_refs, levels = refs[:PIECES], refs[PIECES:]
     step, cr = own_refs[0].shape[0], own_refs[0].shape[2]
     cx = step * PIECES
-    z = Frame(sizes, cx, cr, w0_ref)
-    first = cx * z.even
-    z.clear(first, first + 2 * cx, w0_ref, w1_ref)
+    z = Frame(sizes, cx, cr, levels[0])
+    for t in range(STEPS):
+        z.clear(2 * t + 2, 3 * cx - 2 * t - 2, levels[t])
     for i in range(PIECES):
-        z.place(own_refs[i], w0_ref, cx + i * step, z.own)
-        z.place(pair_refs[i], w0_ref, z.pair_at + i * step, z.own)
-    z.place_edge(r0_ref, w0_ref, cx)
-    z.place_corner(rp_ref, w0_ref, z.pair_at)
-    p_ref[...] = jnp.zeros_like(p_ref)
-    works = [w0_ref, w1_ref]
+        z.place(own_refs[i], levels[0], cx + z.block(i, z.odd) * step, z.own)
     for t in range(1, STEPS):
-        src, dst = works[(t - 1) % 2], works[t % 2]
+        z.blank(cx - 2, cx - 2 + 2 * (1 - z.left), levels[t])
+        z.blank(2 * cx, 2 * cx + 2 * (1 - z.right), levels[t])
+
+
+def near_kernel(sizes, coef_ref, weight_ref, *refs):
+    pair_refs, refs = refs[:PIECES], refs[PIECES:]
+    r0_ref, rp_ref, p_ref, *levels = refs[:2] + refs[2 + STEPS :]
+    step, cr = pair_refs[0].shape[0], pair_refs[0].shape[2]
+    cx = step * PIECES
+    z = Frame(sizes, cx, cr, levels[0])
+    for i in range(PIECES):
+        z.place(pair_refs[i], levels[0], z.pair_at + z.block(i, z.even) * step, z.own)
+    z.place_edge(r0_ref, levels[0], cx)
+    z.place_corner(rp_ref, levels[0], z.pair_at)
+    for t in range(1, STEPS):
         low = (cx + 2 * t) * z.even + 2 * t * z.odd
-        high = (3 * cx - 2 * t) * z.even + (2 * cx - 2 * t) * z.odd
-        z.sweep(coef_ref, src, dst, low, high)
-        edge = low * z.even + (high - STRIP) * z.odd
-        for i in range(STRIP):
-            strip_ref[t - 1, i] = dst[edge + i, :, pl.ds(PAD, z.rows)]
-        z.pressure(
-            weight_ref, p_ref, t - 1,
-            lambda x, f, r, dst=dst: dst[x, f, pl.ds(z.own + r, 8)],
-            cx + 2 * t * z.even, 2 * cx - 2 * t * z.odd,
-        )
+        z.sweep(coef_ref, levels[t - 1], levels[t], low, low + 2 * cx - 4 * t)
+        z.pressure(weight_ref, p_ref, t - 1, z.tile(levels[t]), cx + 2 * t * z.even, cx - 2 * t)
+
+
+def outward(z, coef_ref, levels, t, reach):
+    low = jnp.maximum(z.cx - reach, z.cx - 2 * STEPS * z.left) * z.even
+    high = (z.cx - reach + 4) * z.even
+    low = low + (2 * z.cx + reach - 4) * z.odd
+    high = high + jnp.minimum(2 * z.cx + reach, 2 * z.cx + 2 * STEPS * z.right) * z.odd
+    z.sweep(coef_ref, levels[t - 1], levels[t], low, high)
+
+
+def middle_kernel(sizes, coef_ref, weight_ref, place_ref, *refs):
+    far_refs, refs = refs[:NEAR_PIECES], refs[NEAR_PIECES:]
+    rc_ref, refs = refs[0], refs[1 + 1 + STEPS :]
+    p_ref, levels, pick_ref = refs[0], refs[1 : 1 + STEPS], refs[1 + STEPS]
+    step, cr = far_refs[0].shape[0], far_refs[0].shape[2]
+    cx = step * PIECES
+    z = Frame(sizes, cx, cr, levels[0])
+    for i in range(NEAR_PIECES):
+        z.place(far_refs[i], levels[0], z.far_at + z.block(i, z.even) * step, z.own)
+    z.place_corner(rc_ref, levels[0], z.far_at)
+    for t in range(1, STEPS):
+        reach = 4 - 2 * t
+        outward(z, coef_ref, levels, t, reach)
+        count = min(4, 4 - reach) if reach < 4 else 0
+        count = min(count, 2 * t)
+        low = cx - min(reach, 0)
+        z.pressure(weight_ref, p_ref, t - 1, z.tile(levels[t]), low * z.even + (3 * cx - low - count) * z.odd, count)
+    for t in range(2):
+        pick_ref[t] = picked(place_ref, p_ref[t])
+
+
+def picked(place_ref, value):
+    high, low = halves(value)
+    dot = functools.partial(jnp.dot, preferred_element_type=jnp.float32)
+    return dot(place_ref[...], high) + dot(place_ref[...], low)
 
 
 def far_kernel(sizes, coef_ref, weight_ref, place_ref, *refs):
-    own_refs, far_refs = refs[:PIECES], refs[PIECES : 2 * PIECES]
-    r0_ref, rc_ref, strip_ref, part_ref, out_ref = refs[2 * PIECES : 2 * PIECES + 5]
-    cycle_refs = refs[2 * PIECES + 5 : -3]
-    w0_ref, w1_ref, p_ref = refs[-3:]
-    step, cr = own_refs[0].shape[0], own_refs[0].shape[2]
+    far_refs, refs = refs[: PIECES - NEAR_PIECES], refs[PIECES - NEAR_PIECES :]
+    pick_ref, refs = refs[0], refs[1 + 1 + STEPS :]
+    p_ref, levels, out_ref = refs[0], refs[1 : 1 + STEPS], refs[1 + STEPS]
+    cycle_refs = refs[2 + STEPS :]
+    step, cr = far_refs[0].shape[0], far_refs[0].shape[2]
     cx = step * PIECES
-    z = Frame(sizes, cx, cr, w0_ref)
-    first = cx * z.odd
-    z.clear(first, first + 2 * cx, w0_ref, w1_ref)
-    for i in range(PIECES):
-        z.place(own_refs[i], w0_ref, cx + i * step, z.own)
-        z.place(far_refs[i], w0_ref, z.far_at + i * step, z.own)
-    z.place_edge(r0_ref, w0_ref, cx)
-    z.place_corner(rc_ref, w0_ref, z.far_at)
-    z.blank(cx - 2, cx - 2 + 2 * (1 - z.left), w1_ref)
-    z.blank(2 * cx, 2 * cx + 2 * (1 - z.right), w1_ref)
-    works = [w0_ref, w1_ref]
+    z = Frame(sizes, cx, cr, levels[0])
+    for i in range(NEAR_PIECES, PIECES):
+        z.place(far_refs[i - NEAR_PIECES], levels[0], z.far_at + z.block(i, z.even) * step, z.own)
     for t in range(1, STEPS):
-        src, dst = works[(t - 1) % 2], works[t % 2]
-        reach = HALO - 2 * t
-        low = (cx - reach * z.left) * z.even + (2 * cx - 2 * t) * z.odd
-        high = (cx + 2 * t) * z.even + (2 * cx + reach * z.right) * z.odd
-        z.sweep(coef_ref, src, dst, low, high)
-        edge = (cx + 2 * t) * z.even + (2 * cx - 2 * t - STRIP) * z.odd
-        for i in range(STRIP):
-            dst[edge + i, :, pl.ds(PAD, z.rows)] = strip_ref[t - 1, i]
-        p_ref[t - 1] = part_ref[t - 1]
-        z.pressure(
-            weight_ref, p_ref, t - 1,
-            lambda x, f, r, dst=dst: dst[x, f, pl.ds(z.own + r, 8)],
-            cx * z.even + (2 * cx - 2 * t) * z.odd, (cx + 2 * t) * z.even + 2 * cx * z.odd,
-        )
-    src = works[(STEPS - 1) % 2]
+        outward(z, coef_ref, levels, t, HALO - 2 * t)
+    z.pressure(
+        weight_ref, p_ref, STEPS - 2, z.tile(levels[STEPS - 1]), cx * z.even + (2 * cx - 2) * z.odd, 2
+    )
 
     def store_out(x, f, b, value):
         out_ref[x - cx, f, pl.ds(8 * b, 8)] = value
 
     def body_out(x, carry):
-        z.layer(coef_ref, src, store_out, x, z.own, cr // 8)
+        z.layer(coef_ref, levels[STEPS - 1], store_out, x, z.own, cr // 8)
         return carry
 
     lax.fori_loop(cx, 2 * cx, body_out, 0)
-    z.pressure(weight_ref, p_ref, STEPS - 1, lambda x, f, r: out_ref[x - cx, f, pl.ds(r, 8)], cx, 2 * cx)
-    dot = functools.partial(jnp.dot, preferred_element_type=jnp.float32)
+    z.pressure(weight_ref, p_ref, STEPS - 1, lambda x, f, r: out_ref[x - cx, f, pl.ds(r, 8)], cx, cx)
     for t in range(STEPS):
-        high, low = halves(p_ref[t])
-        picked = dot(place_ref[...], high) + dot(place_ref[...], low)
+        value = pick_ref[t] if t < 2 else picked(place_ref, p_ref[t])
         for k, ref in enumerate(cycle_refs):
-            ref[t] = picked[k * CAP : (k + 1) * CAP]
+            ref[t] = value[k * CAP : (k + 1) * CAP]
 
 
 def inverse_kernel(sizes, *refs):
@@ -547,27 +568,49 @@
     )(diffusivity, axial_speed, coupling, station_cell, owner_row.reshape(-1), lines)
 
     rows = cr + HALO * sides
-    work = pltpu.VMEM((3 * cx, fields, rows + 2 * PAD, ct), jnp.float32)
-    strip, parts = pl.pallas_call(
+    state = (shape(STEPS, cx * cr, ct),) + (shape(3 * cx, fields, rows + 2 * PAD, ct),) * STEPS
+    held = len(state)
+    levels = pl.pallas_call(
+        functools.partial(setup_kernel, sizes),
+        out_shape=state[1:],
+        in_specs=spec(VMEM, PIECES),
+        out_specs=tuple(spec(VMEM, STEPS)),
+        compiler_params=limit(20),
+        cost_estimate=work_for(10**6),
+        name="setup",
+    )(*own)
+    levels = pl.pallas_call(
         functools.partial(near_kernel, sizes),
-        out_shape=(shape(STEPS - 1, STRIP, fields, rows, ct), shape(STEPS - 1, cx * cr, ct)),
-        in_specs=spec(VMEM, 1) + spec(SMEM, 1) + spec(VMEM, 2 * PIECES + 2),
-        out_specs=tuple(spec(VMEM, 2)),
-        scratch_shapes=[work, work],
+        out_shape=state,
+        in_specs=spec(VMEM, 1) + spec(SMEM, 1) + spec(VMEM, PIECES + 2 + STEPS),
+        out_specs=tuple(spec(VMEM, held)),
+        input_output_aliases={4 + PIECES + i: 1 + i for i in range(STEPS)},
         compiler_params=limit(20),
         cost_estimate=work_for(10**7),
         name="near",
-    )(coef, pressure_weights, *own, *pair, r0, rp)
-    modes, *cycles = pl.pallas_call(
+    )(coef, pressure_weights, *pair, r0, rp, *levels)
+    count = NEAR_PIECES
+    *levels, picks = pl.pallas_call(
+        functools.partial(middle_kernel, sizes),
+        out_shape=state + (shape(2, peers * CAP, ct),),
+        in_specs=spec(VMEM, 1) + spec(SMEM, 1) + spec(VMEM, 1 + count + 1 + held),
+        out_specs=tuple(spec(VMEM, held + 1)),
+        input_output_aliases={4 + count + i: i for i in range(held)},
+        compiler_params=limit(20),
+        cost_estimate=work_for(10**7),
+        name="middle",
+    )(coef, pressure_weights, place, *far[:count], rc, *levels)
+    results = pl.pallas_call(
         functools.partial(far_kernel, sizes),
-        out_shape=(shape(cx, fields, cr, ct),) + (shape(STEPS, CAP, ct),) * peers,
-        in_specs=spec(VMEM, 1) + spec(SMEM, 1) + spec(VMEM, 1 + 2 * PIECES + 4),
-        out_specs=tuple(spec(VMEM, 1 + peers)),
-        scratch_shapes=[work, work, pltpu.VMEM((STEPS, cx * cr, ct), jnp.float32)],
+        out_shape=state + (shape(cx, fields, cr, ct),) + (shape(STEPS, CAP, ct),) * peers,
+        in_specs=spec(VMEM, 1) + spec(SMEM, 1) + spec(VMEM, 1 + PIECES - count + 1 + held),
+        out_specs=tuple(spec(VMEM, held + 1 + peers)),
+        input_output_aliases={4 + PIECES - count + i: i for i in range(held)},
         compiler_params=limit(20),
         cost_estimate=work_for(10**7),
         name="rest",
-    )(coef, pressure_weights, place, *own, *far, r0, rc, strip, parts)
+    )(coef, pressure_weights, place, *far[count:], picks, *levels)
+    modes, cycles = results[held], results[held + 1 :]
 
     received = [cycles[0]]
     for k in range(1, peers):

time: 49.2 us -> 51.8 us (1.053)
  the two profiles are of different devices: /device:TPU:9 before, /device:TPU:1 now
where the time goes in v4:
time: 51.8 us; the launch traced here: 51.5 us
  starting transfers between devices  28.5 us (55%)
  Pallas kernels  12.5 us (24%)
  waiting for transfers between devices  7.44 us (14%)
  local copies, waits for them, and re-layouts  2.07 us (4%)
  between operations  0.92 us (2%)
    ppermute x4, starting transfers between devices, local(): far.append(lax.ppermute(x, 'gx', onward))  12.8 us
    ppermute x2, starting transfers between devices, radial(): got.append(lax.ppermute(x[side:side + 1], ('row', 'ta'), hops))  3.82 us
    ppermute x4, waiting for transfers between devices, local(): pair.append(lax.ppermute(x, 'gx', swap))  3.64 us
    ppermute x1, waiting for transfers between devices, local(): received.append(lax.ppermute(cycles[k], ('row', 'ta'), pairs))  3.36 us
    ppermute x2, starting transfers between devices, others(): lax.ppermute(x, 'ta', [((c + k) % cores, c) for c in range(cores)])  3.29 us
    pallas_call x1, Pallas kernels, local(): pl.pallas_call(functools.partial(near_kernel, sizes), out_shape=state, in...  3.26 us
    ppermute x1, starting transfers between devices, local(): rc = lax.ppermute(rp, 'gx', onward)  3.2 us
    ppermute x4, starting transfers between devices, local(): pair.append(lax.ppermute(x, 'gx', swap))  2.93 us
  transfers between devices with their start and end apart: 15, of which 6 were waited for; matrix products, arithmetic and copies ran while one was open for 0% of the time, Pallas kernels for 17%

profile of v4, /device:TPU:1, one launch (start us, length us, event | category | flops | bytes accessed | tf_op | source)
XLA Modules:
  0.0 51.5 jit_solution(4941697511758708557)
XLA Ops:
  0.6 0.1 collective-permute-start
  0.7 0.9 %copy-done = bf16[2,2,2,128,128]{4,3,2,1,0:T(8,128)(2,1)S(1)} copy-done((bf16[2,2,2,128,128]{4,3,2,1,0:T(8,128)(2,1)S(1)}, bf16[2,2,2,128,128]{4,3,2,1,0:T(8,128)(2,1)}, u32[]{:S(2)}) %copy-start) | copy-done | bytes 262168
  1.7 1.1 %copy-done.1 = f32[5,8,32,128]{3,2,1,0:T(8,128)S(1)} copy-done((f32[5,8,32,128]{3,2,1,0:T(8,128)S(1)}, f32[5,8,32,128]{3,2,1,0:T(8,128)}, u32[]{:S(2)}) %copy-start.1) | copy-done | bytes 655384
  2.8 0.0 copy-start.9
  2.8 0.0 copy-start.10
  2.8 0.0 copy-start.4
  2.8 0.4 stage.1.part_ref
  3.2 0.0 collective-permute-done.refs_0_
  3.2 0.3 forward_early.1
  3.5 0.3 forward_late.1
  3.9 2.7 %collective-permute-start.9 = (f32[1,5,40,128]{3,2,1,0:T(8,128)S(1)}, f32[1,5,40,128]{3,2,1,0:T(8,128)S(1)}, u32[]{:S(2)}, u32[]{:S(2)}) collective-permute-start(f32[1,5,40,128]{3,2,1,0:T(8,128)S(1)} %get-tuple-element.34), channel_id=1, source_target_pairs={{0,3},{1,2},{3,0},{2,1},{4,7},{5,6},{7,4},{6,5},{8,11},{9,10},{11,... | collective-permute-start | bytes 307208 | tf_op jit(solution)/shard_map/ppermute | solution.py:539
  6.5 1.2 %collective-permute-start.1 = (f32[2,5,32,128]{3,2,1,0:T(8,128)S(1)}, f32[2,5,32,128]{3,2,1,0:T(8,128)S(1)}, u32[]{:S(2)}, u32[]{:S(2)}) collective-permute-start(f32[2,5,32,128]{3,2,1,0:T(8,128)S(1)} %get-tuple-element.32.refs_2_), channel_id=1, source_target_pairs={{0,4},{4,0},{8,12},{12,8},{16,20},{20,16},{24,28},{28,24},{1,5},{5... | collective-permute-start | bytes 491528 | tf_op jit(solution)/shard_map/ppermute | solution.py:546
  7.8 0.2 collective-permute-start.5
  8.0 1.2 %collective-permute-start.7 = (f32[2,5,32,128]{3,2,1,0:T(8,128)S(1)}, f32[2,5,32,128]{3,2,1,0:T(8,128)S(1)}, u32[]{:S(2)}, u32[]{:S(2)}) collective-permute-start(f32[2,5,32,128]{3,2,1,0:T(8,128)S(1)} %get-tuple-element.31.refs_2_.refs_1_), channel_id=1, source_target_pairs={{0,4},{4,0},{8,12},{12,8},{16,20},{20,16},{24,28},{28,24},{1,5},{5... | collective-permute-start | bytes 491528 | tf_op jit(solution)/shard_map/ppermute | solution.py:546
  9.2 0.2 collective-permute-start.3
  9.5 0.4 collective-permute-done.9
  9.9 1.2 %collective-permute-start.12 = (f32[1,8,5,8,128]{4,3,2,1,0:T(8,128)S(1)}, f32[1,8,5,8,128]{4,3,2,1,0:T(8,128)S(1)}, u32[]{:S(2)}, u32[]{:S(2)}) collective-permute-start(f32[1,8,5,8,128]{4,3,2,1,0:T(8,128)S(1)} %get-tuple-element.35), channel_id=1, source_target_pairs={{0,3},{1,2},{3,0},{2,1},{4,7},{5,6},{7,4},{6,5},{8,11},{9,10},{11,... | collective-permute-start | bytes 491528 | tf_op jit(solution)/shard_map/ppermute | solution.py:539
  11.0 0.8 %collective-permute-done.1.refs_2_ = f32[2,5,32,128]{3,2,1,0:T(8,128)S(1)} collective-permute-done((f32[2,5,32,128]{3,2,1,0:T(8,128)S(1)}, f32[2,5,32,128]{3,2,1,0:T(8,128)S(1)}, u32[]{:S(2)}, u32[]{:S(2)}) %collective-permute-start.1) | collective-permute-done | bytes 163872 | tf_op jit(solution)/shard_map/ppermute | solution.py:546
  11.8 1.2 %collective-permute-start.10 = (f32[1,5,40,128]{3,2,1,0:T(8,128)S(1)}, f32[1,5,40,128]{3,2,1,0:T(8,128)S(1)}, u32[]{:S(2)}, u32[]{:S(2)}) collective-permute-start(f32[1,5,40,128]{3,2,1,0:T(8,128)S(1)} %collective-permute-done.9), channel_id=1, source_target_pairs={{0,4},{4,0},{8,12},{12,8},{16,20},{20,16},{24,28},{28,24},{1,5},{5... | collective-permute-start | bytes 307208 | tf_op jit(solution)/shard_map/ppermute | solution.py:547
  13.0 2.3 %collective-permute-done.5.refs_0_ = f32[2,5,32,128]{3,2,1,0:T(8,128)S(1)} collective-permute-done((f32[2,5,32,128]{3,2,1,0:T(8,128)S(1)}, f32[2,5,32,128]{3,2,1,0:T(8,128)S(1)}, u32[]{:S(2)}, u32[]{:S(2)}) %collective-permute-start.5) | collective-permute-done | bytes 163872 | tf_op jit(solution)/shard_map/ppermute | solution.py:546
  15.3 3.2 %collective-permute-start.6 = (f32[2,5,32,128]{3,2,1,0:T(8,128)S(1)}, f32[2,5,32,128]{3,2,1,0:T(8,128)S(1)}, u32[]{:S(2)}, u32[]{:S(2)}) collective-permute-start(f32[2,5,32,128]{3,2,1,0:T(8,128)S(1)} %collective-permute-done.5.refs_0_), channel_id=1, source_target_pairs={{0,8},{8,16},{12,4},{16,24},{20,12},{28,20},{1,9},{9,17},{13,5},{1... | collective-permute-start | bytes 491528 | tf_op jit(solution)/shard_map/ppermute | solution.py:550
  18.5 0.3 collective-permute-done.7.refs_1_
  18.8 3.2 %collective-permute-start.8 = (f32[2,5,32,128]{3,2,1,0:T(8,128)S(1)}, f32[2,5,32,128]{3,2,1,0:T(8,128)S(1)}, u32[]{:S(2)}, u32[]{:S(2)}) collective-permute-start(f32[2,5,32,128]{3,2,1,0:T(8,128)S(1)} %collective-permute-done.7.refs_1_), channel_id=1, source_target_pairs={{0,8},{8,16},{12,4},{16,24},{20,12},{28,20},{1,9},{9,17},{13,5},{1... | collective-permute-start | bytes 491528 | tf_op jit(solution)/shard_map/ppermute | solution.py:550
  22.0 0.3 collective-permute-done.3.refs_3_
  22.3 3.2 %collective-permute-start.2 = (f32[2,5,32,128]{3,2,1,0:T(8,128)S(1)}, f32[2,5,32,128]{3,2,1,0:T(8,128)S(1)}, u32[]{:S(2)}, u32[]{:S(2)}) collective-permute-start(f32[2,5,32,128]{3,2,1,0:T(8,128)S(1)} %collective-permute-done.1.refs_2_), channel_id=1, source_target_pairs={{0,8},{8,16},{12,4},{16,24},{20,12},{28,20},{1,9},{9,17},{13,5},{1... | collective-permute-start | bytes 491528 | tf_op jit(solution)/shard_map/ppermute | solution.py:550
  25.5 0.0 collective-permute-done.12.refs_4_
  25.5 3.2 %collective-permute-start.4 = (f32[2,5,32,128]{3,2,1,0:T(8,128)S(1)}, f32[2,5,32,128]{3,2,1,0:T(8,128)S(1)}, u32[]{:S(2)}, u32[]{:S(2)}) collective-permute-start(f32[2,5,32,128]{3,2,1,0:T(8,128)S(1)} %collective-permute-done.3.refs_3_), channel_id=1, source_target_pairs={{0,8},{8,16},{12,4},{16,24},{20,12},{28,20},{1,9},{9,17},{13,5},{1... | collective-permute-start | bytes 491528 | tf_op jit(solution)/shard_map/ppermute | solution.py:550
  28.8 0.0 collective-permute-done.10.refs_5_
  28.8 3.2 %collective-permute-start.11 = (f32[1,5,40,128]{3,2,1,0:T(8,128)S(1)}, f32[1,5,40,128]{3,2,1,0:T(8,128)S(1)}, u32[]{:S(2)}, u32[]{:S(2)}) collective-permute-start(f32[1,5,40,128]{3,2,1,0:T(8,128)S(1)} %collective-permute-done.10.refs_5_), channel_id=1, source_target_pairs={{0,8},{8,16},{12,4},{16,24},{20,12},{28,20},{1,9},{9,17},{13,5},{1... | collective-permute-start | bytes 307208 | tf_op jit(solution)/shard_map/ppermute | solution.py:548
  32.0 1.3 %prepare.1 = (f32[5,11,8,128]{3,2,1,0:T(8,128)S(1)}, bf16[32,256]{1,0:T(8,128)(2,1)S(1)}) custom-call(f32[5]{0:T(128)S(1)} %copy-done.7, f32[5]{0:T(128)S(1)} %copy-done.8, f32[5,5]{1,0:T(8,128)S(1)} %copy-done.5, s32[32]{0:T(128)S(1)} %copy-done.9, s32[32]{0:T(128)S(1)} %bitcast.1, f32[2,8,128]{2,1,0:T(8,128)S(1)} %copy-done.3), custom_call_target="tpu_custom_call" | custom-call | flops 1000000 | bytes 1000000 | tf_op jit(solution)/shard_map/prepare/pallas_call | solution.py:553
  33.4 0.5 setup.1
  33.9 3.3 %near.1 = (f32[4,256,128]{2,1,0:T(8,128)S(1)}, f32[24,5,56,128]{3,2,1,0:T(8,128)S(1)}, f32[24,5,56,128]{3,2,1,0:T(8,128)S(1)}, f32[24,5,56,128]{3,2,1,0:T(8,128)S(1)}, f32[24,5,56,128]{3,2,1,0:T(8,128)S(1)}) custom-call(f32[5,11,8,128]{3,2,1,0:T(8,128)S(1)} %get-tuple-element.28.coef_ref, ...), custom_call_target="tpu_custom_call", output_to_operand_aliasing={{1}: (8, {}), {2}: (9, {}), {3}: (10, {}), {4}: (11, {})} | custom-call | flops 10000000 | bytes 1000000 | tf_op jit(solution)/shard_map/near/pallas_call | solution.py:582
  37.1 0.0 collective-permute-done.11.refs_2_
  37.1 0.0 collective-permute-done.6.refs_0_
  37.2 0.0 collective-permute-done.8.refs_1_
  37.2 1.9 %middle.1 = (f32[4,256,128]{2,1,0:T(8,128)S(1)}, f32[24,5,56,128]{3,2,1,0:T(8,128)S(1)}, f32[24,5,56,128]{3,2,1,0:T(8,128)S(1)}, f32[24,5,56,128]{3,2,1,0:T(8,12...) custom-call(f32[5,11,8,128]{3,2,1,0:T(8,128)S(1)} %get-tuple-element, ...), custom_call_target="tpu_custom_call", output_to_operand_aliasing={{0}: (6, {}), {1}: (7, {}), {2}: (8, {}), {3}: (9, {}), {4}... | custom-call | flops 10000000 | bytes 1000000 | tf_op jit(solution)/shard_map/middle/pallas_call | solution.py:593
  39.1 0.0 collective-permute-done.2.refs_0_
  39.1 0.0 collective-permute-done.4.refs_1_
  39.1 0.0 copy-start.6
  39.1 0.0 copy-start.2
  39.1 1.7 %rest.1 = (f32[4,256,128]{2,1,0:T(8,128)S(1)}, f32[24,5,56,128]{3,2,1,0:T(8,128)S(1)}, f32[24,5,56,128]{3,2,1,0:T(8,128)S(1)}, f32[24,5,56,128]{3,2,1,0:T(8,128)...) custom-call(f32[5,11,8,128]{3,2,1,0:T(8,128)S(1)} %get-tuple-element, ...), custom_call_target="tpu_custom_call", output_to_operand_aliasing={{0}: (6, {}), {1}: (7, {}), {2}: (8, {}), {3}: (9, {}), {4}... | custom-call | flops 10000000 | bytes 1000000 | tf_op jit(solution)/shard_map/rest/pallas_call | solution.py:603
  40.8 3.2 %collective-permute-start.13 = (f32[8,5,32,128]{3,2,1,0:T(8,128)S(1)}, f32[8,5,32,128]{3,2,1,0:T(8,128)S(1)}, u32[]{:S(2)}, u32[]{:S(2)}) collective-permute-start(f32[8,5,32,128]{3,2,1,0:T(8,128)S(1)} %get-tuple-element.51.refs_0_), channel_id=1, source_target_pairs={{1,0},{0,1},{3,2},{2,3},{5,4},{4,5},{7,6},{6,7},{9,8},{8,9},{11,10... | collective-permute-start | bytes 1966088 | tf_op jit(solution)/shard_map/ppermute | solution.py:482
  44.0 1.3 %collective-permute-start.14 = (f32[4,16,128]{2,1,0:T(8,128)S(1)}, f32[4,16,128]{2,1,0:T(8,128)S(1)}, u32[]{:S(2)}, u32[]{:S(2)}) collective-permute-start(f32[4,16,128]{2,1,0:T(8,128)S(1)} %get-tuple-element.53), channel_id=1, source_target_pairs={{0,2},{3,1},{4,6},{7,5},{8,10},{11,9},{12,14},{15,13},{16,18},{19,... | collective-permute-start | bytes 98312 | tf_op jit(solution)/shard_map/ppermute | solution.py:620
  45.3 3.4 %collective-permute-done.14.refs_1_ = f32[4,16,128]{2,1,0:T(8,128)S(1)} collective-permute-done((f32[4,16,128]{2,1,0:T(8,128)S(1)}, f32[4,16,128]{2,1,0:T(8,128)S(1)}, u32[]{:S(2)}, u32[]{:S(2)}) %collective-permute-start.14) | collective-permute-done | bytes 32800 | tf_op jit(solution)/shard_map/ppermute | solution.py:620
  48.7 1.4 %spectra.1 = f32[1,16,1056]{2,1,0:T(8,128)} custom-call(f32[4,16,128]{2,1,0:T(8,128)S(1)} %get-tuple-element.52.refs_0_, f32[4,16,128]{2,1,0:T(8,128)S(1)} %collective-permute-done.14.refs_1_, s32[4]{0:T(128)S(1)} %copy-done.6), custom_call_target="tpu_custom_call" | custom-call | flops 1000000 | bytes 1000000 | tf_op jit(solution)/shard_map/spectra/pallas_call | solution.py:632
  50.1 0.0 collective-permute-done.13.refs_1_
  50.1 0.0 copy-done.2
  50.1 1.4 %inverse.1 = f32[5,8,32,128]{3,2,1,0:T(8,128)} custom-call(f32[8,5,32,128]{3,2,1,0:T(8,128)S(1)} %get-tuple-element.51.refs_0_, f32[8,5,32,128]{3,2,1,0:T(8,128)S(1)} %collective-permute-done.13.refs_1_, bf16[2,2,2,128,128]{4,3,2,1,0:T(8,128)(2,1)S(1)} %copy-done.2), custom_call_target="tpu_custom_call" | custom-call | flops 1000000 | bytes 1000000 | tf_op jit(solution)/shard_map/inverse/pallas_call | solution.py:622
  (14 shorter events, 0.0 us)
Async XLA Ops:
  0.6 2.6 %collective-permute-start = (f32[5,8,32,128]{3,2,1,0:T(8,128)}, f32[5,8,32,128]{3,2,1,0:T(8,128)S(1)}, u32[]{:S(2)}, u32[]{:S(2)}) collective-permute-start(f32[5,8,32,128]{3,2,1,0:T(8,128)} %own_ref.1), channel_id=1, source_target_pairs={{1,0},{0,1},{3,2},{2,3},{5,4},{4,5},{7,6},{6,7},{9,8},{8,9},{11,10... | collective-permute-start | bytes 1966088 | tf_op jit(solution)/shard_map/ppermute | solution.py:482
  0.7 0.9 %copy-start = (bf16[2,2,2,128,128]{4,3,2,1,0:T(8,128)(2,1)S(1)}, bf16[2,2,2,128,128]{4,3,2,1,0:T(8,128)(2,1)}, u32[]{:S(2)}) copy-start(bf16[2,2,2,128,128]{4,3,2,1,0:T(8,128)(2,1)} %constant.6.clone.table_ref) | copy-start | bytes 786436
  1.7 1.1 %copy-start.1 = (f32[5,8,32,128]{3,2,1,0:T(8,128)S(1)}, f32[5,8,32,128]{3,2,1,0:T(8,128)}, u32[]{:S(2)}) copy-start(f32[5,8,32,128]{3,2,1,0:T(8,128)} %own_ref.1) | copy-start | bytes 1966084
  2.8 29.2 %copy-start.3 = (f32[2,8,128]{2,1,0:T(8,128)S(1)}, f32[2,8,128]{2,1,0:T(8,128)}, u32[]{:S(2)}) copy-start(f32[2,8,128]{2,1,0:T(8,128)} %constant.7.clone.eigen_ref) | copy-start | bytes 24580
  2.8 29.2 %copy-start.5 = (f32[5,5]{1,0:T(8,128)S(1)}, f32[5,5]{1,0:T(8,128)}, u32[]{:S(2)}) copy-start(f32[5,5]{1,0:T(8,128)} %mix_ref.1) | copy-start | bytes 304
  2.8 29.2 %copy-start.7 = (f32[5]{0:T(128)S(1)}, f32[5]{0:T(128)}, u32[]{:S(2)}) copy-start(f32[5]{0:T(128)} %rate_ref.1) | copy-start | bytes 64
  2.8 29.2 %copy-start.8 = (f32[5]{0:T(128)S(1)}, f32[5]{0:T(128)}, u32[]{:S(2)}) copy-start(f32[5]{0:T(128)} %speed_ref.1) | copy-start | bytes 64
  2.8 29.2 %copy-start.9 = (s32[32]{0:T(128)S(1)}, s32[32]{0:T(128)}, u32[]{:S(2)}) copy-start(s32[32]{0:T(128)} %cell_ref.1) | copy-start | bytes 388
  2.8 29.2 %copy-start.10 = (s32[32,1]{0,1:T(1,128)S(1)}, s32[32,1]{0,1:T(1,128)}, u32[]{:S(2)}) copy-start(s32[32,1]{0,1:T(1,128)} %param.17) | copy-start | bytes 388
  2.8 31.1 %copy-start.4 = (f32[5]{0:T(128)S(1)}, f32[5]{0:T(128)}, u32[]{:S(2)}) copy-start(f32[5]{0:T(128)} %weight_ref.5) | copy-start | bytes 64
  3.9 6.0 %collective-permute-start.9 = (f32[1,5,40,128]{3,2,1,0:T(8,128)S(1)}, f32[1,5,40,128]{3,2,1,0:T(8,128)S(1)}, u32[]{:S(2)}, u32[]{:S(2)}) collective-permute-start(f32[1,5,40,128]{3,2,1,0:T(8,128)S(1)} %get-tuple-element.34), channel_id=1, source_target_pairs={{0,3},{1,2},{3,0},{2,1},{4,7},{5,6},{7,4},{6,5},{8,11},{9,10},{11,... | collective-permute-start | bytes 307208 | tf_op jit(solution)/shard_map/ppermute | solution.py:539
  6.5 5.3 %collective-permute-start.1 = (f32[2,5,32,128]{3,2,1,0:T(8,128)S(1)}, f32[2,5,32,128]{3,2,1,0:T(8,128)S(1)}, u32[]{:S(2)}, u32[]{:S(2)}) collective-permute-start(f32[2,5,32,128]{3,2,1,0:T(8,128)S(1)} %get-tuple-element.32.refs_2_), channel_id=1, source_target_pairs={{0,4},{4,0},{8,12},{12,8},{16,20},{20,16},{24,28},{28,24},{1,5},{5... | collective-permute-start | bytes 491528 | tf_op jit(solution)/shard_map/ppermute | solution.py:546
  7.8 7.5 %collective-permute-start.5 = (f32[2,5,32,128]{3,2,1,0:T(8,128)S(1)}, f32[2,5,32,128]{3,2,1,0:T(8,128)S(1)}, u32[]{:S(2)}, u32[]{:S(2)}) collective-permute-start(f32[2,5,32,128]{3,2,1,0:T(8,128)S(1)} %get-tuple-element.30.refs_1_.refs_0_), channel_id=1, source_target_pairs={{0,4},{4,0},{8,12},{12,8},{16,20},{20,16},{24,28},{28,24},{1,5},{5... | collective-permute-start | bytes 491528 | tf_op jit(solution)/shard_map/ppermute | solution.py:546
  8.0 10.8 %collective-permute-start.7 = (f32[2,5,32,128]{3,2,1,0:T(8,128)S(1)}, f32[2,5,32,128]{3,2,1,0:T(8,128)S(1)}, u32[]{:S(2)}, u32[]{:S(2)}) collective-permute-start(f32[2,5,32,128]{3,2,1,0:T(8,128)S(1)} %get-tuple-element.31.refs_2_.refs_1_), channel_id=1, source_target_pairs={{0,4},{4,0},{8,12},{12,8},{16,20},{20,16},{24,28},{28,24},{1,5},{5... | collective-permute-start | bytes 491528 | tf_op jit(solution)/shard_map/ppermute | solution.py:546
  9.2 13.1 %collective-permute-start.3 = (f32[2,5,32,128]{3,2,1,0:T(8,128)S(1)}, f32[2,5,32,128]{3,2,1,0:T(8,128)S(1)}, u32[]{:S(2)}, u32[]{:S(2)}) collective-permute-start(f32[2,5,32,128]{3,2,1,0:T(8,128)S(1)} %get-tuple-element.33.refs_3_), channel_id=1, source_target_pairs={{0,4},{4,0},{8,12},{12,8},{16,20},{20,16},{24,28},{28,24},{1,5},{5... | collective-permute-start | bytes 491528 | tf_op jit(solution)/shard_map/ppermute | solution.py:546
  9.9 15.7 %collective-permute-start.12 = (f32[1,8,5,8,128]{4,3,2,1,0:T(8,128)S(1)}, f32[1,8,5,8,128]{4,3,2,1,0:T(8,128)S(1)}, u32[]{:S(2)}, u32[]{:S(2)}) collective-permute-start(f32[1,8,5,8,128]{4,3,2,1,0:T(8,128)S(1)} %get-tuple-element.35), channel_id=1, source_target_pairs={{0,3},{1,2},{3,0},{2,1},{4,7},{5,6},{7,4},{6,5},{8,11},{9,10},{11,... | collective-permute-start | bytes 491528 | tf_op jit(solution)/shard_map/ppermute | solution.py:539
  11.8 17.0 %collective-permute-start.10 = (f32[1,5,40,128]{3,2,1,0:T(8,128)S(1)}, f32[1,5,40,128]{3,2,1,0:T(8,128)S(1)}, u32[]{:S(2)}, u32[]{:S(2)}) collective-permute-start(f32[1,5,40,128]{3,2,1,0:T(8,128)S(1)} %collective-permute-done.9), channel_id=1, source_target_pairs={{0,4},{4,0},{8,12},{12,8},{16,20},{20,16},{24,28},{28,24},{1,5},{5... | collective-permute-start | bytes 307208 | tf_op jit(solution)/shard_map/ppermute | solution.py:547
  15.3 21.9 %collective-permute-start.6 = (f32[2,5,32,128]{3,2,1,0:T(8,128)S(1)}, f32[2,5,32,128]{3,2,1,0:T(8,128)S(1)}, u32[]{:S(2)}, u32[]{:S(2)}) collective-permute-start(f32[2,5,32,128]{3,2,1,0:T(8,128)S(1)} %collective-permute-done.5.refs_0_), channel_id=1, source_target_pairs={{0,8},{8,16},{12,4},{16,24},{20,12},{28,20},{1,9},{9,17},{13,5},{1... | collective-permute-start | bytes 491528 | tf_op jit(solution)/shard_map/ppermute | solution.py:550
  18.8 18.4 %collective-permute-start.8 = (f32[2,5,32,128]{3,2,1,0:T(8,128)S(1)}, f32[2,5,32,128]{3,2,1,0:T(8,128)S(1)}, u32[]{:S(2)}, u32[]{:S(2)}) collective-permute-start(f32[2,5,32,128]{3,2,1,0:T(8,128)S(1)} %collective-permute-done.7.refs_1_), channel_id=1, source_target_pairs={{0,8},{8,16},{12,4},{16,24},{20,12},{28,20},{1,9},{9,17},{13,5},{1... | collective-permute-start | bytes 491528 | tf_op jit(solution)/shard_map/ppermute | solution.py:550
  22.3 16.7 %collective-permute-start.2 = (f32[2,5,32,128]{3,2,1,0:T(8,128)S(1)}, f32[2,5,32,128]{3,2,1,0:T(8,128)S(1)}, u32[]{:S(2)}, u32[]{:S(2)}) collective-permute-start(f32[2,5,32,128]{3,2,1,0:T(8,128)S(1)} %collective-permute-done.1.refs_2_), channel_id=1, source_target_pairs={{0,8},{8,16},{12,4},{16,24},{20,12},{28,20},{1,9},{9,17},{13,5},{1... | collective-permute-start | bytes 491528 | tf_op jit(solution)/shard_map/ppermute | solution.py:550
  25.5 13.5 %collective-permute-start.4 = (f32[2,5,32,128]{3,2,1,0:T(8,128)S(1)}, f32[2,5,32,128]{3,2,1,0:T(8,128)S(1)}, u32[]{:S(2)}, u32[]{:S(2)}) collective-permute-start(f32[2,5,32,128]{3,2,1,0:T(8,128)S(1)} %collective-permute-done.3.refs_3_), channel_id=1, source_target_pairs={{0,8},{8,16},{12,4},{16,24},{20,12},{28,20},{1,9},{9,17},{13,5},{1... | collective-permute-start | bytes 491528 | tf_op jit(solution)/shard_map/ppermute | solution.py:550
  28.8 8.4 %collective-permute-start.11 = (f32[1,5,40,128]{3,2,1,0:T(8,128)S(1)}, f32[1,5,40,128]{3,2,1,0:T(8,128)S(1)}, u32[]{:S(2)}, u32[]{:S(2)}) collective-permute-start(f32[1,5,40,128]{3,2,1,0:T(8,128)S(1)} %collective-permute-done.10.refs_5_), channel_id=1, source_target_pairs={{0,8},{8,16},{12,4},{16,24},{20,12},{28,20},{1,9},{9,17},{13,5},{1... | collective-permute-start | bytes 307208 | tf_op jit(solution)/shard_map/ppermute | solution.py:548
  39.1 9.6 %copy-start.6 = (s32[4]{0:T(128)S(1)}, s32[4]{0:T(128)}, u32[]{:S(2)}) copy-start(s32[4]{0:T(128)} %refs_2_.2) | copy-start | bytes 52
  39.1 11.0 %copy-start.2 = (bf16[2,2,2,128,128]{4,3,2,1,0:T(8,128)(2,1)S(1)}, bf16[2,2,2,128,128]{4,3,2,1,0:T(8,128)(2,1)}, u32[]{:S(2)}) copy-start(bf16[2,2,2,128,128]{4,3,2,1,0:T(8,128)(2,1)} %constant.8.clone.refs_2_) | copy-start | bytes 786436
  40.8 9.3 %collective-permute-start.13 = (f32[8,5,32,128]{3,2,1,0:T(8,128)S(1)}, f32[8,5,32,128]{3,2,1,0:T(8,128)S(1)}, u32[]{:S(2)}, u32[]{:S(2)}) collective-permute-start(f32[8,5,32,128]{3,2,1,0:T(8,128)S(1)} %get-tuple-element.51.refs_0_), channel_id=1, source_target_pairs={{1,0},{0,1},{3,2},{2,3},{5,4},{4,5},{7,6},{6,7},{9,8},{8,9},{11,10... | collective-permute-start | bytes 1966088 | tf_op jit(solution)/shard_map/ppermute | solution.py:482
  44.0 4.6 %collective-permute-start.14 = (f32[4,16,128]{2,1,0:T(8,128)S(1)}, f32[4,16,128]{2,1,0:T(8,128)S(1)}, u32[]{:S(2)}, u32[]{:S(2)}) collective-permute-start(f32[4,16,128]{2,1,0:T(8,128)S(1)} %get-tuple-element.53), channel_id=1, source_target_pairs={{0,2},{3,1},{4,6},{7,5},{8,10},{11,9},{12,14},{15,13},{16,18},{19,... | collective-permute-start | bytes 98312 | tf_op jit(solution)/shard_map/ppermute | solution.py:620
